TPU v7x, 512 devices: a whole 4x8x8 slice. The times are simulated.
512 devices in a mesh: row: 32 (over x, z_lo, core), col: 16 (over y, z_hi).
Axes of the slice: x: 4, y: 8, z: 8 (z_hi: 2, z_lo: 4; z = z_hi * 4 + z_lo), core: 2. Of those that a mesh axis runs over, the one named last changes fastest.
Arguments:
- tokens: bfloat16 [192, 8192], P('row', 'col'), may hold values from -6 to 6
- gate_weight: bfloat16 [8192, 20480], P('col', 'row'), may hold values from -0.0625 to 0.0625
- up_weight: bfloat16 [8192, 20480], P('col', 'row'), may hold values from -0.0625 to 0.0625
- down_weight: bfloat16 [20480, 8192], P('row', 'col'), may hold values from -0.0390625 to 0.0390625
- keep_mask: int32 [192, 20480], P('col', 'row'), may hold values 0 or 1
- cotangent: bfloat16 [192, 8192], P('row', 'col'), may hold values from -6 to 6
Outputs:
- mixed_out: bfloat16 [192, 8192], P('row', 'col')
- input_grad: bfloat16 [192, 8192], P('row', 'col')
- gate_grad: bfloat16 [8192, 20480], P('col', 'row')
- up_grad: bfloat16 [8192, 20480], P('col', 'row')
- down_grad: bfloat16 [20480, 8192], P('row', 'col')
All inputs are finite; a program needn't handle non-finite values. No bound on the sum of `keep_mask` on one device may be relied on, other than what follows from the above.
Results may differ from a plain program's by a relative error of at most 0.0049.
Values may be sent and summed in bfloat16 or wider, within the bound.
No kernel may reach another device: no remote copies, remote signals or barrier semaphores. Data moves between devices by JAX's collectives and lax.ppermute only.
A program may use at most 64 MiB of HBM per device.

v0:
```python
import jax
import jax.numpy as jnp
from jax import lax
from jax.sharding import PartitionSpec as P

keep_scale = 1.0 / 0.9
contract_last = (((1,), (1,)), ((), ()))
contract_first = (((0,), (0,)), ((), ()))


def sent_to_all(value, axis):
    copies = jnp.broadcast_to(value, (lax.axis_size(axis), *value.shape))
    return lax.all_to_all(copies, axis, split_axis=0, concat_axis=0, tiled=True)


def joined_along(parts, dim):
    shape = list(parts.shape[1:])
    shape[dim] *= parts.shape[0]
    return jnp.moveaxis(parts, 0, dim).reshape(shape)


def collect(value, axis, dim):
    parts = sent_to_all(value, axis)
    return joined_along(parts, dim)


def split_up(value, dim, devices):
    before, after = (value.shape[:dim], value.shape[dim + 1 :])
    return jnp.moveaxis(value.reshape(*before, devices, -1, *after), dim, 0)


def sum_at_owner(value, axis, dim):
    parts = split_up(value, dim, lax.axis_size(axis))
    arrived = lax.all_to_all(parts, axis, split_axis=0, concat_axis=0, tiled=True)
    return arrived.sum(axis=0)


def side_by_side(arrays, axis, dim, along):
    ends, at = ([], 0)
    for a in arrays[:-1]:
        at += a.shape[along]
        ends.append(at)
    both = jnp.concatenate(arrays, axis=along)
    return tuple(jnp.split(sum_at_owner(both, axis, dim), ends, axis=along))


def side_by_side_2(arrays, axis, dim, along):
    both = jnp.concatenate(arrays, axis=along)
    filled, at, gathered = (lax.all_gather(both, axis, axis=dim, tiled=True), 0, [])
    for a in arrays:
        gathered.append(lax.slice_in_dim(filled, at, at + a.shape[along], axis=along))
        at += a.shape[along]
    return tuple(gathered)


def project_in(tokens, gate_weight, up_weight):
    gathered = collect(tokens, "row", 0)
    gate_part = jnp.dot(gathered, gate_weight, preferred_element_type=jnp.float32)
    up_part = jnp.dot(gathered, up_weight, preferred_element_type=jnp.float32)
    gate_value, up_value = side_by_side((gate_part, up_part), "col", 0, 1)
    return (gathered, gate_value, up_value)


def body(tokens, gate_weight, up_weight, down_weight, keep_mask, cotangent):
    gathered, gate_value, up_value = project_in(tokens, gate_weight, up_weight)
    keep_factor = keep_mask.astype(jnp.float32) * keep_scale
    sigmoid_gate = jax.nn.sigmoid(gate_value)
    silu_gate = gate_value * sigmoid_gate
    hidden = (silu_gate * up_value * keep_factor).astype(jnp.bfloat16)
    hidden_all = collect(hidden, "col", 0)
    row_block = hidden_all
    mixed_out = sum_at_owner(
        jnp.dot(row_block, down_weight, preferred_element_type=jnp.float32), "row", 0
    ).astype(jnp.bfloat16)
    cot_all = collect(cotangent, "row", 0)
    row_block = cot_all
    grad_hidden = sum_at_owner(
        lax.dot_general(row_block, down_weight, contract_last, preferred_element_type=jnp.float32),
        "col",
        0,
    )
    down_grad = lax.dot_general(
        hidden_all, cot_all, contract_first, preferred_element_type=jnp.float32
    ).astype(jnp.bfloat16)
    gathered, gate_value, up_value = project_in(tokens, gate_weight, up_weight)
    sigmoid_gate = jax.nn.sigmoid(gate_value)
    silu_gate = gate_value * sigmoid_gate
    grad_pre = grad_hidden * keep_factor
    grad_gate = (
        grad_pre * up_value * sigmoid_gate * (1.0 + gate_value * (1.0 - sigmoid_gate))
    ).astype(jnp.bfloat16)
    grad_up = (grad_pre * silu_gate).astype(jnp.bfloat16)
    gate_all, up_all = side_by_side_2((grad_gate, grad_up), "col", 0, 1)
    gate_grad = lax.dot_general(
        gathered, gate_all, contract_first, preferred_element_type=jnp.float32
    ).astype(jnp.bfloat16)
    up_grad = lax.dot_general(
        gathered, up_all, contract_first, preferred_element_type=jnp.float32
    ).astype(jnp.bfloat16)
    first = lax.dot_general(
        gate_all, gate_weight, contract_last, preferred_element_type=jnp.float32
    )
    second = lax.dot_general(up_all, up_weight, contract_last, preferred_element_type=jnp.float32)
    input_grad = sum_at_owner(first + second, "row", 0).astype(jnp.bfloat16)
    return (mixed_out, input_grad, gate_grad, up_grad, down_grad)


def solution(mesh):
    placed = (
        P("row", "col"),
        P("col", "row"),
        P("col", "row"),
        P("row", "col"),
        P("col", "row"),
        P("row", "col"),
    )
    return jax.shard_map(
        body,
        mesh=mesh,
        in_specs=placed,
        out_specs=(
            P("row", "col"),
            P("row", "col"),
            P("col", "row"),
            P("col", "row"),
            P("row", "col"),
        ),
        check_vma=False,
    )
```

profile of v0, /device:TPU:1, one launch (start us, length us, event | category | flops | bytes accessed | tf_op | source)
XLA Modules:
  0.0 253.3 jit_solution(3303021606894709824)
XLA Ops:
  0.6 0.0 copy-start
  0.6 0.0 copy-start.2
  0.7 0.8 broadcast_in_dim.12
  1.5 22.4 %all_to_all.37 = bf16[32,6,512]{2,1,0:T(8,128)(2,1)S(1)} all-to-all(bf16[32,6,512]{2,1,0:T(8,128)(2,1)S(1)} %broadcast_in_dim.12), channel_id=1, replica_groups=mesh['row'=32,'col'=16] {'row'}, dimensions={0} | all-to-all | bytes 393216 | tf_op jit(solution)/shard_map/all_to_all | solution.py:13
  23.9 0.0 copy-start.3
  23.9 1.4 broadcast_in_dim.10
  25.3 3.7 %all-to-all-start = ((bf16[32,6,512]{2,1,0:T(8,128)(2,1)}), bf16[32,6,512]{2,1,0:T(8,128)(2,1)S(1)}, u32[]{:S(2)}, u32[]{:S(2)}) async-start(bf16[32,6,512]{2,1,0:T(8,128)(2,1)} %broadcast_in_dim.10), calls=%async_computation | async-start | bytes 524288 | tf_op jit(solution)/shard_map/all_to_all | solution.py:13
  29.0 0.0 copy-done.3
  29.0 0.1 dot_general.37
  29.1 0.0 copy-done.2
  29.1 0.0 copy-start.1
  29.1 1.2 fusion.2
  30.3 9.8 %all-to-all-done = bf16[32,6,512]{2,1,0:T(8,128)(2,1)S(1)} async-done(((bf16[32,6,512]{2,1,0:T(8,128)(2,1)}), bf16[32,6,512]{2,1,0:T(8,128)(2,1)S(1)}, u32[]{:S(2)}, u32[]{:S(2)}) %all-to-all-start) | async-done | bytes 196640 | tf_op jit(solution)/shard_map/all_to_all | solution.py:13
  40.2 12.7 %all-to-all-start.5 = ((f32[16,12,640]{2,1,0:T(8,128)}), f32[16,12,640]{2,1,0:T(8,128)}, u32[]{:S(2)}, u32[]{:S(2)}) async-start(f32[16,12,640]{2,1,0:T(8,128)} %fusion.2), calls=%async_computation.5 | async-start | bytes 1310720 | tf_op jit(solution)/shard_map/all_to_all | solution.py:34
  52.9 0.1 reshape.33
  53.0 0.0 copy-done.1
  53.0 0.3 fusion.15
  53.3 0.0 copy-done
  53.3 0.3 fusion.14
  53.7 0.1 pad_maximum_fusion
  53.7 1.2 reshape.34
  54.9 22.6 %all-to-all-done.5 = f32[16,12,640]{2,1,0:T(8,128)} async-done(((f32[16,12,640]{2,1,0:T(8,128)}), f32[16,12,640]{2,1,0:T(8,128)}, u32[]{:S(2)}, u32[]{:S(2)}) %all-to-all-start.5) | async-done | bytes 491552 | tf_op jit(solution)/shard_map/all_to_all | solution.py:34
  77.5 8.0 %all-to-all-start.1 = ((f32[16,12,1280]{2,1,0:T(8,128)}), f32[16,12,1280]{2,1,0:T(8,128)S(1)}, u32[]{:S(2)}, u32[]{:S(2)}) async-start(f32[16,12,1280]{2,1,0:T(8,128)} %reshape.34), calls=%async_computation.1 | async-start | bytes 2621440 | tf_op jit(solution)/shard_map/all_to_all | solution.py:34
  85.5 1.7 reduce_sum.42
  87.3 37.2 %all-to-all-done.1 = f32[16,12,1280]{2,1,0:T(8,128)S(1)} async-done(((f32[16,12,1280]{2,1,0:T(8,128)}), f32[16,12,1280]{2,1,0:T(8,128)S(1)}, u32[]{:S(2)}, u32[]{:S(2)}) %all-to-all-start.1) | async-done | bytes 983072 | tf_op jit(solution)/shard_map/all_to_all | solution.py:34
  124.4 0.1 reduce_sum.40
  124.5 0.8 multiply_convert_fusion.1
  125.4 0.8 broadcast_in_dim.11
  126.1 14.3 %all-to-all-start.2 = ((bf16[16,12,640]{2,1,0:T(8,128)(2,1)}), bf16[16,12,640]{2,1,0:T(8,128)(2,1)S(1)}, u32[]{:S(2)}, u32[]{:S(2)}) async-start(bf16[16,12,640]{2,1,0:T(8,128)(2,1)} %broadcast_in_dim.11), calls=%async_computation.2 | async-start | bytes 655360 | tf_op jit(solution)/shard_map/all_to_all | solution.py:13
  140.5 60.1 %all-gather = bf16[16,12,1280]{2,1,0:T(8,128)(2,1)} all-gather(bf16[1,12,1280]{2,1,0:T(8,128)(2,1)S(1)} %maximum_bitcast_fusion), channel_id=1, replica_groups=mesh['row'=32,'col'=16] {'col'}, dimensions={0}, use_global_device_ids=true | all-gather | bytes 522240 | tf_op jit(solution)/shard_map/all_gather | solution.py:49
  200.6 1.2 reshape.39
  201.8 0.4 fusion.10
  202.2 0.4 convolution_add_fusion
  202.6 0.8 reshape.35
  203.4 0.0 all-to-all-done.2
  203.4 10.2 %all-to-all-start.6 = ((f32[32,6,512]{2,1,0:T(8,128)}), f32[32,6,512]{2,1,0:T(8,128)S(1)}, u32[]{:S(2)}, u32[]{:S(2)}) async-start(f32[32,6,512]{2,1,0:T(8,128)} %reshape.35), calls=%async_computation.6 | async-start | bytes 1048576 | tf_op jit(solution)/shard_map/all_to_all | solution.py:34
  213.7 0.8 dot_general.35
  214.5 0.0 copy-start.4
  214.5 1.3 fusion.4
  215.8 1.0 copy.18
  216.8 13.6 %all-to-all-done.6 = f32[32,6,512]{2,1,0:T(8,128)S(1)} async-done(((f32[32,6,512]{2,1,0:T(8,128)}), f32[32,6,512]{2,1,0:T(8,128)S(1)}, u32[]{:S(2)}, u32[]{:S(2)}) %all-to-all-start.6) | async-done | bytes 393248 | tf_op jit(solution)/shard_map/all_to_all | solution.py:34
  230.4 4.4 %all-to-all-start.3 = ((f32[32,6,512]{2,1,0:T(8,128)}), f32[32,6,512]{2,1,0:T(8,128)}, u32[]{:S(2)}, u32[]{:S(2)}) async-start(f32[32,6,512]{2,1,0:T(8,128)} %copy.18), calls=%async_computation.3 | async-start | bytes 1048576 | tf_op jit(solution)/shard_map/all_to_all | solution.py:34
  234.8 0.0 copy-done.4
  234.9 0.1 reshape.37
  234.9 0.4 fusion
  235.3 1.1 copy.21
  236.4 0.4 fusion.1
  236.8 1.1 copy.22
  237.8 0.1 reshape.36
  237.9 1.2 convolution_convert_fusion
  239.1 0.7 reduce_sum.43
  239.7 11.9 %all-to-all-done.3 = f32[32,6,512]{2,1,0:T(8,128)} async-done(((f32[32,6,512]{2,1,0:T(8,128)}), f32[32,6,512]{2,1,0:T(8,128)}, u32[]{:S(2)}, u32[]{:S(2)}) %all-to-all-start.3) | async-done | bytes 393248 | tf_op jit(solution)/shard_map/all_to_all | solution.py:34
  251.6 1.7 reduce_sum.41
  (1 shorter events, 0.0 us)
Async XLA Ops:
  0.6 52.7 %copy-start = (bf16[512,640]{1,0:T(8,128)(2,1)S(1)}, bf16[512,640]{1,0:T(8,128)(2,1)}, u32[]{:S(2)}) copy-start(bf16[512,640]{1,0:T(8,128)(2,1)} %param.7) | copy-start | bytes 1966084
  0.6 28.4 %copy-start.2 = (bf16[640,512]{1,0:T(8,128)(2,1)S(1)}, bf16[640,512]{1,0:T(8,128)(2,1)}, u32[]{:S(2)}) copy-start(bf16[640,512]{1,0:T(8,128)(2,1)} %param.9) | copy-start | bytes 1966084
  23.9 5.1 %copy-start.3 = (bf16[32,6,512]{2,1,0:T(8,128)(2,1)}, bf16[32,6,512]{2,1,0:T(8,128)(2,1)S(1)}, u32[]{:S(2)}) copy-start(bf16[32,6,512]{2,1,0:T(8,128)(2,1)S(1)} %all_to_all.37) | copy-start | bytes 589828
  25.3 14.9 %all-to-all-start = ((bf16[32,6,512]{2,1,0:T(8,128)(2,1)}), bf16[32,6,512]{2,1,0:T(8,128)(2,1)S(1)}, u32[]{:S(2)}, u32[]{:S(2)}) async-start(bf16[32,6,512]{2,1,0:T(8,128)(2,1)} %broadcast_in_dim.10), calls=%async_computation | async-start | bytes 524288 | tf_op jit(solution)/shard_map/all_to_all | solution.py:13
  29.1 23.9 %copy-start.1 = (bf16[512,640]{1,0:T(8,128)(2,1)S(1)}, bf16[512,640]{1,0:T(8,128)(2,1)}, u32[]{:S(2)}) copy-start(bf16[512,640]{1,0:T(8,128)(2,1)} %param.8) | copy-start | bytes 1966084
  40.2 37.3 %all-to-all-start.5 = ((f32[16,12,640]{2,1,0:T(8,128)}), f32[16,12,640]{2,1,0:T(8,128)}, u32[]{:S(2)}, u32[]{:S(2)}) async-start(f32[16,12,640]{2,1,0:T(8,128)} %fusion.2), calls=%async_computation.5 | async-start | bytes 1310720 | tf_op jit(solution)/shard_map/all_to_all | solution.py:34
  77.5 46.9 %all-to-all-start.1 = ((f32[16,12,1280]{2,1,0:T(8,128)}), f32[16,12,1280]{2,1,0:T(8,128)S(1)}, u32[]{:S(2)}, u32[]{:S(2)}) async-start(f32[16,12,1280]{2,1,0:T(8,128)} %reshape.34), calls=%async_computation.1 | async-start | bytes 2621440 | tf_op jit(solution)/shard_map/all_to_all | solution.py:34
  126.1 77.3 %all-to-all-start.2 = ((bf16[16,12,640]{2,1,0:T(8,128)(2,1)}), bf16[16,12,640]{2,1,0:T(8,128)(2,1)S(1)}, u32[]{:S(2)}, u32[]{:S(2)}) async-start(bf16[16,12,640]{2,1,0:T(8,128)(2,1)} %broadcast_in_dim.11), calls=%async_computation.2 | async-start | bytes 655360 | tf_op jit(solution)/shard_map/all_to_all | solution.py:13
  203.4 27.0 %all-to-all-start.6 = ((f32[32,6,512]{2,1,0:T(8,128)}), f32[32,6,512]{2,1,0:T(8,128)S(1)}, u32[]{:S(2)}, u32[]{:S(2)}) async-start(f32[32,6,512]{2,1,0:T(8,128)} %reshape.35), calls=%async_computation.6 | async-start | bytes 1048576 | tf_op jit(solution)/shard_map/all_to_all | solution.py:34
  214.5 20.4 %copy-start.4 = (bf16[32,6,512]{2,1,0:T(8,128)(2,1)S(1)}, bf16[32,6,512]{2,1,0:T(8,128)(2,1)}, u32[]{:S(2)}) copy-start(bf16[32,6,512]{2,1,0:T(8,128)(2,1)} %copy-done.3) | copy-start | bytes 589828
  230.4 21.2 %all-to-all-start.3 = ((f32[32,6,512]{2,1,0:T(8,128)}), f32[32,6,512]{2,1,0:T(8,128)}, u32[]{:S(2)}, u32[]{:S(2)}) async-start(f32[32,6,512]{2,1,0:T(8,128)} %copy.18), calls=%async_computation.3 | async-start | bytes 1048576 | tf_op jit(solution)/shard_map/all_to_all | solution.py:34
where the time goes:
time: 254 us; the launch traced here: 253 us
  waiting for transfers between devices  95.1 us (37%)
  blocking collectives  82.5 us (32%)
  starting transfers between devices  53.4 us (21%)
  local copies, waits for them, and re-layouts  10.5 us (4%)
  matrix products  5.9 us (2%)
  other arithmetic  5.09 us (2%)
    all_to_all x4, waiting for transfers between devices, sum_at_owner(): lax.all_to_all(parts, axis, split_axis=0, concat_axis=0, tiled=True)  85.2 us
    all_gather x1, blocking collectives, side_by_side_2(): lax.all_gather(both, axis, axis=dim, tiled=True)  60.1 us
    all_to_all x4, starting transfers between devices, sum_at_owner(): lax.all_to_all(parts, axis, split_axis=0, concat_axis=0, tiled=True)  35.4 us
    all_to_all x1, blocking collectives, sent_to_all(): return lax.all_to_all(copies, axis, split_axis=0, concat_axis=0, tiled=True)  22.4 us
    all_to_all x2, starting transfers between devices, sent_to_all(): return lax.all_to_all(copies, axis, split_axis=0, concat_axis=0, tiled=True)  18 us
    all_to_all x2, waiting for transfers between devices, sent_to_all(): return lax.all_to_all(copies, axis, split_axis=0, concat_axis=0, tiled=True)  9.84 us
  transfers between devices with their start and end apart: 6, of which 5 were waited for; matrix products, arithmetic and copies ran while one was open for 6% of the time, Pallas kernels for 0%

commit v1 on v0

v1 whole, which is shorter than its diff:
```python
import jax
import jax.numpy as jnp
from jax import lax
from jax.sharding import PartitionSpec as P

keep_scale = 1.0 / 0.9
contract_last = (((1,), (1,)), ((), ()))
contract_first = (((0,), (0,)), ((), ()))
lanes = 128


def exchange(blocks, axis):
    return lax.all_to_all(blocks, axis, split_axis=0, concat_axis=0, tiled=True)


def sent_to_all(block, axis):
    copies = jnp.broadcast_to(block, (lax.axis_size(axis), *block.shape))
    return exchange(copies, axis)


def dot(a, b, dims=(((1,), (0,)), ((), ()))):
    return lax.dot_general(a, b, dims, preferred_element_type=jnp.float32)


def body(tokens, gate_weight, up_weight, down_weight, keep_mask, cotangent):
    bf16 = jnp.bfloat16
    rows, cols = lax.axis_size("row"), lax.axis_size("col")
    own, width = tokens.shape
    total = own * rows
    share, units = keep_mask.shape

    packed = jnp.concatenate([tokens.reshape(-1, lanes), cotangent.reshape(-1, lanes)], axis=0)
    arrived = sent_to_all(packed, "row")
    half = packed.shape[0] // 2
    all_tokens = arrived[:, :half].reshape(total, width)
    all_cot = arrived[:, half:].reshape(total, width)

    parts = [
        dot(all_tokens, gate_weight),
        dot(all_tokens, up_weight),
        dot(all_cot, down_weight, contract_last),
    ]
    parts = jnp.concatenate([p.astype(bf16).reshape(cols, share, units) for p in parts], axis=1)
    sums = exchange(parts, "col").astype(jnp.float32).sum(axis=0)
    gate_value, up_value, grad_hidden = jnp.split(sums, 3, axis=0)

    keep_factor = keep_mask.astype(jnp.float32) * keep_scale
    sigmoid_gate = jax.nn.sigmoid(gate_value)
    silu_gate = gate_value * sigmoid_gate
    hidden = silu_gate * up_value * keep_factor
    grad_pre = grad_hidden * keep_factor
    grad_gate = grad_pre * up_value * sigmoid_gate * (1.0 + gate_value * (1.0 - sigmoid_gate))
    grad_up = grad_pre * silu_gate
    mine = jnp.concatenate([hidden, grad_gate, grad_up], axis=0).astype(bf16)
    spread = sent_to_all(mine, "col")
    hidden_all, gate_all, up_all = (a.reshape(total, units) for a in jnp.split(spread, 3, axis=1))

    out_part = dot(hidden_all, down_weight).astype(bf16)
    in_part = (
        dot(gate_all, gate_weight, contract_last) + dot(up_all, up_weight, contract_last)
    ).astype(bf16)
    parts = jnp.concatenate([p.reshape(rows, -1, lanes) for p in (out_part, in_part)], axis=1)
    sums = exchange(parts, "row").astype(jnp.float32).sum(axis=0).astype(bf16)
    mixed_out, input_grad = (a.reshape(own, width) for a in jnp.split(sums, 2, axis=0))

    down_grad = dot(hidden_all, all_cot, contract_first).astype(bf16)
    gate_grad = dot(all_tokens, gate_all, contract_first).astype(bf16)
    up_grad = dot(all_tokens, up_all, contract_first).astype(bf16)
    return (mixed_out, input_grad, gate_grad, up_grad, down_grad)


def solution(mesh):
    by_row, by_col = P("row", "col"), P("col", "row")
    return jax.shard_map(
        body,
        mesh=mesh,
        in_specs=(by_row, by_col, by_col, by_row, by_col, by_row),
        out_specs=(by_row, by_row, by_col, by_col, by_row),
        check_vma=False,
    )
```

time: 254 us -> 131 us (0.52)
  waiting for transfers between devices: 95.1 us -> 10.4 us
  starting transfers between devices: 53.4 us -> 5.75 us
  blocking collectives: 82.5 us -> 96.3 us
  other arithmetic: 5.09 us -> 1.25 us
    all_to_all x6 -> x1, waiting for transfers between devices: 95.1 us -> 10.4 us  [exchange(): return lax.all_to_all(blocks, axis, split_axis=0, concat_axis=0, tiled=True)]
    all_to_all x1 -> x3, blocking collectives: 22.4 us -> 96.3 us  [exchange(): return lax.all_to_all(blocks, axis, split_axis=0, concat_axis=0, tiled=True)]
    all_gather x1 -> x0, blocking collectives: 60.1 us -> none  [side_by_side_2(): lax.all_gather(both, axis, axis=dim, tiled=True)]
    all_to_all x6 -> x1, starting transfers between devices: 53.4 us -> 5.75 us  [exchange(): return lax.all_to_all(blocks, axis, split_axis=0, concat_axis=0, tiled=True)]
    reduce_sum x4 -> x2, other arithmetic: 4.17 us -> 0.2 us  [the longest x1 0.13 us: body(): sums = exchange(parts, 'col').astype(jnp.float32).sum(axis=0)]
    reshape x5 -> x14, local copies, waits for them, and re-layouts: 2.23 us -> 6.16 us  [the longest x2 1.23 us: body(): a.reshape(own, width)]
    broadcast_in_dim x3 -> x2, local copies, waits for them, and re-layouts: 2.98 us -> 0.12 us  [sent_to_all(): copies = jnp.broadcast_to(block, (lax.axis_size(axis), *block.shape))]
  transfers between devices with their start and end apart: 6 -> 1, of which waited for: 5 -> 1; matrix products, arithmetic and copies ran while one was open for 6% -> 3% of each run, Pallas kernels for 0% -> 0%
where the time goes in v1:
time: 131 us
  blocking collectives  96.3 us (74%)
  waiting for transfers between devices  10.4 us (8%)
  local copies, waits for them, and re-layouts  9.53 us (7%)
  matrix products  6.49 us (5%)
  starting transfers between devices  5.75 us (4%)
    all_to_all x3, blocking collectives, exchange(): return lax.all_to_all(blocks, axis, split_axis=0, concat_axis=0, tiled=True)  96.3 us
    all_to_all x1, waiting for transfers between devices, exchange(): return lax.all_to_all(blocks, axis, split_axis=0, concat_axis=0, tiled=True)  10.4 us
    dot_general x9, matrix products, dot(): return lax.dot_general(a, b, dims, preferred_element_type=jnp.float32)  6.49 us
    all_to_all x1, starting transfers between devices, exchange(): return lax.all_to_all(blocks, axis, split_axis=0, concat_axis=0, tiled=True)  5.75 us
  transfers between devices with their start and end apart: 1, of which 1 were waited for; matrix products, arithmetic and copies ran while one was open for 3% of the time, Pallas kernels for 0%

profile of v1, /device:TPU:1, one launch (start us, length us, event | category | flops | bytes accessed | tf_op | source)
XLA Modules:
  0.0 130.5 jit_solution(13509729902003332584)
XLA Ops:
  0.6 0.0 copy-start
  0.6 0.8 reshape.52
  1.4 0.7 reshape.53
  2.2 0.1 broadcast_in_dim.6
  2.2 25.2 %all_to_all.20 = bf16[32,48,128]{2,1,0:T(8,128)(2,1)S(1)} all-to-all(bf16[32,48,128]{2,1,0:T(8,128)(2,1)S(1)} %broadcast_in_dim.6), channel_id=1, replica_groups=mesh['row'=32,'col'=16] {'row'}, dimensions={0} | all-to-all | bytes 786432 | tf_op jit(solution)/shard_map/all_to_all | solution.py:13
  27.4 0.1 reshape.54
  27.6 0.1 reshape.57
  27.7 0.0 copy-done
  27.7 0.0 copy-start.2
  27.7 0.4 convolution_convert_fusion.3
  28.1 0.1 reshape.58
  28.2 0.6 copy-done.2
  28.8 0.0 copy-start.1
  28.8 0.3 convolution_convert_fusion.4
  29.2 0.1 reshape.56
  29.2 0.7 copy-done.1
  29.9 1.0 convolution_convert_fusion.5
  30.9 1.0 reshape.55
  31.9 0.2 pad_maximum_fusion
  32.1 39.6 %all_to_all.21 = bf16[16,36,640]{2,1,0:T(8,128)(2,1)S(1)} all-to-all(bf16[16,36,640]{2,1,0:T(8,128)(2,1)S(1)} %pad_maximum_fusion), channel_id=1, replica_groups=mesh['row'=32,'col'=16] {'col'}, dimensions={0} | all-to-all | bytes 1474560 | tf_op jit(solution)/shard_map/all_to_all | solution.py:13
  71.8 0.0 copy-start.4
  71.8 0.1 convert_reduce_fusion
  71.9 0.6 copy-done.4
  72.6 0.1 broadcast_in_dim.7
  72.7 31.4 %all_to_all.22 = bf16[16,36,640]{2,1,0:T(8,128)(2,1)S(1)} all-to-all(bf16[16,36,640]{2,1,0:T(8,128)(2,1)S(1)} %broadcast_in_dim.7), channel_id=1, replica_groups=mesh['row'=32,'col'=16] {'col'}, dimensions={0} | all-to-all | bytes 1474560 | tf_op jit(solution)/shard_map/all_to_all | solution.py:13
  104.1 0.8 fusion.2
  105.0 0.1 reshape.59
  105.0 0.3 convolution_convert_fusion.6
  105.4 0.8 reshape.60
  106.2 1.0 reshape.62
  107.2 0.1 reshape.61
  107.3 0.4 fusion.5
  107.6 0.0 copy-start.3
  107.7 0.4 fusion
  108.0 0.1 reshape.63
  108.2 0.4 copy-done.3
  108.6 0.8 pad_maximum_fusion.1
  109.4 5.8 %all-to-all-start.3 = ((bf16[32,48,128]{2,1,0:T(8,128)(2,1)}), bf16[32,48,128]{2,1,0:T(8,128)(2,1)S(1)}, u32[]{:S(2)}, u32[]{:S(2)}) async-start(bf16[32,48,128]{2,1,0:T(8,128)(2,1)} %pad_maximum_fusion.1), calls=%async_computation.3 | async-start | bytes 786432 | tf_op jit(solution)/shard_map/all_to_all | solution.py:13
  115.1 1.2 convolution_convert_fusion
  116.3 1.2 convolution_convert_fusion.1
  117.6 1.2 convolution_convert_fusion.2
  118.8 10.4 %all-to-all-done.3 = bf16[32,48,128]{2,1,0:T(8,128)(2,1)S(1)} async-done(((bf16[32,48,128]{2,1,0:T(8,128)(2,1)}), bf16[32,48,128]{2,1,0:T(8,128)(2,1)S(1)}, u32[]{:S(2)}, u32[]{:S(2)}) %all-to-all-start.3) | async-done | bytes 393248 | tf_op jit(solution)/shard_map/all_to_all | solution.py:13
  129.2 0.1 reduce_sum.22
  129.3 0.6 reshape.65
  129.9 0.6 reshape.64
  (5 shorter events, 0.1 us)
Async XLA Ops:
  0.6 27.1 %copy-start = (bf16[640,512]{1,0:T(8,128)(2,1)S(1)}, bf16[640,512]{1,0:T(8,128)(2,1)}, u32[]{:S(2)}) copy-start(bf16[640,512]{1,0:T(8,128)(2,1)} %param.9) | copy-start | bytes 1966084
  27.7 1.1 copy-start.2
  28.8 1.1 copy-start.1
  71.8 0.8 copy-start.4
  107.6 0.9 copy-start.3
  109.4 19.9 %all-to-all-start.3 = ((bf16[32,48,128]{2,1,0:T(8,128)(2,1)}), bf16[32,48,128]{2,1,0:T(8,128)(2,1)S(1)}, u32[]{:S(2)}, u32[]{:S(2)}) async-start(bf16[32,48,128]{2,1,0:T(8,128)(2,1)} %pad_maximum_fusion.1), calls=%async_computation.3 | async-start | bytes 786432 | tf_op jit(solution)/shard_map/all_to_all | solution.py:13

commit v2 on v1

v2 whole, which is shorter than its diff:
```python
import jax
import jax.numpy as jnp
from jax import lax
from jax.sharding import Mesh
from jax.sharding import PartitionSpec as P

keep_scale = 1.0 / 0.9
contract_last = (((1,), (1,)), ((), ()))
contract_first = (((0,), (0,)), ((), ()))
lanes = 128
plane = ("x", "zl")


def exchange(blocks, axis):
    return lax.all_to_all(blocks, axis, split_axis=0, concat_axis=0, tiled=True)


def sent_to_all(block, axis):
    copies = jnp.broadcast_to(block, (lax.axis_size(axis), *block.shape))
    return exchange(copies, axis)


def swapped(value, axis):
    return lax.ppermute(value, axis, [(0, 1), (1, 0)])


def in_order(mine, other, axis, dim):
    first = lax.axis_index(axis) == 0
    a, b = jnp.where(first, mine, other), jnp.where(first, other, mine)
    return jnp.stack([a, b], axis=dim)


def dot(a, b, dims=(((1,), (0,)), ((), ()))):
    return lax.dot_general(a, b, dims, preferred_element_type=jnp.float32)


def body(tokens, gate_weight, up_weight, down_weight, keep_mask, cotangent):
    bf16, f32 = jnp.bfloat16, jnp.float32
    own, width = tokens.shape
    share, units = keep_mask.shape
    ring = lax.axis_size("y")
    total = share * 2 * ring
    chips = total // own // 2

    packed = jnp.concatenate([tokens.reshape(-1, lanes), cotangent.reshape(-1, lanes)], axis=0)
    half = packed.shape[0] // 2
    near = sent_to_all(packed, plane)
    both = in_order(near, swapped(near, "core"), "core", 1)
    all_tokens = both[:, :, :half].reshape(total, width)
    all_cot = both[:, :, half:].reshape(total, width)

    parts = [
        dot(all_tokens, gate_weight),
        dot(all_tokens, up_weight),
        dot(all_cot, down_weight, contract_last),
    ]
    parts = jnp.concatenate([p.astype(bf16).reshape(ring, 2 * share, units) for p in parts], axis=1)
    sums = exchange(parts, "y").astype(f32).sum(axis=0)
    sums = sums + swapped(sums, "zh")
    gate_value, up_value, grad_hidden = jnp.split(sums, 3, axis=0)

    keep = keep_mask.astype(bf16)
    keep = in_order(keep, swapped(keep, "zh"), "zh", 0).reshape(2 * share, units)
    keep_factor = keep.astype(f32) * keep_scale
    sigmoid_gate = jax.nn.sigmoid(gate_value)
    silu_gate = gate_value * sigmoid_gate
    hidden = silu_gate * up_value * keep_factor
    grad_pre = grad_hidden * keep_factor
    grad_gate = grad_pre * up_value * sigmoid_gate * (1.0 + gate_value * (1.0 - sigmoid_gate))
    grad_up = grad_pre * silu_gate
    mine = jnp.concatenate([hidden, grad_gate, grad_up], axis=0).astype(bf16)
    spread = sent_to_all(mine, "y")
    hidden_all, gate_all, up_all = (a.reshape(total, units) for a in jnp.split(spread, 3, axis=1))

    out_part = dot(hidden_all, down_weight)
    in_part = dot(gate_all, gate_weight, contract_last) + dot(up_all, up_weight, contract_last)
    parts = jnp.stack([p.reshape(chips, 2, -1, lanes) for p in (out_part, in_part)], axis=2)
    core = lax.axis_index("core")
    kept = jnp.where(core == 0, parts[:, 0], parts[:, 1])
    given = jnp.where(core == 0, parts[:, 1], parts[:, 0])
    parts = (kept + swapped(given, "core")).astype(bf16).reshape(chips, -1, lanes)
    sums = exchange(parts, plane).astype(f32).sum(axis=0).astype(bf16)
    mixed_out, input_grad = (a.reshape(own, width) for a in jnp.split(sums, 2, axis=0))

    down_grad = dot(hidden_all, all_cot, contract_first).astype(bf16)
    gate_grad = dot(all_tokens, gate_all, contract_first).astype(bf16)
    up_grad = dot(all_tokens, up_all, contract_first).astype(bf16)
    return (mixed_out, input_grad, gate_grad, up_grad, down_grad)


def solution(mesh):
    fine = Mesh(mesh.devices.reshape(4, 4, 2, 8, 2), ("x", "zl", "core", "y", "zh"))
    row, col = ("x", "zl", "core"), ("y", "zh")
    by_row, by_col = P(row, col), P(col, row)
    return jax.shard_map(
        body,
        mesh=fine,
        in_specs=(by_row, by_col, by_col, by_row, by_col, by_row),
        out_specs=(by_row, by_row, by_col, by_col, by_row),
        check_vma=False,
    )
```

time: 131 us -> 119 us (0.908)
  blocking collectives: 96.3 us -> 38.4 us
  starting transfers between devices: 5.75 us -> 40.7 us
  waiting for transfers between devices: 10.4 us -> 25.2 us
  local copies, waits for them, and re-layouts: 9.53 us -> 4.54 us
    all_to_all x3 -> x2, blocking collectives: 96.3 us -> 38.4 us  [exchange(): return lax.all_to_all(blocks, axis, split_axis=0, concat_axis=0, tiled=True)]
    ppermute x0 -> x4, starting transfers between devices: none -> 27.4 us  [swapped(): return lax.ppermute(value, axis, [(0, 1), (1, 0)])]
    all_to_all x1 -> x2, waiting for transfers between devices: 10.4 us -> 19.6 us  [exchange(): return lax.all_to_all(blocks, axis, split_axis=0, concat_axis=0, tiled=True)]
    all_to_all x1 -> x2, starting transfers between devices: 5.75 us -> 13.3 us  [exchange(): return lax.all_to_all(blocks, axis, split_axis=0, concat_axis=0, tiled=True)]
    ppermute x0 -> x4, waiting for transfers between devices: none -> 5.61 us  [swapped(): return lax.ppermute(value, axis, [(0, 1), (1, 0)])]
    reshape x10 -> x2, local copies, waits for them, and re-layouts: 3.44 us -> 0.25 us  [the longest x1 0.13 us: body(): all_tokens = both[:, :, :half].reshape(total, width)]
  transfers between devices with their start and end apart: 1 -> 6, of which waited for: 1 -> 5; matrix products, arithmetic and copies ran while one was open for 3% -> 3% of each run, Pallas kernels for 0% -> 0%
where the time goes in v2:
time: 119 us; the launch traced here: 118 us
  starting transfers between devices  40.7 us (34%)
  blocking collectives  38.4 us (32%)
  waiting for transfers between devices  25.2 us (21%)
  matrix products  5.78 us (5%)
  local copies, waits for them, and re-layouts  4.54 us (4%)
  other arithmetic  2.07 us (2%)
    all_to_all x2, blocking collectives, exchange(): return lax.all_to_all(blocks, axis, split_axis=0, concat_axis=0, tiled=True)  38.4 us
    ppermute x4, starting transfers between devices, swapped(): return lax.ppermute(value, axis, [(0, 1), (1, 0)])  27.4 us
    all_to_all x2, waiting for transfers between devices, exchange(): return lax.all_to_all(blocks, axis, split_axis=0, concat_axis=0, tiled=True)  19.6 us
    all_to_all x2, starting transfers between devices, exchange(): return lax.all_to_all(blocks, axis, split_axis=0, concat_axis=0, tiled=True)  13.3 us
    dot_general x9, matrix products, dot(): return lax.dot_general(a, b, dims, preferred_element_type=jnp.float32)  5.78 us
    ppermute x4, waiting for transfers between devices, swapped(): return lax.ppermute(value, axis, [(0, 1), (1, 0)])  5.61 us
  transfers between devices with their start and end apart: 6, of which 5 were waited for; matrix products, arithmetic and copies ran while one was open for 3% of the time, Pallas kernels for 0%

profile of v2, /device:TPU:1, one launch (start us, length us, event | category | flops | bytes accessed | tf_op | source)
XLA Modules:
  0.0 117.5 jit_solution(5807913643148238579)
XLA Ops:
  0.6 0.0 copy-start
  0.6 0.8 reshape.57
  1.4 0.7 reshape.58
  2.2 17.7 %all_to_all.20 = bf16[16,48,128]{2,1,0:T(8,128)(2,1)S(1)} all-to-all(bf16[16,48,128]{2,1,0:T(8,128)(2,1)S(1)} %broadcast_in_dim.6), channel_id=1, replica_groups=mesh['x'=4,'zl'=4,'core'=2,'y'=8,'zh'=2] {'x','zl'}, dimensions={0} | all-to-all | bytes 393216 | tf_op jit(solution)/shard_map/all_to_all | solution.py:15
  19.9 4.8 %collective-permute-start = (bf16[16,48,128]{2,1,0:T(8,128)(2,1)S(1)}, bf16[16,48,128]{2,1,0:T(8,128)(2,1)S(1)}, u32[]{:S(2)}, u32[]{:S(2)}) collective-permute-start(bf16[16,48,128]{2,1,0:T(8,128)(2,1)S(1)} %all_to_all.20), channel_id=1, source_target_pairs={{0,16},{16,0},{1,17},{17,1},{2,18},{18,2},{3,19},{19,3},{4,20},{20... | collective-permute-start | bytes 589832 | tf_op jit(solution)/shard_map/ppermute | solution.py:24
  24.7 1.0 collective-permute-done
  25.8 0.1 fusion.1
  25.8 0.0 copy-start.1
  25.9 0.1 reshape.59
  26.0 0.0 copy-done
  26.0 0.3 convolution_convert_fusion.5
  26.3 0.6 copy-done.1
  26.9 0.0 copy-start.2
  26.9 0.3 convolution_convert_fusion.4
  27.3 0.1 reshape.62
  27.4 0.6 copy-done.2
  28.0 0.4 convolution_convert_fusion.3
  28.4 0.9 pad_maximum_fusion
  29.3 0.0 copy-start.3
  29.3 7.0 %all-to-all-start.1 = ((bf16[8,72,640]{2,1,0:T(8,128)(2,1)}), bf16[8,72,640]{2,1,0:T(8,128)(2,1)S(1)}, u32[]{:S(2)}, u32[]{:S(2)}) async-start(bf16[8,72,640]{2,1,0:T(8,128)(2,1)} %pad_maximum_fusion), calls=%async_computation.1 | async-start | bytes 1474560 | tf_op jit(solution)/shard_map/all_to_all | solution.py:15
  36.3 0.0 copy-done.3
  36.3 7.9 %collective-permute-start.2 = (bf16[12,640]{1,0:T(8,128)(2,1)S(1)}, bf16[12,640]{1,0:T(8,128)(2,1)S(1)}, u32[]{:S(2)}, u32[]{:S(2)}) collective-permute-start(bf16[12,640]{1,0:T(8,128)(2,1)S(1)} %convert_element_type.38), channel_id=1, source_target_pairs={{0,1},{1,0},{2,3},{3,2},{4,5},{5,4},{6,7},{7,6},{8,9},{9,8},{10,11... | collective-permute-start | bytes 46088 | tf_op jit(solution)/shard_map/ppermute | solution.py:24
  44.3 14.5 %all-to-all-done.1 = bf16[8,72,640]{2,1,0:T(8,128)(2,1)S(1)} async-done(((bf16[8,72,640]{2,1,0:T(8,128)(2,1)}), bf16[8,72,640]{2,1,0:T(8,128)(2,1)S(1)}, u32[]{:S(2)}, u32[]{:S(2)}) %all-to-all-start.1) | async-done | bytes 737312 | tf_op jit(solution)/shard_map/all_to_all | solution.py:15
  58.8 0.1 convert_reduce_fusion
  58.9 7.9 %collective-permute-start.1 = (f32[72,640]{1,0:T(8,128)S(1)}, f32[72,640]{1,0:T(8,128)S(1)}, u32[]{:S(2)}, u32[]{:S(2)}) collective-permute-start(f32[72,640]{1,0:T(8,128)S(1)} %convert_reduce_fusion), channel_id=1, source_target_pairs={{0,1},{1,0},{2,3},{3,2},{4,5},{5,4},{6,7},{7,6},{8,9},{9,8},{10,11... | collective-permute-start | bytes 552968 | tf_op jit(solution)/shard_map/ppermute | solution.py:24
  66.9 0.0 collective-permute-done.2
  66.9 4.4 %collective-permute-done.1 = f32[72,640]{1,0:T(8,128)S(1)} collective-permute-done((f32[72,640]{1,0:T(8,128)S(1)}, f32[72,640]{1,0:T(8,128)S(1)}, u32[]{:S(2)}, u32[]{:S(2)}) %collective-permute-start.1) | collective-permute-done | bytes 184352 | tf_op jit(solution)/shard_map/ppermute | solution.py:24
  71.4 0.1 multiply_convert_fusion.2
  71.5 0.1 broadcast_in_dim.7
  71.5 20.7 %all_to_all.21 = bf16[8,72,640]{2,1,0:T(8,128)(2,1)S(1)} all-to-all(bf16[8,72,640]{2,1,0:T(8,128)(2,1)S(1)} %broadcast_in_dim.7), channel_id=1, replica_groups=mesh['x'=4,'zl'=4,'core'=2,'y'=8,'zh'=2] {'y'}, dimensions={0} | all-to-all | bytes 1474560 | tf_op jit(solution)/shard_map/all_to_all | solution.py:15
  92.2 0.1 fusion.4
  92.3 0.4 fusion.7
  92.7 0.4 convolution_add_fusion
  93.1 0.3 fusion.6
  93.5 0.1 fusion.3
  93.6 6.7 %collective-permute-start.3 = (f32[16,2,24,128]{3,2,1,0:T(8,128)S(1)}, f32[16,2,24,128]{3,2,1,0:T(8,128)S(1)}, u32[]{:S(2)}, u32[]{:S(2)}) collective-permute-start(f32[16,2,24,128]{3,2,1,0:T(8,128)S(1)} %select_bitcast_fusion), channel_id=1, source_target_pairs={{0,16},{16,0},{1,17},{17,1},{2,18},{18,2},{3,19},{19,3},{4,20},{20... | collective-permute-start | bytes 1179656 | tf_op jit(solution)/shard_map/ppermute | solution.py:24
  100.3 1.2 %convolution_convert_fusion = bf16[640,512]{1,0:T(8,128)(2,1)} fusion(bf16[192,640]{1,0:T(8,128)(2,1)S(1)} %bitcast.50, bf16[192,512]{1,0:T(8,128)(2,1)S(1)} %reshape.62), kind=kOutput, calls=%fused_computation.1 | convolution fusion | flops 126156800 | bytes 1097728 | tf_op jit(solution)/shard_map/dot_general | solution.py:34
  101.5 0.1 collective-permute-done.3
  101.6 0.8 fusion
  102.4 6.4 %all-to-all-start.3 = ((bf16[16,48,128]{2,1,0:T(8,128)(2,1)}), bf16[16,48,128]{2,1,0:T(8,128)(2,1)S(1)}, u32[]{:S(2)}, u32[]{:S(2)}) async-start(bf16[16,48,128]{2,1,0:T(8,128)(2,1)} %bitcast.13), calls=%async_computation.3 | async-start | bytes 393216 | tf_op jit(solution)/shard_map/all_to_all | solution.py:15
  108.8 1.2 %convolution_convert_fusion.1 = bf16[512,640]{1,0:T(8,128)(2,1)} fusion(bf16[192,512]{1,0:T(8,128)(2,1)S(1)} %reshape.59, bf16[192,640]{1,0:T(8,128)(2,1)S(1)} %bitcast.48), kind=kOutput, calls=%fused_computation.2 | convolution fusion | flops 126156800 | bytes 1097728 | tf_op jit(solution)/shard_map/dot_general | solution.py:34
  110.0 1.2 %convolution_convert_fusion.2 = bf16[512,640]{1,0:T(8,128)(2,1)} fusion(bf16[192,512]{1,0:T(8,128)(2,1)S(1)} %reshape.59, bf16[192,640]{1,0:T(8,128)(2,1)S(1)} %bitcast.46), kind=kOutput, calls=%fused_computation.3 | convolution fusion | flops 126156800 | bytes 1097728 | tf_op jit(solution)/shard_map/dot_general | solution.py:34
  111.3 5.0 %all-to-all-done.3 = bf16[16,48,128]{2,1,0:T(8,128)(2,1)S(1)} async-done(((bf16[16,48,128]{2,1,0:T(8,128)(2,1)}), bf16[16,48,128]{2,1,0:T(8,128)(2,1)S(1)}, u32[]{:S(2)}, u32[]{:S(2)}) %all-to-all-start.3) | async-done | bytes 196640 | tf_op jit(solution)/shard_map/all_to_all | solution.py:15
  116.3 0.6 reshape.68
  116.9 0.6 reshape.69
  (16 shorter events, 0.3 us)
Async XLA Ops:
  0.6 25.4 %copy-start = (bf16[512,640]{1,0:T(8,128)(2,1)S(1)}, bf16[512,640]{1,0:T(8,128)(2,1)}, u32[]{:S(2)}) copy-start(bf16[512,640]{1,0:T(8,128)(2,1)} %param.7) | copy-start | bytes 1966084
  19.9 5.9 %collective-permute-start = (bf16[16,48,128]{2,1,0:T(8,128)(2,1)S(1)}, bf16[16,48,128]{2,1,0:T(8,128)(2,1)S(1)}, u32[]{:S(2)}, u32[]{:S(2)}) collective-permute-start(bf16[16,48,128]{2,1,0:T(8,128)(2,1)S(1)} %all_to_all.20), channel_id=1, source_target_pairs={{0,16},{16,0},{1,17},{17,1},{2,18},{18,2},{3,19},{19,3},{4,20},{20... | collective-permute-start | bytes 589832 | tf_op jit(solution)/shard_map/ppermute | solution.py:24
  25.8 1.1 copy-start.1
  26.9 1.1 copy-start.2
  29.3 7.0 %copy-start.3 = (s32[12,640]{1,0:T(8,128)S(1)}, s32[12,640]{1,0:T(8,128)}, u32[]{:S(2)}) copy-start(s32[12,640]{1,0:T(8,128)} %param.10) | copy-start | bytes 92164
  29.3 29.5 %all-to-all-start.1 = ((bf16[8,72,640]{2,1,0:T(8,128)(2,1)}), bf16[8,72,640]{2,1,0:T(8,128)(2,1)S(1)}, u32[]{:S(2)}, u32[]{:S(2)}) async-start(bf16[8,72,640]{2,1,0:T(8,128)(2,1)} %pad_maximum_fusion), calls=%async_computation.1 | async-start | bytes 1474560 | tf_op jit(solution)/shard_map/all_to_all | solution.py:15
  36.3 30.5 %collective-permute-start.2 = (bf16[12,640]{1,0:T(8,128)(2,1)S(1)}, bf16[12,640]{1,0:T(8,128)(2,1)S(1)}, u32[]{:S(2)}, u32[]{:S(2)}) collective-permute-start(bf16[12,640]{1,0:T(8,128)(2,1)S(1)} %convert_element_type.38), channel_id=1, source_target_pairs={{0,1},{1,0},{2,3},{3,2},{4,5},{5,4},{6,7},{7,6},{8,9},{9,8},{10,11... | collective-permute-start | bytes 46088 | tf_op jit(solution)/shard_map/ppermute | solution.py:24
  58.9 12.5 %collective-permute-start.1 = (f32[72,640]{1,0:T(8,128)S(1)}, f32[72,640]{1,0:T(8,128)S(1)}, u32[]{:S(2)}, u32[]{:S(2)}) collective-permute-start(f32[72,640]{1,0:T(8,128)S(1)} %convert_reduce_fusion), channel_id=1, source_target_pairs={{0,1},{1,0},{2,3},{3,2},{4,5},{5,4},{6,7},{7,6},{8,9},{9,8},{10,11... | collective-permute-start | bytes 552968 | tf_op jit(solution)/shard_map/ppermute | solution.py:24
  93.6 8.0 %collective-permute-start.3 = (f32[16,2,24,128]{3,2,1,0:T(8,128)S(1)}, f32[16,2,24,128]{3,2,1,0:T(8,128)S(1)}, u32[]{:S(2)}, u32[]{:S(2)}) collective-permute-start(f32[16,2,24,128]{3,2,1,0:T(8,128)S(1)} %select_bitcast_fusion), channel_id=1, source_target_pairs={{0,16},{16,0},{1,17},{17,1},{2,18},{18,2},{3,19},{19,3},{4,20},{20... | collective-permute-start | bytes 1179656 | tf_op jit(solution)/shard_map/ppermute | solution.py:24
  102.4 13.9 %all-to-all-start.3 = ((bf16[16,48,128]{2,1,0:T(8,128)(2,1)}), bf16[16,48,128]{2,1,0:T(8,128)(2,1)S(1)}, u32[]{:S(2)}, u32[]{:S(2)}) async-start(bf16[16,48,128]{2,1,0:T(8,128)(2,1)} %bitcast.13), calls=%async_computation.3 | async-start | bytes 393216 | tf_op jit(solution)/shard_map/all_to_all | solution.py:15

commit v3 on v2

--- a/solution.py
+++ b/solution.py
@@ -1,6 +1,8 @@
 import jax
 import jax.numpy as jnp
 from jax import lax
+from jax.experimental import pallas as pl
+from jax.experimental.pallas import tpu as pltpu
 from jax.sharding import Mesh
 from jax.sharding import PartitionSpec as P
 
@@ -24,14 +26,49 @@
     return lax.ppermute(value, axis, [(0, 1), (1, 0)])
 
 
-def in_order(mine, other, axis, dim):
-    first = lax.axis_index(axis) == 0
+def in_order(mine, other, first, dim):
     a, b = jnp.where(first, mine, other), jnp.where(first, other, mine)
     return jnp.stack([a, b], axis=dim)
 
 
 def dot(a, b, dims=(((1,), (0,)), ((), ()))):
     return lax.dot_general(a, b, dims, preferred_element_type=jnp.float32)
+
+
+def products(tokens, cotangent, gate_weight, up_weight, down_weight, keep_mask, ring):
+    total, units = tokens.shape[0], gate_weight.shape[1]
+    rows = total // ring
+
+    def kernel(t_ref, c_ref, g_ref, u_ref, d_ref, k_ref, out_ref, keep_ref):
+        def put(at, value):
+            value = value.astype(out_ref.dtype)
+            for y in range(ring):
+                out_ref[y, at * rows : (at + 1) * rows, :] = value[y * rows : (y + 1) * rows]
+
+        keep_ref[...] = k_ref[...].astype(jnp.float32)
+        put(0, dot(t_ref[...], g_ref[...]))
+        put(1, dot(t_ref[...], u_ref[...]))
+        put(2, dot(c_ref[...], d_ref[...], contract_last))
+
+    operands = (tokens, cotangent, gate_weight, up_weight, down_weight, keep_mask)
+    operands = tuple(pltpu.with_memory_space_constraint(a, pltpu.VMEM) for a in operands)
+    in_vmem = pl.BlockSpec(memory_space=pltpu.VMEM)
+    return pl.pallas_call(
+        kernel,
+        out_shape=(
+            pltpu.VMEM((ring, 3 * rows, units), tokens.dtype),
+            pltpu.VMEM(keep_mask.shape, jnp.float32),
+        ),
+        in_specs=[in_vmem] * len(operands),
+        out_specs=(in_vmem, in_vmem),
+        cost_estimate=pl.CostEstimate(
+            flops=6 * total * tokens.shape[1] * units,
+            bytes_accessed=sum(2 * a.size for a in operands),
+            transcendentals=0,
+        ),
+        compiler_params=pltpu.CompilerParams(vmem_limit_bytes=8 << 20),
+        name="products",
+    )(*operands)
 
 
 def body(tokens, gate_weight, up_weight, down_weight, keep_mask, cotangent):
@@ -42,26 +79,23 @@
     total = share * 2 * ring
     chips = total // own // 2
 
-    packed = jnp.concatenate([tokens.reshape(-1, lanes), cotangent.reshape(-1, lanes)], axis=0)
+    packed = jnp.concatenate([tokens, cotangent], axis=0).reshape(-1, lanes)
     half = packed.shape[0] // 2
+    places = lax.axis_index("core"), lax.axis_index("zh")
+    packed, core, side = lax.optimization_barrier((packed, *places))
     near = sent_to_all(packed, plane)
-    both = in_order(near, swapped(near, "core"), "core", 1)
+    both = in_order(near, swapped(near, "core"), core == 0, 1)
     all_tokens = both[:, :, :half].reshape(total, width)
     all_cot = both[:, :, half:].reshape(total, width)
 
-    parts = [
-        dot(all_tokens, gate_weight),
-        dot(all_tokens, up_weight),
-        dot(all_cot, down_weight, contract_last),
-    ]
-    parts = jnp.concatenate([p.astype(bf16).reshape(ring, 2 * share, units) for p in parts], axis=1)
+    parts, keep = products(all_tokens, all_cot, gate_weight, up_weight, down_weight, keep_mask, ring)
     sums = exchange(parts, "y").astype(f32).sum(axis=0)
-    sums = sums + swapped(sums, "zh")
+    other = swapped(jnp.concatenate([sums, keep], axis=0), "zh")
+    sums = sums + other[: sums.shape[0]]
+    keep = in_order(keep, other[sums.shape[0] :], side == 0, 0).reshape(2 * share, units)
     gate_value, up_value, grad_hidden = jnp.split(sums, 3, axis=0)
 
-    keep = keep_mask.astype(bf16)
-    keep = in_order(keep, swapped(keep, "zh"), "zh", 0).reshape(2 * share, units)
-    keep_factor = keep.astype(f32) * keep_scale
+    keep_factor = keep * keep_scale
     sigmoid_gate = jax.nn.sigmoid(gate_value)
     silu_gate = gate_value * sigmoid_gate
     hidden = silu_gate * up_value * keep_factor
@@ -75,12 +109,11 @@
     out_part = dot(hidden_all, down_weight)
     in_part = dot(gate_all, gate_weight, contract_last) + dot(up_all, up_weight, contract_last)
     parts = jnp.stack([p.reshape(chips, 2, -1, lanes) for p in (out_part, in_part)], axis=2)
-    core = lax.axis_index("core")
     kept = jnp.where(core == 0, parts[:, 0], parts[:, 1])
     given = jnp.where(core == 0, parts[:, 1], parts[:, 0])
     parts = (kept + swapped(given, "core")).astype(bf16).reshape(chips, -1, lanes)
     sums = exchange(parts, plane).astype(f32).sum(axis=0).astype(bf16)
-    mixed_out, input_grad = (a.reshape(own, width) for a in jnp.split(sums, 2, axis=0))
+    mixed_out, input_grad = jnp.split(sums.reshape(2 * own, width), 2, axis=0)
 
     down_grad = dot(hidden_all, all_cot, contract_first).astype(bf16)
     gate_grad = dot(all_tokens, gate_all, contract_first).astype(bf16)

time: 119 us -> 116 us (0.975)
  blocking collectives: 38.4 us -> 69.4 us
  starting transfers between devices: 40.7 us -> 24.4 us
  waiting for transfers between devices: 25.2 us -> 10.3 us
  local copies, waits for them, and re-layouts: 4.54 us -> 2.95 us
    all_to_all x2 -> x3, blocking collectives: 38.4 us -> 69.4 us  [exchange(): return lax.all_to_all(blocks, axis, split_axis=0, concat_axis=0, tiled=True)]
    all_to_all x2 -> x1, waiting for transfers between devices: 19.6 us -> 5.02 us  [exchange(): return lax.all_to_all(blocks, axis, split_axis=0, concat_axis=0, tiled=True)]
    ppermute x4 -> x3, starting transfers between devices: 27.4 us -> 18.3 us  [swapped(): return lax.ppermute(value, axis, [(0, 1), (1, 0)])]
    all_to_all x2 -> x1, starting transfers between devices: 13.3 us -> 6.13 us  [exchange(): return lax.all_to_all(blocks, axis, split_axis=0, concat_axis=0, tiled=True)]
    reshape x4 -> x1, local copies, waits for them, and re-layouts: 2.72 us -> 0.02 us  [body(): packed = jnp.concatenate([tokens, cotangent], axis=0).reshape(-1, lanes)]
    split x1 -> x3, local copies, waits for them, and re-layouts: 0.01 us -> 1.23 us  [body(): mixed_out, input_grad = jnp.split(sums.reshape(2 * own, width), 2, axis=0)]
    dot_general x9 -> x6, matrix products: 5.78 us -> 4.75 us  [dot(): return lax.dot_general(a, b, dims, preferred_element_type=jnp.float32)]
    ppermute x4 -> x3, waiting for transfers between devices: 5.61 us -> 5.25 us  [swapped(): return lax.ppermute(value, axis, [(0, 1), (1, 0)])]
  transfers between devices with their start and end apart: 6 -> 4, of which waited for: 5 -> 4; matrix products, arithmetic and copies ran while one was open for 3% -> 3% of each run, Pallas kernels for 0% -> 0%
where the time goes in v3:
time: 116 us; the launch traced here: 115 us
  blocking collectives  69.4 us (60%)
  starting transfers between devices  24.4 us (21%)
  waiting for transfers between devices  10.3 us (9%)
  matrix products  4.75 us (4%)
  local copies, waits for them, and re-layouts  2.95 us (3%)
  other arithmetic  1.84 us (2%)
    all_to_all x3, blocking collectives, exchange(): return lax.all_to_all(blocks, axis, split_axis=0, concat_axis=0, tiled=True)  69.4 us
    ppermute x3, starting transfers between devices, swapped(): return lax.ppermute(value, axis, [(0, 1), (1, 0)])  18.3 us
    all_to_all x1, starting transfers between devices, exchange(): return lax.all_to_all(blocks, axis, split_axis=0, concat_axis=0, tiled=True)  6.13 us
    ppermute x3, waiting for transfers between devices, swapped(): return lax.ppermute(value, axis, [(0, 1), (1, 0)])  5.25 us
    all_to_all x1, waiting for transfers between devices, exchange(): return lax.all_to_all(blocks, axis, split_axis=0, concat_axis=0, tiled=True)  5.02 us
    dot_general x6, matrix products, dot(): return lax.dot_general(a, b, dims, preferred_element_type=jnp.float32)  4.75 us
  transfers between devices with their start and end apart: 4, of which 4 were waited for; matrix products, arithmetic and copies ran while one was open for 3% of the time, Pallas kernels for 0%

profile of v3, /device:TPU:1, one launch (start us, length us, event | category | flops | bytes accessed | tf_op | source)
XLA Modules:
  0.0 115.2 jit_solution(13666168932379375787)
XLA Ops:
  0.6 0.7 pad_maximum_fusion.3
  1.4 17.7 %all_to_all.20 = bf16[16,48,128]{2,1,0:T(8,128)(2,1)S(1)} all-to-all(bf16[16,48,128]{2,1,0:T(8,128)(2,1)S(1)} %broadcast_in_dim.6), channel_id=1, replica_groups=mesh['x'=4,'zl'=4,'core'=2,'y'=8,'zh'=2] {'x','zl'}, dimensions={0} | all-to-all | bytes 393216 | tf_op jit(solution)/shard_map/all_to_all | solution.py:17
  19.1 4.8 %collective-permute-start = (bf16[16,48,128]{2,1,0:T(8,128)(2,1)S(1)}, bf16[16,48,128]{2,1,0:T(8,128)(2,1)S(1)}, u32[]{:S(2)}, u32[]{:S(2)}) collective-permute-start(bf16[16,48,128]{2,1,0:T(8,128)(2,1)S(1)} %all_to_all.20), channel_id=1, source_target_pairs={{0,16},{16,0},{1,17},{17,1},{2,18},{18,2},{3,19},{19,3},{4,20},{20... | collective-permute-start | bytes 589832 | tf_op jit(solution)/shard_map/ppermute | solution.py:26
  23.9 1.0 collective-permute-done
  25.0 0.0 copy-start.2
  25.0 0.0 copy-start
  25.0 0.0 copy-start.1
  25.0 0.0 copy-start.3
  25.1 0.1 reshape.42.t_ref
  25.2 0.1 reshape.43.c_ref
  25.4 0.7 copy-done.2
  26.1 0.2 copy-done
  26.3 0.2 copy-done.1
  26.5 0.0 copy-done.3
  26.5 0.7 products.1
  27.2 27.8 %all_to_all.21 = bf16[8,72,640]{2,1,0:T(8,128)(2,1)S(1)} all-to-all(bf16[8,72,640]{2,1,0:T(8,128)(2,1)S(1)} %get-tuple-element.12), channel_id=1, replica_groups=mesh['x'=4,'zl'=4,'core'=2,'y'=8,'zh'=2] {'y'}, dimensions={0} | all-to-all | bytes 1474560 | tf_op jit(solution)/shard_map/all_to_all | solution.py:17
  55.0 0.1 convert_reduce_fusion
  55.1 7.9 %collective-permute-start.1 = (f32[84,640]{1,0:T(8,128)S(1)}, f32[84,640]{1,0:T(8,128)S(1)}, u32[]{:S(2)}, u32[]{:S(2)}) collective-permute-start(f32[84,640]{1,0:T(8,128)S(1)} %pad_maximum_fusion), channel_id=1, source_target_pairs={{0,1},{1,0},{2,3},{3,2},{4,5},{5,4},{6,7},{7,6},{8,9},{9,8},{10,11... | collective-permute-start | bytes 645128 | tf_op jit(solution)/shard_map/ppermute | solution.py:26
  63.1 4.1 %collective-permute-done.1 = f32[84,640]{1,0:T(8,128)S(1)} collective-permute-done((f32[84,640]{1,0:T(8,128)S(1)}, f32[84,640]{1,0:T(8,128)S(1)}, u32[]{:S(2)}, u32[]{:S(2)}) %collective-permute-start.1) | collective-permute-done | bytes 215072 | tf_op jit(solution)/shard_map/ppermute | solution.py:26
  67.2 0.1 multiply_convert_fusion.2
  67.3 0.1 broadcast_in_dim.7
  67.4 23.9 %all_to_all.22 = bf16[8,72,640]{2,1,0:T(8,128)(2,1)S(1)} all-to-all(bf16[8,72,640]{2,1,0:T(8,128)(2,1)S(1)} %broadcast_in_dim.7), channel_id=1, replica_groups=mesh['x'=4,'zl'=4,'core'=2,'y'=8,'zh'=2] {'y'}, dimensions={0} | all-to-all | bytes 1474560 | tf_op jit(solution)/shard_map/all_to_all | solution.py:17
  91.2 0.1 fusion.4
  91.3 0.4 fusion.7
  91.7 0.4 convolution_add_fusion
  92.1 0.3 fusion.6
  92.5 0.1 fusion.3
  92.7 5.5 %collective-permute-start.2 = (f32[16,2,24,128]{3,2,1,0:T(8,128)S(1)}, f32[16,2,24,128]{3,2,1,0:T(8,128)S(1)}, u32[]{:S(2)}, u32[]{:S(2)}) collective-permute-start(f32[16,2,24,128]{3,2,1,0:T(8,128)S(1)} %select_bitcast_fusion), channel_id=1, source_target_pairs={{0,16},{16,0},{1,17},{17,1},{2,18},{18,2},{3,19},{19,3},{4,20},{20... | collective-permute-start | bytes 1179656 | tf_op jit(solution)/shard_map/ppermute | solution.py:26
  98.2 1.2 %convolution_convert_fusion = bf16[640,512]{1,0:T(8,128)(2,1)} fusion(bf16[192,640]{1,0:T(8,128)(2,1)S(1)} %bitcast.41, bf16[192,512]{1,0:T(8,128)(2,1)S(1)} %reshape.43.c_ref), kind=kOutput, calls=%fused_computation.1 | convolution fusion | flops 126156800 | bytes 1097728 | tf_op jit(solution)/shard_map/dot_general | solution.py:35
  99.4 0.1 collective-permute-done.2
  99.5 0.7 fusion
  100.3 6.1 %all-to-all-start.3 = ((bf16[16,48,128]{2,1,0:T(8,128)(2,1)}), bf16[16,48,128]{2,1,0:T(8,128)(2,1)S(1)}, u32[]{:S(2)}, u32[]{:S(2)}) async-start(bf16[16,48,128]{2,1,0:T(8,128)(2,1)} %bitcast.10), calls=%async_computation.3 | async-start | bytes 393216 | tf_op jit(solution)/shard_map/all_to_all | solution.py:17
  106.4 1.2 %convolution_convert_fusion.1 = bf16[512,640]{1,0:T(8,128)(2,1)} fusion(bf16[192,512]{1,0:T(8,128)(2,1)S(1)} %reshape.42.t_ref, bf16[192,640]{1,0:T(8,128)(2,1)S(1)} %bitcast.39), kind=kOutput, calls=%fused_computation.2 | convolution fusion | flops 126156800 | bytes 1097728 | tf_op jit(solution)/shard_map/dot_general | solution.py:35
  107.7 1.2 %convolution_convert_fusion.2 = bf16[512,640]{1,0:T(8,128)(2,1)} fusion(bf16[192,512]{1,0:T(8,128)(2,1)S(1)} %reshape.42.t_ref, bf16[192,640]{1,0:T(8,128)(2,1)S(1)} %bitcast.37), kind=kOutput, calls=%fused_computation.3 | convolution fusion | flops 126156800 | bytes 1097728 | tf_op jit(solution)/shard_map/dot_general | solution.py:35
  108.9 5.0 %all-to-all-done.3 = bf16[16,48,128]{2,1,0:T(8,128)(2,1)S(1)} async-done(((bf16[16,48,128]{2,1,0:T(8,128)(2,1)}), bf16[16,48,128]{2,1,0:T(8,128)(2,1)S(1)}, u32[]{:S(2)}, u32[]{:S(2)}) %all-to-all-start.3) | async-done | bytes 196640 | tf_op jit(solution)/shard_map/all_to_all | solution.py:17
  114.0 0.6 split.35
  114.6 0.6 split.37
  (17 shorter events, 0.4 us)
Async XLA Ops:
  19.1 5.9 %collective-permute-start = (bf16[16,48,128]{2,1,0:T(8,128)(2,1)S(1)}, bf16[16,48,128]{2,1,0:T(8,128)(2,1)S(1)}, u32[]{:S(2)}, u32[]{:S(2)}) collective-permute-start(bf16[16,48,128]{2,1,0:T(8,128)(2,1)S(1)} %all_to_all.20), channel_id=1, source_target_pairs={{0,16},{16,0},{1,17},{17,1},{2,18},{18,2},{3,19},{19,3},{4,20},{20... | collective-permute-start | bytes 589832 | tf_op jit(solution)/shard_map/ppermute | solution.py:26
  25.0 1.1 copy-start.2
  25.0 1.3 %copy-start = (bf16[512,640]{1,0:T(8,128)(2,1)S(1)}, bf16[512,640]{1,0:T(8,128)(2,1)}, u32[]{:S(2)}) copy-start(bf16[512,640]{1,0:T(8,128)(2,1)} %u_ref.1) | copy-start | bytes 1966084
  25.0 1.4 %copy-start.1 = (bf16[512,640]{1,0:T(8,128)(2,1)S(1)}, bf16[512,640]{1,0:T(8,128)(2,1)}, u32[]{:S(2)}) copy-start(bf16[512,640]{1,0:T(8,128)(2,1)} %g_ref.1) | copy-start | bytes 1966084
  25.0 1.4 %copy-start.3 = (s32[12,640]{1,0:T(8,128)S(1)}, s32[12,640]{1,0:T(8,128)}, u32[]{:S(2)}) copy-start(s32[12,640]{1,0:T(8,128)} %k_ref.1) | copy-start | bytes 92164
  55.1 12.0 %collective-permute-start.1 = (f32[84,640]{1,0:T(8,128)S(1)}, f32[84,640]{1,0:T(8,128)S(1)}, u32[]{:S(2)}, u32[]{:S(2)}) collective-permute-start(f32[84,640]{1,0:T(8,128)S(1)} %pad_maximum_fusion), channel_id=1, source_target_pairs={{0,1},{1,0},{2,3},{3,2},{4,5},{5,4},{6,7},{7,6},{8,9},{9,8},{10,11... | collective-permute-start | bytes 645128 | tf_op jit(solution)/shard_map/ppermute | solution.py:26
  92.7 6.9 %collective-permute-start.2 = (f32[16,2,24,128]{3,2,1,0:T(8,128)S(1)}, f32[16,2,24,128]{3,2,1,0:T(8,128)S(1)}, u32[]{:S(2)}, u32[]{:S(2)}) collective-permute-start(f32[16,2,24,128]{3,2,1,0:T(8,128)S(1)} %select_bitcast_fusion), channel_id=1, source_target_pairs={{0,16},{16,0},{1,17},{17,1},{2,18},{18,2},{3,19},{19,3},{4,20},{20... | collective-permute-start | bytes 1179656 | tf_op jit(solution)/shard_map/ppermute | solution.py:26
  100.3 13.7 %all-to-all-start.3 = ((bf16[16,48,128]{2,1,0:T(8,128)(2,1)}), bf16[16,48,128]{2,1,0:T(8,128)(2,1)S(1)}, u32[]{:S(2)}, u32[]{:S(2)}) async-start(bf16[16,48,128]{2,1,0:T(8,128)(2,1)} %bitcast.10), calls=%async_computation.3 | async-start | bytes 393216 | tf_op jit(solution)/shard_map/all_to_all | solution.py:17

commit v4 on v2

v4 whole, which is shorter than its diff:
```python
import jax
import jax.numpy as jnp
from jax import lax
from jax.experimental import pallas as pl
from jax.experimental.pallas import tpu as pltpu
from jax.sharding import Mesh
from jax.sharding import PartitionSpec as P

keep_scale = 1.0 / 0.9
contract_last = (((1,), (1,)), ((), ()))
contract_first = (((0,), (0,)), ((), ()))
lanes = 128
plane = ("x", "zl")


def exchange(blocks, axis):
    return lax.all_to_all(blocks, axis, split_axis=0, concat_axis=0, tiled=True)


def sent_to_all(block, axis):
    copies = jnp.broadcast_to(block, (lax.axis_size(axis), *block.shape))
    return exchange(copies, axis)


def swapped(value, axis):
    return lax.ppermute(value, axis, [(0, 1), (1, 0)])


def in_order(mine, other, first, dim):
    a, b = jnp.where(first, mine, other), jnp.where(first, other, mine)
    return jnp.stack([a, b], axis=dim)


def dot(a, b, dims=(((1,), (0,)), ((), ()))):
    return lax.dot_general(a, b, dims, preferred_element_type=jnp.float32)


def vmem_call(kernel, operands, outs, flops, scratch=(), limit=8 << 20, out_space=pltpu.VMEM):
    space, to = (pl.BlockSpec(memory_space=m) for m in (pltpu.VMEM, out_space))
    read = 4 * sum(a.size for a in operands)
    operands = [pltpu.with_memory_space_constraint(a, pltpu.VMEM) for a in operands]
    return pl.pallas_call(
        kernel,
        out_shape=tuple(out_space(*o) for o in outs),
        in_specs=[space] * len(operands),
        out_specs=(to,) * len(outs),
        scratch_shapes=scratch,
        cost_estimate=pl.CostEstimate(flops=flops, bytes_accessed=read, transcendentals=0),
        compiler_params=pltpu.CompilerParams(vmem_limit_bytes=limit),
    )(*operands)


def read_weights(near, weights, keep_mask):
    def kernel(n_ref, g_hbm, u_hbm, d_hbm, k_hbm, g_ref, u_ref, d_ref, keep_ref, mask, sems):
        pairs = ((g_hbm, g_ref), (u_hbm, u_ref), (d_hbm, d_ref), (k_hbm, mask))
        moves = [pltpu.make_async_copy(*pair, sems.at[i]) for i, pair in enumerate(pairs)]
        for move in moves:
            move.start()
        moves[3].wait()
        keep_ref[...] = mask[...].astype(jnp.float32)
        for move in moves[:3]:
            move.wait()

    space, far = (pl.BlockSpec(memory_space=m) for m in (pltpu.VMEM, pltpu.HBM))
    operands = [pltpu.with_memory_space_constraint(a, pltpu.HBM) for a in (*weights, keep_mask)]
    return pl.pallas_call(
        kernel,
        out_shape=(
            *(pltpu.VMEM(w.shape, w.dtype) for w in weights),
            pltpu.VMEM(keep_mask.shape, jnp.float32),
        ),
        in_specs=[space, far, far, far, far],
        out_specs=(space,) * 4,
        scratch_shapes=[
            pltpu.VMEM(keep_mask.shape, keep_mask.dtype),
            pltpu.SemaphoreType.DMA((4,)),
        ],
        cost_estimate=pl.CostEstimate(flops=10**9, bytes_accessed=2 << 20, transcendentals=0),
        compiler_params=pltpu.CompilerParams(vmem_limit_bytes=4 << 20),
        name="read_weights",
    )(near, *operands)


def back_products(spread, weights):
    _, _, down_weight = weights
    ring, rows, units = spread.shape
    rows = rows // 3
    total, width = ring * rows, down_weight.shape[1]

    def kernel(s_ref, g_ref, u_ref, d_ref, out_ref):
        hidden, gate, up = (
            s_ref[:, m * rows : (m + 1) * rows, :].reshape(total, units) for m in range(3)
        )
        out_ref[0] = dot(hidden, d_ref[...])
        out_ref[1] = dot(gate, g_ref[...], contract_last) + dot(up, u_ref[...], contract_last)

    outs = (((2, total, width), jnp.float32),)
    flops = 6 * total * width * units
    return vmem_call(kernel, (spread, *weights), outs, flops)[0]


def weight_gradients(spread, tokens, cotangent):
    _, rows, units = spread.shape
    rows = rows // 3
    total, width = tokens.shape

    def kernel(s_ref, t_ref, c_ref, down_hbm, gate_hbm, up_hbm, down_ref, gate_ref, up_ref, sems):
        hidden, gate, up = (
            s_ref[:, m * rows : (m + 1) * rows, :].reshape(total, units) for m in range(3)
        )
        jobs = (
            (gate_ref, gate_hbm, t_ref, gate),
            (up_ref, up_hbm, t_ref, up),
            (down_ref, down_hbm, None, None),
        )
        moves = []
        for i, (ref, hbm, x_ref, y) in enumerate(jobs):
            x, y = (hidden, c_ref[...]) if x_ref is None else (x_ref[...], y)
            ref[...] = dot(x, y, contract_first).astype(ref.dtype)
            moves.append(pltpu.make_async_copy(ref, hbm, sems.at[i]))
            moves[i].start()
        for move in moves:
            move.wait()

    kind = tokens.dtype
    outs = (((units, width), kind), ((width, units), kind), ((width, units), kind))
    scratch = [*(pltpu.VMEM(*o) for o in outs), pltpu.SemaphoreType.DMA((3,))]
    flops = 6 * total * width * units
    return vmem_call(kernel, (spread, tokens, cotangent), outs, flops, scratch, out_space=pltpu.HBM)


def own_outputs(arrived, own, width):
    def kernel(a_ref, out_ref, in_ref, flat):
        flat[...] = a_ref[...].astype(jnp.float32).sum(axis=0)
        for ref, start in ((out_ref, 0), (in_ref, flat.shape[0] // 2)):
            for c in range(width // lanes):
                piece = flat[pl.ds(start + c, own, stride=width // lanes), :]
                ref[:, c * lanes : (c + 1) * lanes] = piece.astype(ref.dtype)

    space = pl.BlockSpec(memory_space=pltpu.VMEM)
    out = jax.ShapeDtypeStruct((own, width), arrived.dtype)
    return pl.pallas_call(
        kernel,
        out_shape=(out, out),
        in_specs=[space],
        out_specs=(space, space),
        scratch_shapes=[pltpu.VMEM(arrived.shape[1:], jnp.float32)],
        compiler_params=pltpu.CompilerParams(vmem_limit_bytes=4 << 20),
        name="own_outputs",
    )(pltpu.with_memory_space_constraint(arrived, pltpu.VMEM))


def products(tokens, cotangent, weights, ring):
    total, units = tokens.shape[0], weights[0].shape[1]
    rows = total // ring

    def kernel(t_ref, c_ref, g_ref, u_ref, d_ref, out_ref):
        def put(at, value):
            value = value.astype(out_ref.dtype).reshape(ring, rows, units)
            out_ref[:, at * rows : (at + 1) * rows, :] = value

        put(0, dot(t_ref[...], g_ref[...]))
        put(1, dot(t_ref[...], u_ref[...]))
        put(2, dot(c_ref[...], d_ref[...], contract_last))

    outs = (((ring, 3 * rows, units), tokens.dtype),)
    flops = 6 * tokens.size * units
    return vmem_call(kernel, (tokens, cotangent, *weights), outs, flops)[0]


def body(tokens, gate_weight, up_weight, down_weight, keep_mask, cotangent):
    bf16, f32 = jnp.bfloat16, jnp.float32
    own, width = tokens.shape
    share, units = keep_mask.shape
    ring = lax.axis_size("y")
    total = share * 2 * ring
    chips = total // own // 2

    packed = jnp.concatenate([tokens, cotangent], axis=0).reshape(-1, lanes)
    half = packed.shape[0] // 2
    first_core, first_side = lax.axis_index("core") == 0, lax.axis_index("zh") == 0
    packed, first_core, first_side = lax.optimization_barrier((packed, first_core, first_side))
    near = sent_to_all(packed, plane)
    weights = (gate_weight, up_weight, down_weight)
    other = swapped(near, "core")
    *weights, keep = read_weights(near[0, :8], weights, keep_mask)
    both = in_order(near, other, first_core, 1)
    all_tokens = both[:, :, :half].reshape(total, width)
    all_cot = both[:, :, half:].reshape(total, width)

    parts = products(all_tokens, all_cot, weights, ring)
    sums = exchange(parts, "y").astype(f32).sum(axis=0)
    other = swapped(jnp.concatenate([sums, keep], axis=0), "zh")
    sums = sums + other[: sums.shape[0]]
    keep = in_order(keep, other[sums.shape[0] :], first_side, 0).reshape(2 * share, units)
    gate_value, up_value, grad_hidden = jnp.split(sums, 3, axis=0)

    keep_factor = keep * keep_scale
    sigmoid_gate = jax.nn.sigmoid(gate_value)
    silu_gate = gate_value * sigmoid_gate
    hidden = silu_gate * up_value * keep_factor
    grad_pre = grad_hidden * keep_factor
    grad_gate = grad_pre * up_value * sigmoid_gate * (1.0 + gate_value * (1.0 - sigmoid_gate))
    grad_up = grad_pre * silu_gate
    mine = jnp.concatenate([hidden, grad_gate, grad_up], axis=0).astype(bf16)
    spread = sent_to_all(mine, "y")

    parts = back_products(spread, weights).reshape(2, chips, 2, -1, lanes)
    kept = jnp.where(first_core, parts[:, :, 0], parts[:, :, 1])
    given = jnp.where(first_core, parts[:, :, 1], parts[:, :, 0])
    other = swapped(given, "core")
    down_grad, gate_grad, up_grad = weight_gradients(spread, all_tokens, all_cot)
    parts = jnp.swapaxes((kept + other).astype(bf16), 0, 1).reshape(chips, -1, lanes)
    mixed_out, input_grad = own_outputs(exchange(parts, plane), own, width)
    return (mixed_out, input_grad, gate_grad, up_grad, down_grad)


def solution(mesh):
    fine = Mesh(mesh.devices.reshape(4, 4, 2, 8, 2), ("x", "zl", "core", "y", "zh"))
    row, col = ("x", "zl", "core"), ("y", "zh")
    by_row, by_col = P(row, col), P(col, row)

    return jax.shard_map(
        body,
        mesh=fine,
        in_specs=(by_row, by_col, by_col, by_row, by_col, by_row),
        out_specs=(by_row, by_row, by_col, by_col, by_row),
        check_vma=False,
    )
```

time: 119 us -> 116 us (0.975)
  blocking collectives: 38.4 us -> 69.6 us
  starting transfers between devices: 40.7 us -> 22.8 us
  waiting for transfers between devices: 25.2 us -> 14.3 us
  matrix products: 5.78 us -> 0 us
  Pallas kernels: 0 us -> 5.42 us
  local copies, waits for them, and re-layouts: 4.54 us -> 0.55 us
    all_to_all x2 -> x3, blocking collectives: 38.4 us -> 69.6 us  [exchange(): return lax.all_to_all(blocks, axis, split_axis=0, concat_axis=0, tiled=True)]
    all_to_all x2 -> x1, waiting for transfers between devices: 19.6 us -> 5.66 us  [exchange(): return lax.all_to_all(blocks, axis, split_axis=0, concat_axis=0, tiled=True)]
    ppermute x4 -> x3, starting transfers between devices: 27.4 us -> 17.5 us  [swapped(): return lax.ppermute(value, axis, [(0, 1), (1, 0)])]
    all_to_all x2 -> x1, starting transfers between devices: 13.3 us -> 5.38 us  [exchange(): return lax.all_to_all(blocks, axis, split_axis=0, concat_axis=0, tiled=True)]
    dot_general x9 -> x0, matrix products: 5.78 us -> none  [dot(): return lax.dot_general(a, b, dims, preferred_element_type=jnp.float32)]
    pallas_call x0 -> x5, Pallas kernels: none -> 5.42 us  [the longest x3 3.26 us: vmem_call(): pl.pallas_call(kernel, out_shape=tuple((out_space(*o) for o in outs)), in...]
    ppermute x4 -> x3, waiting for transfers between devices: 5.61 us -> 8.62 us  [swapped(): return lax.ppermute(value, axis, [(0, 1), (1, 0)])]
    reshape x4 -> x2, local copies, waits for them, and re-layouts: 2.72 us -> 0.07 us  [the longest x1 0.05 us: body(): parts = back_products(spread, weights).reshape(2, chips, 2, -1, lanes)]
  transfers between devices with their start and end apart: 6 -> 4, of which waited for: 5 -> 3; matrix products, arithmetic and copies ran while one was open for 3% -> 0% of each run, Pallas kernels for 0% -> 3%
where the time goes in v4:
time: 116 us; the launch traced here: 115 us
  blocking collectives  69.6 us (60%)
  starting transfers between devices  22.8 us (20%)
  waiting for transfers between devices  14.3 us (12%)
  Pallas kernels  5.42 us (5%)
  other arithmetic  1.87 us (2%)
    all_to_all x3, blocking collectives, exchange(): return lax.all_to_all(blocks, axis, split_axis=0, concat_axis=0, tiled=True)  69.6 us
    ppermute x3, starting transfers between devices, swapped(): return lax.ppermute(value, axis, [(0, 1), (1, 0)])  17.5 us
    ppermute x3, waiting for transfers between devices, swapped(): return lax.ppermute(value, axis, [(0, 1), (1, 0)])  8.62 us
    all_to_all x1, waiting for transfers between devices, exchange(): return lax.all_to_all(blocks, axis, split_axis=0, concat_axis=0, tiled=True)  5.66 us
    all_to_all x1, starting transfers between devices, exchange(): return lax.all_to_all(blocks, axis, split_axis=0, concat_axis=0, tiled=True)  5.38 us
    pallas_call x3, Pallas kernels, vmem_call(): pl.pallas_call(kernel, out_shape=tuple((out_space(*o) for o in outs)), in...  3.26 us
  transfers between devices with their start and end apart: 4, of which 3 were waited for; matrix products, arithmetic and copies ran while one was open for 0% of the time, Pallas kernels for 3%

profile of v4, /device:TPU:1, one launch (start us, length us, event | category | flops | bytes accessed | tf_op | source)
XLA Modules:
  0.0 115.5 jit_solution(16673271904449627948)
XLA Ops:
  0.6 0.7 pad_maximum_fusion.3
  1.4 17.7 %all_to_all.20 = bf16[16,48,128]{2,1,0:T(8,128)(2,1)S(1)} all-to-all(bf16[16,48,128]{2,1,0:T(8,128)(2,1)S(1)} %broadcast_in_dim.6), channel_id=1, replica_groups=mesh['x'=4,'zl'=4,'core'=2,'y'=8,'zh'=2] {'x','zl'}, dimensions={0} | all-to-all | bytes 393216 | tf_op jit(solution)/shard_map/all_to_all | solution.py:17
  19.1 4.8 %collective-permute-start = (bf16[16,48,128]{2,1,0:T(8,128)(2,1)S(1)}, bf16[16,48,128]{2,1,0:T(8,128)(2,1)S(1)}, u32[]{:S(2)}, u32[]{:S(2)}) collective-permute-start(bf16[16,48,128]{2,1,0:T(8,128)(2,1)S(1)} %all_to_all.20), channel_id=1, source_target_pairs={{0,16},{16,0},{1,17},{17,1},{2,18},{18,2},{3,19},{19,3},{4,20},{20... | collective-permute-start | bytes 589832 | tf_op jit(solution)/shard_map/ppermute | solution.py:26
  24.0 1.5 %read_weights.1 = (bf16[512,640]{1,0:T(8,128)(2,1)S(1)}, bf16[512,640]{1,0:T(8,128)(2,1)S(1)}, bf16[640,512]{1,0:T(8,128)(2,1)S(1)}, f32[12,640]{1,0:T(8,128)S(1)}) custom-call(bf16[8,128]{1,0:T(8,128)(2,1)S(1)} %slice_bitcast_fusion.n_ref, bf16[512,640]{1,0:T(8,128)(2,1)} %g_hbm.1, bf16[512,640]{1,0:T(8,128)(2,1)} %u_hbm.1, bf16[640,512]{1,0:T(8,128)(2,1)} %d_hbm.1, ...), custom_call_target="tpu_custom_call" | custom-call | flops 1000000000 | bytes 2097152 | tf_op jit(solution)/shard_map/read_weights/pallas_call | solution.py:66
  25.5 0.0 collective-permute-done
  25.5 0.1 select_bitcast_fusion.1
  25.6 0.1 reshape.34.c_ref
  25.8 0.0 copy-start
  25.8 0.1 reshape.33.t_ref
  25.9 0.0 copy-start.2
  25.9 0.7 shard_map.101
  26.6 0.0 copy-done
  26.6 0.0 copy-done.2
  26.7 29.2 %all_to_all.21 = bf16[8,72,640]{2,1,0:T(8,128)(2,1)S(1)} all-to-all(bf16[8,72,640]{2,1,0:T(8,128)(2,1)S(1)} %shard_map.101), channel_id=1, replica_groups=mesh['x'=4,'zl'=4,'core'=2,'y'=8,'zh'=2] {'y'}, dimensions={0} | all-to-all | bytes 1474560 | tf_op jit(solution)/shard_map/all_to_all | solution.py:17
  55.8 0.1 convert_reduce_fusion
  55.9 7.9 %collective-permute-start.1 = (f32[84,640]{1,0:T(8,128)S(1)}, f32[84,640]{1,0:T(8,128)S(1)}, u32[]{:S(2)}, u32[]{:S(2)}) collective-permute-start(f32[84,640]{1,0:T(8,128)S(1)} %pad_maximum_fusion), channel_id=1, source_target_pairs={{0,1},{1,0},{2,3},{3,2},{4,5},{5,4},{6,7},{7,6},{8,9},{9,8},{10,11... | collective-permute-start | bytes 645128 | tf_op jit(solution)/shard_map/ppermute | solution.py:26
  63.9 7.3 %collective-permute-done.1 = f32[84,640]{1,0:T(8,128)S(1)} collective-permute-done((f32[84,640]{1,0:T(8,128)S(1)}, f32[84,640]{1,0:T(8,128)S(1)}, u32[]{:S(2)}, u32[]{:S(2)}) %collective-permute-start.1) | collective-permute-done | bytes 215072 | tf_op jit(solution)/shard_map/ppermute | solution.py:26
  71.3 0.1 multiply_convert_fusion.2
  71.3 0.1 broadcast_in_dim.7
  71.4 22.8 %all_to_all.22.s_ref = bf16[8,72,640]{2,1,0:T(8,128)(2,1)S(1)} all-to-all(bf16[8,72,640]{2,1,0:T(8,128)(2,1)S(1)} %broadcast_in_dim.7), channel_id=1, replica_groups=mesh['x'=4,'zl'=4,'core'=2,'y'=8,'zh'=2] {'y'}, dimensions={0} | all-to-all | bytes 1474560 | tf_op jit(solution)/shard_map/all_to_all | solution.py:17
  94.2 0.7 shard_map.102
  94.9 0.1 reshape.35
  95.0 0.1 fusion.3
  95.0 0.1 select_bitcast_fusion
  95.1 0.0 copy-start.1
  95.1 0.0 copy-start.3
  95.1 4.7 %collective-permute-start.2 = (f32[2,16,24,128]{3,2,0,1:T(8,128)S(1)}, f32[2,16,24,128]{3,2,0,1:T(8,128)S(1)}, u32[]{:S(2)}, u32[]{:S(2)}) collective-permute-start(f32[2,16,24,128]{3,2,0,1:T(8,128)S(1)} %select_bitcast_fusion), channel_id=1, source_target_pairs={{0,16},{16,0},{1,17},{17,1},{2,18},{18,2},{3,19},{19,3},{4,20},{20... | collective-permute-start | bytes 1179656 | tf_op jit(solution)/shard_map/ppermute | solution.py:26
  99.8 1.3 %collective-permute-done.2 = f32[2,16,24,128]{3,2,0,1:T(8,128)S(1)} collective-permute-done((f32[2,16,24,128]{3,2,0,1:T(8,128)S(1)}, f32[2,16,24,128]{3,2,0,1:T(8,128)S(1)}, u32[]{:S(2)}, u32[]{:S(2)}) %collective-permute-start.2) | collective-permute-done | bytes 393248 | tf_op jit(solution)/shard_map/ppermute | solution.py:26
  101.1 0.8 fusion
  101.9 5.4 %all-to-all-start.3 = ((bf16[16,48,128]{2,1,0:T(8,128)(2,1)}), bf16[16,48,128]{2,1,0:T(8,128)(2,1)S(1)}, u32[]{:S(2)}, u32[]{:S(2)}) async-start(bf16[16,48,128]{2,1,0:T(8,128)(2,1)} %bitcast.8), calls=%async_computation.3 | async-start | bytes 393216 | tf_op jit(solution)/shard_map/all_to_all | solution.py:17
  107.3 0.0 copy-done.1
  107.3 0.0 copy-done.3
  107.3 1.8 %shard_map.103 = (bf16[640,512]{1,0:T(8,128)(2,1)}, bf16[512,640]{1,0:T(8,128)(2,1)}, bf16[512,640]{1,0:T(8,128)(2,1)}) custom-call(bf16[8,72,640]{2,1,0:T(8,128)(2,1)S(1)} %all_to_all.22.s_ref, bf16[192,512]{1,0:T(8,128)(2,1)S(1)} %copy-done.3, bf16[192,512]{1,0:T(8,128)(2,1)S(1)} %copy-done.1), custom_call_target="tpu_custom_call" | custom-call | flops 377487360 | bytes 2260992 | tf_op jit(solution)/shard_map/pallas_call | solution.py:42
  109.2 5.7 %all-to-all-done.3.a_ref = bf16[16,48,128]{2,1,0:T(8,128)(2,1)S(1)} async-done(((bf16[16,48,128]{2,1,0:T(8,128)(2,1)}), bf16[16,48,128]{2,1,0:T(8,128)(2,1)S(1)}, u32[]{:S(2)}, u32[]{:S(2)}) %all-to-all-start.3) | async-done | bytes 196640 | tf_op jit(solution)/shard_map/all_to_all | solution.py:17
  114.8 0.6 own_outputs.1
  (12 shorter events, 0.2 us)
Async XLA Ops:
  19.1 6.4 %collective-permute-start = (bf16[16,48,128]{2,1,0:T(8,128)(2,1)S(1)}, bf16[16,48,128]{2,1,0:T(8,128)(2,1)S(1)}, u32[]{:S(2)}, u32[]{:S(2)}) collective-permute-start(bf16[16,48,128]{2,1,0:T(8,128)(2,1)S(1)} %all_to_all.20), channel_id=1, source_target_pairs={{0,16},{16,0},{1,17},{17,1},{2,18},{18,2},{3,19},{19,3},{4,20},{20... | collective-permute-start | bytes 589832 | tf_op jit(solution)/shard_map/ppermute | solution.py:26
  25.8 0.9 copy-start
  25.9 0.7 copy-start.2
  55.9 15.2 %collective-permute-start.1 = (f32[84,640]{1,0:T(8,128)S(1)}, f32[84,640]{1,0:T(8,128)S(1)}, u32[]{:S(2)}, u32[]{:S(2)}) collective-permute-start(f32[84,640]{1,0:T(8,128)S(1)} %pad_maximum_fusion), channel_id=1, source_target_pairs={{0,1},{1,0},{2,3},{3,2},{4,5},{5,4},{6,7},{7,6},{8,9},{9,8},{10,11... | collective-permute-start | bytes 645128 | tf_op jit(solution)/shard_map/ppermute | solution.py:26
  95.1 12.2 %copy-start.1 = (bf16[192,512]{1,0:T(8,128)(2,1)S(1)}, bf16[192,512]{1,0:T(8,128)(2,1)}, u32[]{:S(2)}) copy-start(bf16[192,512]{1,0:T(8,128)(2,1)} %copy-done) | copy-start | bytes 589828
  95.1 12.2 %copy-start.3 = (bf16[192,512]{1,0:T(8,128)(2,1)S(1)}, bf16[192,512]{1,0:T(8,128)(2,1)}, u32[]{:S(2)}) copy-start(bf16[192,512]{1,0:T(8,128)(2,1)} %copy-done.2) | copy-start | bytes 589828
  95.1 6.0 %collective-permute-start.2 = (f32[2,16,24,128]{3,2,0,1:T(8,128)S(1)}, f32[2,16,24,128]{3,2,0,1:T(8,128)S(1)}, u32[]{:S(2)}, u32[]{:S(2)}) collective-permute-start(f32[2,16,24,128]{3,2,0,1:T(8,128)S(1)} %select_bitcast_fusion), channel_id=1, source_target_pairs={{0,16},{16,0},{1,17},{17,1},{2,18},{18,2},{3,19},{19,3},{4,20},{20... | collective-permute-start | bytes 1179656 | tf_op jit(solution)/shard_map/ppermute | solution.py:26
  101.9 12.9 %all-to-all-start.3 = ((bf16[16,48,128]{2,1,0:T(8,128)(2,1)}), bf16[16,48,128]{2,1,0:T(8,128)(2,1)S(1)}, u32[]{:S(2)}, u32[]{:S(2)}) async-start(bf16[16,48,128]{2,1,0:T(8,128)(2,1)} %bitcast.8), calls=%async_computation.3 | async-start | bytes 393216 | tf_op jit(solution)/shard_map/all_to_all | solution.py:17

commit v5 on v4

--- a/solution.py
+++ b/solution.py
@@ -57,7 +57,7 @@
         for move in moves:
             move.start()
         moves[3].wait()
-        keep_ref[...] = mask[...].astype(jnp.float32)
+        keep_ref[...] = mask[...].astype(keep_ref.dtype)
         for move in moves[:3]:
             move.wait()
 
@@ -67,7 +67,7 @@
         kernel,
         out_shape=(
             *(pltpu.VMEM(w.shape, w.dtype) for w in weights),
-            pltpu.VMEM(keep_mask.shape, jnp.float32),
+            pltpu.VMEM(keep_mask.shape, jnp.bfloat16),
         ),
         in_specs=[space, far, far, far, far],
         out_specs=(space,) * 4,
@@ -150,22 +150,39 @@
     )(pltpu.with_memory_space_constraint(arrived, pltpu.VMEM))
 
 
-def products(tokens, cotangent, weights, ring):
+def products(tokens, cotangent, weights, place, ring):
     total, units = tokens.shape[0], weights[0].shape[1]
     rows = total // ring
 
-    def kernel(t_ref, c_ref, g_ref, u_ref, d_ref, out_ref):
-        def put(at, value):
-            value = value.astype(out_ref.dtype).reshape(ring, rows, units)
-            out_ref[:, at * rows : (at + 1) * rows, :] = value
+    def kernel(at_ref, t_ref, c_ref, g_ref, u_ref, d_ref, out_ref, lost_ref, whole):
+        own = pl.ds(pl.multiple_of(at_ref[0] * rows, rows), rows)
+
+        def put(m, value):
+            to = slice(m * rows, (m + 1) * rows)
+            out_ref[:, to, :] = value.astype(out_ref.dtype).reshape(ring, rows, units)
+            whole[...] = value
+            kept = whole[own, :]
+            lost_ref[to, :] = kept - kept.astype(out_ref.dtype).astype(jnp.float32)
 
         put(0, dot(t_ref[...], g_ref[...]))
         put(1, dot(t_ref[...], u_ref[...]))
         put(2, dot(c_ref[...], d_ref[...], contract_last))
 
-    outs = (((ring, 3 * rows, units), tokens.dtype),)
-    flops = 6 * tokens.size * units
-    return vmem_call(kernel, (tokens, cotangent, *weights), outs, flops)[0]
+    space, smem = (pl.BlockSpec(memory_space=m) for m in (pltpu.VMEM, pltpu.SMEM))
+    operands = (tokens, cotangent, *weights)
+    operands = [pltpu.with_memory_space_constraint(a, pltpu.VMEM) for a in operands]
+    return pl.pallas_call(
+        kernel,
+        out_shape=(
+            pltpu.VMEM((ring, 3 * rows, units), tokens.dtype),
+            pltpu.VMEM((3 * rows, units), jnp.float32),
+        ),
+        in_specs=[smem] + [space] * len(operands),
+        out_specs=(space, space),
+        scratch_shapes=[pltpu.VMEM((total, units), jnp.float32)],
+        compiler_params=pltpu.CompilerParams(vmem_limit_bytes=8 << 20),
+        name="products",
+    )(place, *operands)
 
 
 def body(tokens, gate_weight, up_weight, down_weight, keep_mask, cotangent):
@@ -179,7 +196,10 @@
     packed = jnp.concatenate([tokens, cotangent], axis=0).reshape(-1, lanes)
     half = packed.shape[0] // 2
     first_core, first_side = lax.axis_index("core") == 0, lax.axis_index("zh") == 0
-    packed, first_core, first_side = lax.optimization_barrier((packed, first_core, first_side))
+    place = lax.axis_index("y").reshape(1)
+    packed, first_core, first_side, place = lax.optimization_barrier(
+        (packed, first_core, first_side, place)
+    )
     near = sent_to_all(packed, plane)
     weights = (gate_weight, up_weight, down_weight)
     other = swapped(near, "core")
@@ -188,11 +208,16 @@
     all_tokens = both[:, :, :half].reshape(total, width)
     all_cot = both[:, :, half:].reshape(total, width)
 
-    parts = products(all_tokens, all_cot, weights, ring)
-    sums = exchange(parts, "y").astype(f32).sum(axis=0)
-    other = swapped(jnp.concatenate([sums, keep], axis=0), "zh")
-    sums = sums + other[: sums.shape[0]]
-    keep = in_order(keep, other[sums.shape[0] :], first_side, 0).reshape(2 * share, units)
+    parts, lost = products(all_tokens, all_cot, weights, place, ring)
+    sums = exchange(parts, "y").astype(f32).sum(axis=0) + lost
+    high = lax.reduce_precision(sums, 8, 7)
+    rows = 2 * share
+    low = sums[:rows] - high[:rows]
+    other = swapped(jnp.concatenate([high.astype(bf16), low.astype(bf16), keep], axis=0), "zh")
+    keep = in_order(keep, other[4 * rows :], first_side, 0).reshape(rows, units).astype(f32)
+    other = other[: 4 * rows].astype(f32)
+    low = jnp.concatenate([other[3 * rows :], jnp.zeros_like(sums[rows:])], axis=0)
+    sums = sums + (other[: 3 * rows] + low)
     gate_value, up_value, grad_hidden = jnp.split(sums, 3, axis=0)
 
     keep_factor = keep * keep_scale

time: 116 us -> 113 us (0.974)
  waiting for transfers between devices: 14.3 us -> 10.6 us
    ppermute x3, waiting for transfers between devices: 8.62 us -> 4.99 us  [swapped(): return lax.ppermute(value, axis, [(0, 1), (1, 0)])]
    pallas_call x3 -> x2, Pallas kernels: 3.26 us -> 2.58 us  [vmem_call(): pl.pallas_call(kernel, out_shape=tuple((out_space(*o) for o in outs)), in...]
where the time goes in v5:
time: 113 us; the launch traced here: 112 us
  blocking collectives  69.6 us (62%)
  starting transfers between devices  22.9 us (20%)
  waiting for transfers between devices  10.6 us (9%)
  Pallas kernels  5.44 us (5%)
  other arithmetic  1.92 us (2%)
    all_to_all x3, blocking collectives, exchange(): return lax.all_to_all(blocks, axis, split_axis=0, concat_axis=0, tiled=True)  69.6 us
    ppermute x3, starting transfers between devices, swapped(): return lax.ppermute(value, axis, [(0, 1), (1, 0)])  17.4 us
    all_to_all x1, waiting for transfers between devices, exchange(): return lax.all_to_all(blocks, axis, split_axis=0, concat_axis=0, tiled=True)  5.65 us
    all_to_all x1, starting transfers between devices, exchange(): return lax.all_to_all(blocks, axis, split_axis=0, concat_axis=0, tiled=True)  5.51 us
    ppermute x3, waiting for transfers between devices, swapped(): return lax.ppermute(value, axis, [(0, 1), (1, 0)])  4.99 us
    pallas_call x2, Pallas kernels, vmem_call(): pl.pallas_call(kernel, out_shape=tuple((out_space(*o) for o in outs)), in...  2.58 us
  transfers between devices with their start and end apart: 4, of which 3 were waited for; matrix products, arithmetic and copies ran while one was open for 0% of the time, Pallas kernels for 3%

profile of v5, /device:TPU:1, one launch (start us, length us, event | category | flops | bytes accessed | tf_op | source)
XLA Modules:
  0.0 112.1 jit_solution(682730889300069082)
XLA Ops:
  0.6 0.7 pad_maximum_fusion.3
  1.4 17.7 %all_to_all.20 = bf16[16,48,128]{2,1,0:T(8,128)(2,1)S(1)} all-to-all(bf16[16,48,128]{2,1,0:T(8,128)(2,1)S(1)} %broadcast_in_dim.7), channel_id=1, replica_groups=mesh['x'=4,'zl'=4,'core'=2,'y'=8,'zh'=2] {'x','zl'}, dimensions={0} | all-to-all | bytes 393216 | tf_op jit(solution)/shard_map/all_to_all | solution.py:17
  19.1 4.8 %collective-permute-start = (bf16[16,48,128]{2,1,0:T(8,128)(2,1)S(1)}, bf16[16,48,128]{2,1,0:T(8,128)(2,1)S(1)}, u32[]{:S(2)}, u32[]{:S(2)}) collective-permute-start(bf16[16,48,128]{2,1,0:T(8,128)(2,1)S(1)} %all_to_all.20), channel_id=1, source_target_pairs={{0,16},{16,0},{1,17},{17,1},{2,18},{18,2},{3,19},{19,3},{4,20},{20... | collective-permute-start | bytes 589832 | tf_op jit(solution)/shard_map/ppermute | solution.py:26
  24.0 1.5 %read_weights.1 = (bf16[512,640]{1,0:T(8,128)(2,1)S(1)}, bf16[512,640]{1,0:T(8,128)(2,1)S(1)}, bf16[640,512]{1,0:T(8,128)(2,1)S(1)}, bf16[12,640]{1,0:T(8,128)(2,1)S(1)}) custom-call(bf16[8,128]{1,0:T(8,128)(2,1)S(1)} %slice_bitcast_fusion.n_ref, bf16[512,640]{1,0:T(8,128)(2,1)} %g_hbm.1, bf16[512,640]{1,0:T(8,128)(2,1)} %u_hbm.1, bf16[640,512]{1,0:T(8,128)(2,1)} %d_hbm.1, ...), custom_call_target="tpu_custom_call" | custom-call | flops 1000000000 | bytes 2097152 | tf_op jit(solution)/shard_map/read_weights/pallas_call | solution.py:66
  25.5 0.0 collective-permute-done
  25.6 0.1 reshape.39.c_ref
  25.7 0.0 copy-start
  25.8 0.1 reshape.38.t_ref
  25.9 0.0 copy-start.2
  25.9 0.7 products.1
  26.6 0.0 copy-done
  26.7 0.0 copy-done.2
  26.7 29.2 %all_to_all.21 = bf16[8,72,640]{2,1,0:T(8,128)(2,1)S(1)} all-to-all(bf16[8,72,640]{2,1,0:T(8,128)(2,1)S(1)} %get-tuple-element.26), channel_id=1, replica_groups=mesh['x'=4,'zl'=4,'core'=2,'y'=8,'zh'=2] {'y'}, dimensions={0} | all-to-all | bytes 1474560 | tf_op jit(solution)/shard_map/all_to_all | solution.py:17
  55.8 0.1 convert_reduce_fusion
  56.0 7.9 %collective-permute-start.1 = (bf16[108,640]{1,0:T(8,128)(2,1)S(1)}, bf16[108,640]{1,0:T(8,128)(2,1)S(1)}, u32[]{:S(2)}, u32[]{:S(2)}) collective-permute-start(bf16[108,640]{1,0:T(8,128)(2,1)S(1)} %pad_maximum_fusion.1), channel_id=1, source_target_pairs={{0,1},{1,0},{2,3},{3,2},{4,5},{5,4},{6,7},{7,6},{8,9},{9,8},{10,11... | collective-permute-start | bytes 414728 | tf_op jit(solution)/shard_map/ppermute | solution.py:26
  64.0 3.7 %collective-permute-done.1 = bf16[108,640]{1,0:T(8,128)(2,1)S(1)} collective-permute-done((bf16[108,640]{1,0:T(8,128)(2,1)S(1)}, bf16[108,640]{1,0:T(8,128)(2,1)S(1)}, u32[]{:S(2)}, u32[]{:S(2)}) %collective-permute-start.1) | collective-permute-done | bytes 138272 | tf_op jit(solution)/shard_map/ppermute | solution.py:26
  67.8 0.1 multiply_convert_fusion.2
  67.8 0.1 broadcast_in_dim.8
  67.9 22.8 %all_to_all.22.s_ref = bf16[8,72,640]{2,1,0:T(8,128)(2,1)S(1)} all-to-all(bf16[8,72,640]{2,1,0:T(8,128)(2,1)S(1)} %broadcast_in_dim.8), channel_id=1, replica_groups=mesh['x'=4,'zl'=4,'core'=2,'y'=8,'zh'=2] {'y'}, dimensions={0} | all-to-all | bytes 1474560 | tf_op jit(solution)/shard_map/all_to_all | solution.py:17
  90.7 0.7 shard_map.101
  91.4 0.1 reshape.40
  91.5 0.1 fusion.5
  91.6 0.1 select_bitcast_fusion
  91.6 0.0 copy-start.1
  91.6 0.0 copy-start.3
  91.7 4.7 %collective-permute-start.2 = (f32[2,16,24,128]{3,2,0,1:T(8,128)S(1)}, f32[2,16,24,128]{3,2,0,1:T(8,128)S(1)}, u32[]{:S(2)}, u32[]{:S(2)}) collective-permute-start(f32[2,16,24,128]{3,2,0,1:T(8,128)S(1)} %select_bitcast_fusion), channel_id=1, source_target_pairs={{0,16},{16,0},{1,17},{17,1},{2,18},{18,2},{3,19},{19,3},{4,20},{20... | collective-permute-start | bytes 1179656 | tf_op jit(solution)/shard_map/ppermute | solution.py:26
  96.3 1.3 %collective-permute-done.2 = f32[2,16,24,128]{3,2,0,1:T(8,128)S(1)} collective-permute-done((f32[2,16,24,128]{3,2,0,1:T(8,128)S(1)}, f32[2,16,24,128]{3,2,0,1:T(8,128)S(1)}, u32[]{:S(2)}, u32[]{:S(2)}) %collective-permute-start.2) | collective-permute-done | bytes 393248 | tf_op jit(solution)/shard_map/ppermute | solution.py:26
  97.6 0.8 fusion
  98.4 5.5 %all-to-all-start.3 = ((bf16[16,48,128]{2,1,0:T(8,128)(2,1)}), bf16[16,48,128]{2,1,0:T(8,128)(2,1)S(1)}, u32[]{:S(2)}, u32[]{:S(2)}) async-start(bf16[16,48,128]{2,1,0:T(8,128)(2,1)} %bitcast.9), calls=%async_computation.3 | async-start | bytes 393216 | tf_op jit(solution)/shard_map/all_to_all | solution.py:17
  103.9 0.0 copy-done.1
  103.9 0.0 copy-done.3
  103.9 1.8 %shard_map.102 = (bf16[640,512]{1,0:T(8,128)(2,1)}, bf16[512,640]{1,0:T(8,128)(2,1)}, bf16[512,640]{1,0:T(8,128)(2,1)}) custom-call(bf16[8,72,640]{2,1,0:T(8,128)(2,1)S(1)} %all_to_all.22.s_ref, bf16[192,512]{1,0:T(8,128)(2,1)S(1)} %copy-done.3, bf16[192,512]{1,0:T(8,128)(2,1)S(1)} %copy-done.1), custom_call_target="tpu_custom_call" | custom-call | flops 377487360 | bytes 2260992 | tf_op jit(solution)/shard_map/pallas_call | solution.py:42
  105.8 5.7 %all-to-all-done.3.a_ref = bf16[16,48,128]{2,1,0:T(8,128)(2,1)S(1)} async-done(((bf16[16,48,128]{2,1,0:T(8,128)(2,1)}), bf16[16,48,128]{2,1,0:T(8,128)(2,1)S(1)}, u32[]{:S(2)}, u32[]{:S(2)}) %all-to-all-start.3) | async-done | bytes 196640 | tf_op jit(solution)/shard_map/all_to_all | solution.py:17
  111.4 0.6 own_outputs.1
  (18 shorter events, 0.3 us)
Async XLA Ops:
  19.1 6.4 %collective-permute-start = (bf16[16,48,128]{2,1,0:T(8,128)(2,1)S(1)}, bf16[16,48,128]{2,1,0:T(8,128)(2,1)S(1)}, u32[]{:S(2)}, u32[]{:S(2)}) collective-permute-start(bf16[16,48,128]{2,1,0:T(8,128)(2,1)S(1)} %all_to_all.20), channel_id=1, source_target_pairs={{0,16},{16,0},{1,17},{17,1},{2,18},{18,2},{3,19},{19,3},{4,20},{20... | collective-permute-start | bytes 589832 | tf_op jit(solution)/shard_map/ppermute | solution.py:26
  25.7 0.9 copy-start
  25.9 0.7 copy-start.2
  56.0 11.6 %collective-permute-start.1 = (bf16[108,640]{1,0:T(8,128)(2,1)S(1)}, bf16[108,640]{1,0:T(8,128)(2,1)S(1)}, u32[]{:S(2)}, u32[]{:S(2)}) collective-permute-start(bf16[108,640]{1,0:T(8,128)(2,1)S(1)} %pad_maximum_fusion.1), channel_id=1, source_target_pairs={{0,1},{1,0},{2,3},{3,2},{4,5},{5,4},{6,7},{7,6},{8,9},{9,8},{10,11... | collective-permute-start | bytes 414728 | tf_op jit(solution)/shard_map/ppermute | solution.py:26
  91.6 12.3 %copy-start.1 = (bf16[192,512]{1,0:T(8,128)(2,1)S(1)}, bf16[192,512]{1,0:T(8,128)(2,1)}, u32[]{:S(2)}) copy-start(bf16[192,512]{1,0:T(8,128)(2,1)} %copy-done) | copy-start | bytes 589828
  91.6 12.3 %copy-start.3 = (bf16[192,512]{1,0:T(8,128)(2,1)S(1)}, bf16[192,512]{1,0:T(8,128)(2,1)}, u32[]{:S(2)}) copy-start(bf16[192,512]{1,0:T(8,128)(2,1)} %copy-done.2) | copy-start | bytes 589828
  91.7 6.0 %collective-permute-start.2 = (f32[2,16,24,128]{3,2,0,1:T(8,128)S(1)}, f32[2,16,24,128]{3,2,0,1:T(8,128)S(1)}, u32[]{:S(2)}, u32[]{:S(2)}) collective-permute-start(f32[2,16,24,128]{3,2,0,1:T(8,128)S(1)} %select_bitcast_fusion), channel_id=1, source_target_pairs={{0,16},{16,0},{1,17},{17,1},{2,18},{18,2},{3,19},{19,3},{4,20},{20... | collective-permute-start | bytes 1179656 | tf_op jit(solution)/shard_map/ppermute | solution.py:26
  98.4 13.0 %all-to-all-start.3 = ((bf16[16,48,128]{2,1,0:T(8,128)(2,1)}), bf16[16,48,128]{2,1,0:T(8,128)(2,1)S(1)}, u32[]{:S(2)}, u32[]{:S(2)}) async-start(bf16[16,48,128]{2,1,0:T(8,128)(2,1)} %bitcast.9), calls=%async_computation.3 | async-start | bytes 393216 | tf_op jit(solution)/shard_map/all_to_all | solution.py:17

commit v6 on v5

--- a/solution.py
+++ b/solution.py
@@ -210,14 +210,10 @@
 
     parts, lost = products(all_tokens, all_cot, weights, place, ring)
     sums = exchange(parts, "y").astype(f32).sum(axis=0) + lost
-    high = lax.reduce_precision(sums, 8, 7)
     rows = 2 * share
-    low = sums[:rows] - high[:rows]
-    other = swapped(jnp.concatenate([high.astype(bf16), low.astype(bf16), keep], axis=0), "zh")
-    keep = in_order(keep, other[4 * rows :], first_side, 0).reshape(rows, units).astype(f32)
-    other = other[: 4 * rows].astype(f32)
-    low = jnp.concatenate([other[3 * rows :], jnp.zeros_like(sums[rows:])], axis=0)
-    sums = sums + (other[: 3 * rows] + low)
+    other = swapped(jnp.concatenate([sums.astype(bf16), keep], axis=0), "zh")
+    keep = in_order(keep, other[3 * rows :], first_side, 0).reshape(rows, units).astype(f32)
+    sums = sums + other[: 3 * rows].astype(f32)
     gate_value, up_value, grad_hidden = jnp.split(sums, 3, axis=0)
 
     keep_factor = keep * keep_scale

time: 113 us -> 112 us (level)
  no operation moved by 1% of the time
where the time goes in v6:
time: 112 us; the launch traced here: 111 us
  blocking collectives  69.6 us (62%)
  starting transfers between devices  22.3 us (20%)
  waiting for transfers between devices  9.98 us (9%)
  Pallas kernels  5.44 us (5%)
  other arithmetic  1.87 us (2%)
    all_to_all x3, blocking collectives, exchange(): return lax.all_to_all(blocks, axis, split_axis=0, concat_axis=0, tiled=True)  69.6 us
    ppermute x3, starting transfers between devices, swapped(): return lax.ppermute(value, axis, [(0, 1), (1, 0)])  17.4 us
    all_to_all x1, waiting for transfers between devices, exchange(): return lax.all_to_all(blocks, axis, split_axis=0, concat_axis=0, tiled=True)  5.65 us
    all_to_all x1, starting transfers between devices, exchange(): return lax.all_to_all(blocks, axis, split_axis=0, concat_axis=0, tiled=True)  4.85 us
    ppermute x3, waiting for transfers between devices, swapped(): return lax.ppermute(value, axis, [(0, 1), (1, 0)])  4.33 us
    pallas_call x2, Pallas kernels, vmem_call(): pl.pallas_call(kernel, out_shape=tuple((out_space(*o) for o in outs)), in...  2.58 us
  transfers between devices with their start and end apart: 4, of which 3 were waited for; matrix products, arithmetic and copies ran while one was open for 0% of the time, Pallas kernels for 3%

profile of v6, /device:TPU:1, one launch (start us, length us, event | category | flops | bytes accessed | tf_op | source)
XLA Modules:
  0.0 110.7 jit_solution(17882195179730200956)
XLA Ops:
  0.6 0.7 pad_maximum_fusion.3
  1.4 17.7 %all_to_all.20 = bf16[16,48,128]{2,1,0:T(8,128)(2,1)S(1)} all-to-all(bf16[16,48,128]{2,1,0:T(8,128)(2,1)S(1)} %broadcast_in_dim.6), channel_id=1, replica_groups=mesh['x'=4,'zl'=4,'core'=2,'y'=8,'zh'=2] {'x','zl'}, dimensions={0} | all-to-all | bytes 393216 | tf_op jit(solution)/shard_map/all_to_all | solution.py:17
  19.1 4.8 %collective-permute-start = (bf16[16,48,128]{2,1,0:T(8,128)(2,1)S(1)}, bf16[16,48,128]{2,1,0:T(8,128)(2,1)S(1)}, u32[]{:S(2)}, u32[]{:S(2)}) collective-permute-start(bf16[16,48,128]{2,1,0:T(8,128)(2,1)S(1)} %all_to_all.20), channel_id=1, source_target_pairs={{0,16},{16,0},{1,17},{17,1},{2,18},{18,2},{3,19},{19,3},{4,20},{20... | collective-permute-start | bytes 589832 | tf_op jit(solution)/shard_map/ppermute | solution.py:26
  24.0 1.5 %read_weights.1 = (bf16[512,640]{1,0:T(8,128)(2,1)S(1)}, bf16[512,640]{1,0:T(8,128)(2,1)S(1)}, bf16[640,512]{1,0:T(8,128)(2,1)S(1)}, bf16[12,640]{1,0:T(8,128)(2,1)S(1)}) custom-call(bf16[8,128]{1,0:T(8,128)(2,1)S(1)} %slice_bitcast_fusion.n_ref, bf16[512,640]{1,0:T(8,128)(2,1)} %g_hbm.1, bf16[512,640]{1,0:T(8,128)(2,1)} %u_hbm.1, bf16[640,512]{1,0:T(8,128)(2,1)} %d_hbm.1, ...), custom_call_target="tpu_custom_call" | custom-call | flops 1000000000 | bytes 2097152 | tf_op jit(solution)/shard_map/read_weights/pallas_call | solution.py:66
  25.5 0.0 collective-permute-done
  25.6 0.1 reshape.39.c_ref
  25.7 0.0 copy-start
  25.8 0.1 reshape.38.t_ref
  25.9 0.0 copy-start.2
  25.9 0.7 products.1
  26.6 0.0 copy-done
  26.7 0.0 copy-done.2
  26.7 29.2 %all_to_all.21 = bf16[8,72,640]{2,1,0:T(8,128)(2,1)S(1)} all-to-all(bf16[8,72,640]{2,1,0:T(8,128)(2,1)S(1)} %get-tuple-element.26), channel_id=1, replica_groups=mesh['x'=4,'zl'=4,'core'=2,'y'=8,'zh'=2] {'y'}, dimensions={0} | all-to-all | bytes 1474560 | tf_op jit(solution)/shard_map/all_to_all | solution.py:17
  55.8 0.1 convert_reduce_fusion
  56.0 7.9 %collective-permute-start.1 = (bf16[84,640]{1,0:T(8,128)(2,1)S(1)}, bf16[84,640]{1,0:T(8,128)(2,1)S(1)}, u32[]{:S(2)}, u32[]{:S(2)}) collective-permute-start(bf16[84,640]{1,0:T(8,128)(2,1)S(1)} %pad_maximum_fusion.1), channel_id=1, source_target_pairs={{0,1},{1,0},{2,3},{3,2},{4,5},{5,4},{6,7},{7,6},{8,9},{9,8},{10,11... | collective-permute-start | bytes 322568 | tf_op jit(solution)/shard_map/ppermute | solution.py:26
  63.9 3.0 %collective-permute-done.1 = bf16[84,640]{1,0:T(8,128)(2,1)S(1)} collective-permute-done((bf16[84,640]{1,0:T(8,128)(2,1)S(1)}, bf16[84,640]{1,0:T(8,128)(2,1)S(1)}, u32[]{:S(2)}, u32[]{:S(2)}) %collective-permute-start.1) | collective-permute-done | bytes 107552 | tf_op jit(solution)/shard_map/ppermute | solution.py:26
  67.0 0.1 multiply_convert_fusion.2
  67.1 0.1 broadcast_in_dim.7
  67.2 22.8 %all_to_all.22.s_ref = bf16[8,72,640]{2,1,0:T(8,128)(2,1)S(1)} all-to-all(bf16[8,72,640]{2,1,0:T(8,128)(2,1)S(1)} %broadcast_in_dim.7), channel_id=1, replica_groups=mesh['x'=4,'zl'=4,'core'=2,'y'=8,'zh'=2] {'y'}, dimensions={0} | all-to-all | bytes 1474560 | tf_op jit(solution)/shard_map/all_to_all | solution.py:17
  89.9 0.7 shard_map.101
  90.7 0.1 reshape.40
  90.8 0.1 fusion.4
  90.8 0.1 select_bitcast_fusion
  90.9 0.0 copy-start.1
  90.9 0.0 copy-start.3
  90.9 4.7 %collective-permute-start.2 = (f32[2,16,24,128]{3,2,0,1:T(8,128)S(1)}, f32[2,16,24,128]{3,2,0,1:T(8,128)S(1)}, u32[]{:S(2)}, u32[]{:S(2)}) collective-permute-start(f32[2,16,24,128]{3,2,0,1:T(8,128)S(1)} %select_bitcast_fusion), channel_id=1, source_target_pairs={{0,16},{16,0},{1,17},{17,1},{2,18},{18,2},{3,19},{19,3},{4,20},{20... | collective-permute-start | bytes 1179656 | tf_op jit(solution)/shard_map/ppermute | solution.py:26
  95.6 1.3 %collective-permute-done.2 = f32[2,16,24,128]{3,2,0,1:T(8,128)S(1)} collective-permute-done((f32[2,16,24,128]{3,2,0,1:T(8,128)S(1)}, f32[2,16,24,128]{3,2,0,1:T(8,128)S(1)}, u32[]{:S(2)}, u32[]{:S(2)}) %collective-permute-start.2) | collective-permute-done | bytes 393248 | tf_op jit(solution)/shard_map/ppermute | solution.py:26
  96.9 0.8 fusion
  97.7 4.9 %all-to-all-start.3 = ((bf16[16,48,128]{2,1,0:T(8,128)(2,1)}), bf16[16,48,128]{2,1,0:T(8,128)(2,1)S(1)}, u32[]{:S(2)}, u32[]{:S(2)}) async-start(bf16[16,48,128]{2,1,0:T(8,128)(2,1)} %bitcast.9), calls=%async_computation.3 | async-start | bytes 393216 | tf_op jit(solution)/shard_map/all_to_all | solution.py:17
  102.5 0.0 copy-done.1
  102.5 0.0 copy-done.3
  102.5 1.8 %shard_map.102 = (bf16[640,512]{1,0:T(8,128)(2,1)}, bf16[512,640]{1,0:T(8,128)(2,1)}, bf16[512,640]{1,0:T(8,128)(2,1)}) custom-call(bf16[8,72,640]{2,1,0:T(8,128)(2,1)S(1)} %all_to_all.22.s_ref, bf16[192,512]{1,0:T(8,128)(2,1)S(1)} %copy-done.3, bf16[192,512]{1,0:T(8,128)(2,1)S(1)} %copy-done.1), custom_call_target="tpu_custom_call" | custom-call | flops 377487360 | bytes 2260992 | tf_op jit(solution)/shard_map/pallas_call | solution.py:42
  104.4 5.7 %all-to-all-done.3.a_ref = bf16[16,48,128]{2,1,0:T(8,128)(2,1)S(1)} async-done(((bf16[16,48,128]{2,1,0:T(8,128)(2,1)}), bf16[16,48,128]{2,1,0:T(8,128)(2,1)S(1)}, u32[]{:S(2)}, u32[]{:S(2)}) %all-to-all-start.3) | async-done | bytes 196640 | tf_op jit(solution)/shard_map/all_to_all | solution.py:17
  110.0 0.6 own_outputs.1
  (14 shorter events, 0.3 us)
Async XLA Ops:
  19.1 6.4 %collective-permute-start = (bf16[16,48,128]{2,1,0:T(8,128)(2,1)S(1)}, bf16[16,48,128]{2,1,0:T(8,128)(2,1)S(1)}, u32[]{:S(2)}, u32[]{:S(2)}) collective-permute-start(bf16[16,48,128]{2,1,0:T(8,128)(2,1)S(1)} %all_to_all.20), channel_id=1, source_target_pairs={{0,16},{16,0},{1,17},{17,1},{2,18},{18,2},{3,19},{19,3},{4,20},{20... | collective-permute-start | bytes 589832 | tf_op jit(solution)/shard_map/ppermute | solution.py:26
  25.7 0.9 copy-start
  25.9 0.7 copy-start.2
  56.0 10.9 %collective-permute-start.1 = (bf16[84,640]{1,0:T(8,128)(2,1)S(1)}, bf16[84,640]{1,0:T(8,128)(2,1)S(1)}, u32[]{:S(2)}, u32[]{:S(2)}) collective-permute-start(bf16[84,640]{1,0:T(8,128)(2,1)S(1)} %pad_maximum_fusion.1), channel_id=1, source_target_pairs={{0,1},{1,0},{2,3},{3,2},{4,5},{5,4},{6,7},{7,6},{8,9},{9,8},{10,11... | collective-permute-start | bytes 322568 | tf_op jit(solution)/shard_map/ppermute | solution.py:26
  90.9 11.6 %copy-start.1 = (bf16[192,512]{1,0:T(8,128)(2,1)S(1)}, bf16[192,512]{1,0:T(8,128)(2,1)}, u32[]{:S(2)}) copy-start(bf16[192,512]{1,0:T(8,128)(2,1)} %copy-done) | copy-start | bytes 589828
  90.9 11.6 %copy-start.3 = (bf16[192,512]{1,0:T(8,128)(2,1)S(1)}, bf16[192,512]{1,0:T(8,128)(2,1)}, u32[]{:S(2)}) copy-start(bf16[192,512]{1,0:T(8,128)(2,1)} %copy-done.2) | copy-start | bytes 589828
  90.9 6.0 %collective-permute-start.2 = (f32[2,16,24,128]{3,2,0,1:T(8,128)S(1)}, f32[2,16,24,128]{3,2,0,1:T(8,128)S(1)}, u32[]{:S(2)}, u32[]{:S(2)}) collective-permute-start(f32[2,16,24,128]{3,2,0,1:T(8,128)S(1)} %select_bitcast_fusion), channel_id=1, source_target_pairs={{0,16},{16,0},{1,17},{17,1},{2,18},{18,2},{3,19},{19,3},{4,20},{20... | collective-permute-start | bytes 1179656 | tf_op jit(solution)/shard_map/ppermute | solution.py:26
  97.7 12.4 %all-to-all-start.3 = ((bf16[16,48,128]{2,1,0:T(8,128)(2,1)}), bf16[16,48,128]{2,1,0:T(8,128)(2,1)S(1)}, u32[]{:S(2)}, u32[]{:S(2)}) async-start(bf16[16,48,128]{2,1,0:T(8,128)(2,1)} %bitcast.9), calls=%async_computation.3 | async-start | bytes 393216 | tf_op jit(solution)/shard_map/all_to_all | solution.py:17

commit v7 on v6

--- a/solution.py
+++ b/solution.py
@@ -26,11 +26,6 @@
     return lax.ppermute(value, axis, [(0, 1), (1, 0)])
 
 
-def in_order(mine, other, first, dim):
-    a, b = jnp.where(first, mine, other), jnp.where(first, other, mine)
-    return jnp.stack([a, b], axis=dim)
-
-
 def dot(a, b, dims=(((1,), (0,)), ((), ()))):
     return lax.dot_general(a, b, dims, preferred_element_type=jnp.float32)
 
@@ -50,14 +45,23 @@
     )(*operands)
 
 
-def read_weights(near, weights, keep_mask):
-    def kernel(n_ref, g_hbm, u_hbm, d_hbm, k_hbm, g_ref, u_ref, d_ref, keep_ref, mask, sems):
+def read_weights(core, near, weights, keep_mask):
+    half = keep_mask.shape[0] // 2
+
+    def kernel(
+        core_ref, n_ref, g_hbm, u_hbm, d_hbm, k_hbm,
+        g_ref, u_ref, d_ref, keep_ref, mask, ordered, sems,
+    ):
         pairs = ((g_hbm, g_ref), (u_hbm, u_ref), (d_hbm, d_ref), (k_hbm, mask))
         moves = [pltpu.make_async_copy(*pair, sems.at[i]) for i, pair in enumerate(pairs)]
         for move in moves:
             move.start()
         moves[3].wait()
-        keep_ref[...] = mask[...].astype(keep_ref.dtype)
+        whole = mask[...].astype(jnp.float32)
+        a, b, first = whole[:half], whole[half:], core_ref[0] == 0
+        ordered[:half, :] = jnp.where(first, a, b)
+        ordered[half:, :] = jnp.where(first, b, a)
+        keep_ref[...] = ordered[...].astype(keep_ref.dtype)
         for move in moves[:3]:
             move.wait()
 
@@ -69,16 +73,57 @@
             *(pltpu.VMEM(w.shape, w.dtype) for w in weights),
             pltpu.VMEM(keep_mask.shape, jnp.bfloat16),
         ),
-        in_specs=[space, far, far, far, far],
+        in_specs=[pl.BlockSpec(memory_space=pltpu.SMEM), space, far, far, far, far],
         out_specs=(space,) * 4,
         scratch_shapes=[
             pltpu.VMEM(keep_mask.shape, keep_mask.dtype),
+            pltpu.VMEM(keep_mask.shape, jnp.float32),
             pltpu.SemaphoreType.DMA((4,)),
         ],
         cost_estimate=pl.CostEstimate(flops=10**9, bytes_accessed=2 << 20, transcendentals=0),
         compiler_params=pltpu.CompilerParams(vmem_limit_bytes=4 << 20),
         name="read_weights",
-    )(near, *operands)
+    )(core, near, *operands)
+
+
+def activations(side, sums, other, keep, ring):
+    rows, units = sums.shape
+    rows = rows // 3
+    half = rows // 2
+
+    def kernel(side_ref, s_ref, o_ref, k_ref, out_ref, factor):
+        mine = k_ref[...].astype(jnp.float32)
+        far = o_ref[3 * rows :, :].astype(jnp.float32)
+        first = side_ref[0] == 0
+        factor[:half, :] = jnp.where(first, mine, far)
+        factor[half:, :] = jnp.where(first, far, mine)
+        cuts = [slice(m * rows, (m + 1) * rows) for m in range(3)]
+        gate, up, grad = (s_ref[c, :] + o_ref[c, :].astype(jnp.float32) for c in cuts)
+        keep_factor = factor[...] * keep_scale
+        sigmoid_gate = jax.nn.sigmoid(gate)
+        silu_gate = gate * sigmoid_gate
+        grad_pre = grad * keep_factor
+        values = (
+            silu_gate * up * keep_factor,
+            grad_pre * up * sigmoid_gate * (1.0 + gate * (1.0 - sigmoid_gate)),
+            grad_pre * silu_gate,
+        )
+        for cut, value in zip(cuts, values):
+            value = value.astype(out_ref.dtype)
+            for y in range(ring):
+                out_ref[y, cut, :] = value
+
+    space, smem = (pl.BlockSpec(memory_space=m) for m in (pltpu.VMEM, pltpu.SMEM))
+    operands = [pltpu.with_memory_space_constraint(a, pltpu.VMEM) for a in (sums, other, keep)]
+    return pl.pallas_call(
+        kernel,
+        out_shape=pltpu.VMEM((ring, 3 * rows, units), jnp.bfloat16),
+        in_specs=[smem, space, space, space],
+        out_specs=space,
+        scratch_shapes=[pltpu.VMEM((rows, units), jnp.float32)],
+        compiler_params=pltpu.CompilerParams(vmem_limit_bytes=4 << 20),
+        name="activations",
+    )(side, *operands)
 
 
 def back_products(spread, weights):
@@ -188,47 +233,30 @@
 def body(tokens, gate_weight, up_weight, down_weight, keep_mask, cotangent):
     bf16, f32 = jnp.bfloat16, jnp.float32
     own, width = tokens.shape
-    share, units = keep_mask.shape
+    share, _ = keep_mask.shape
     ring = lax.axis_size("y")
     total = share * 2 * ring
     chips = total // own // 2
 
     packed = jnp.concatenate([tokens, cotangent], axis=0).reshape(-1, lanes)
     half = packed.shape[0] // 2
-    first_core, first_side = lax.axis_index("core") == 0, lax.axis_index("zh") == 0
-    place = lax.axis_index("y").reshape(1)
-    packed, first_core, first_side, place = lax.optimization_barrier(
-        (packed, first_core, first_side, place)
-    )
+    places = tuple(lax.axis_index(axis).reshape(1) for axis in ("core", "zh", "y"))
+    packed, core, side, place = lax.optimization_barrier((packed, *places))
     near = sent_to_all(packed, plane)
     weights = (gate_weight, up_weight, down_weight)
     other = swapped(near, "core")
-    *weights, keep = read_weights(near[0, :8], weights, keep_mask)
-    both = in_order(near, other, first_core, 1)
+    *weights, keep = read_weights(core, near[0, :8], weights, keep_mask)
+    both = jnp.stack([near, other], axis=1)
     all_tokens = both[:, :, :half].reshape(total, width)
     all_cot = both[:, :, half:].reshape(total, width)
 
     parts, lost = products(all_tokens, all_cot, weights, place, ring)
     sums = exchange(parts, "y").astype(f32).sum(axis=0) + lost
-    rows = 2 * share
     other = swapped(jnp.concatenate([sums.astype(bf16), keep], axis=0), "zh")
-    keep = in_order(keep, other[3 * rows :], first_side, 0).reshape(rows, units).astype(f32)
-    sums = sums + other[: 3 * rows].astype(f32)
-    gate_value, up_value, grad_hidden = jnp.split(sums, 3, axis=0)
-
-    keep_factor = keep * keep_scale
-    sigmoid_gate = jax.nn.sigmoid(gate_value)
-    silu_gate = gate_value * sigmoid_gate
-    hidden = silu_gate * up_value * keep_factor
-    grad_pre = grad_hidden * keep_factor
-    grad_gate = grad_pre * up_value * sigmoid_gate * (1.0 + gate_value * (1.0 - sigmoid_gate))
-    grad_up = grad_pre * silu_gate
-    mine = jnp.concatenate([hidden, grad_gate, grad_up], axis=0).astype(bf16)
-    spread = sent_to_all(mine, "y")
+    spread = exchange(activations(side, sums, other, keep, ring), "y")
 
     parts = back_products(spread, weights).reshape(2, chips, 2, -1, lanes)
-    kept = jnp.where(first_core, parts[:, :, 0], parts[:, :, 1])
-    given = jnp.where(first_core, parts[:, :, 1], parts[:, :, 0])
+    kept, given = parts[:, :, 0], parts[:, :, 1]
     other = swapped(given, "core")
     down_grad, gate_grad, up_grad = weight_gradients(spread, all_tokens, all_cot)
     parts = jnp.swapaxes((kept + other).astype(bf16), 0, 1).reshape(chips, -1, lanes)

time: 112 us -> 111 us (level)
  no operation moved by 1% of the time
where the time goes in v7:
time: 111 us; the launch traced here: 110 us
  blocking collectives  69.6 us (63%)
  starting transfers between devices  22.3 us (20%)
  waiting for transfers between devices  9.99 us (9%)
  Pallas kernels  5.55 us (5%)
  other arithmetic  1.65 us (1%)
    all_to_all x3, blocking collectives, exchange(): return lax.all_to_all(blocks, axis, split_axis=0, concat_axis=0, tiled=True)  69.6 us
    ppermute x3, starting transfers between devices, swapped(): return lax.ppermute(value, axis, [(0, 1), (1, 0)])  17.4 us
    all_to_all x1, waiting for transfers between devices, exchange(): return lax.all_to_all(blocks, axis, split_axis=0, concat_axis=0, tiled=True)  5.66 us
    all_to_all x1, starting transfers between devices, exchange(): return lax.all_to_all(blocks, axis, split_axis=0, concat_axis=0, tiled=True)  4.85 us
    ppermute x3, waiting for transfers between devices, swapped(): return lax.ppermute(value, axis, [(0, 1), (1, 0)])  4.33 us
    pallas_call x2, Pallas kernels, vmem_call(): pl.pallas_call(kernel, out_shape=tuple((out_space(*o) for o in outs)), in...  2.57 us
  transfers between devices with their start and end apart: 4, of which 3 were waited for; matrix products, arithmetic and copies ran while one was open for 0% of the time, Pallas kernels for 3%

profile of v7, /device:TPU:1, one launch (start us, length us, event | category | flops | bytes accessed | tf_op | source)
XLA Modules:
  0.0 110.5 jit_solution(11861563639395866219)
XLA Ops:
  0.6 0.7 pad_maximum_fusion.2
  1.4 17.7 %all_to_all.20 = bf16[16,48,128]{2,1,0:T(8,128)(2,1)S(1)} all-to-all(bf16[16,48,128]{2,1,0:T(8,128)(2,1)S(1)} %broadcast_in_dim.3), channel_id=1, replica_groups=mesh['x'=4,'zl'=4,'core'=2,'y'=8,'zh'=2] {'x','zl'}, dimensions={0} | all-to-all | bytes 393216 | tf_op jit(solution)/shard_map/all_to_all | solution.py:17
  19.1 4.8 %collective-permute-start = (bf16[16,48,128]{2,1,0:T(8,128)(2,1)S(1)}, bf16[16,48,128]{2,1,0:T(8,128)(2,1)S(1)}, u32[]{:S(2)}, u32[]{:S(2)}) collective-permute-start(bf16[16,48,128]{2,1,0:T(8,128)(2,1)S(1)} %all_to_all.20), channel_id=1, source_target_pairs={{0,16},{16,0},{1,17},{17,1},{2,18},{18,2},{3,19},{19,3},{4,20},{20... | collective-permute-start | bytes 589832 | tf_op jit(solution)/shard_map/ppermute | solution.py:26
  23.9 1.5 %read_weights.1 = (bf16[512,640]{1,0:T(8,128)(2,1)S(1)}, bf16[512,640]{1,0:T(8,128)(2,1)S(1)}, bf16[640,512]{1,0:T(8,128)(2,1)S(1)}, bf16[12,640]{1,0:T(8,128)(2,1)S(1)}) custom-call(s32[1]{0:T(128)} %bitcast.core_ref, bf16[8,128]{1,0:T(8,128)(2,1)S(1)} %slice_bitcast_fusion.n_ref, bf16[512,640]{1,0:T(8,128)(2,1)} %g_hbm.1, bf16[512,640]{1,0:T(8,128)(2,1)} %u_hbm.1, ...), custom_call_target="tpu_custom_call" | custom-call | flops 1000000000 | bytes 2097152 | tf_op jit(solution)/shard_map/read_weights/pallas_call | solution.py:70
  25.5 0.0 collective-permute-done
  25.6 0.1 reshape.39.c_ref
  25.7 0.0 copy-start
  25.7 0.1 reshape.38.t_ref
  25.9 0.0 copy-start.2
  25.9 0.7 products.1
  26.6 0.0 copy-done
  26.6 0.0 copy-done.2
  26.6 29.2 %all_to_all.21 = bf16[8,72,640]{2,1,0:T(8,128)(2,1)S(1)} all-to-all(bf16[8,72,640]{2,1,0:T(8,128)(2,1)S(1)} %get-tuple-element.27), channel_id=1, replica_groups=mesh['x'=4,'zl'=4,'core'=2,'y'=8,'zh'=2] {'y'}, dimensions={0} | all-to-all | bytes 1474560 | tf_op jit(solution)/shard_map/all_to_all | solution.py:17
  55.8 0.1 convert_reduce_fusion
  55.9 7.9 %collective-permute-start.1 = (bf16[84,640]{1,0:T(8,128)(2,1)S(1)}, bf16[84,640]{1,0:T(8,128)(2,1)S(1)}, u32[]{:S(2)}, u32[]{:S(2)}) collective-permute-start(bf16[84,640]{1,0:T(8,128)(2,1)S(1)} %pad_maximum_fusion.1), channel_id=1, source_target_pairs={{0,1},{1,0},{2,3},{3,2},{4,5},{5,4},{6,7},{7,6},{8,9},{9,8},{10,11... | collective-permute-start | bytes 322568 | tf_op jit(solution)/shard_map/ppermute | solution.py:26
  63.9 3.0 %collective-permute-done.1.o_ref = bf16[84,640]{1,0:T(8,128)(2,1)S(1)} collective-permute-done((bf16[84,640]{1,0:T(8,128)(2,1)S(1)}, bf16[84,640]{1,0:T(8,128)(2,1)S(1)}, u32[]{:S(2)}, u32[]{:S(2)}) %collective-permute-start.1) | collective-permute-done | bytes 107552 | tf_op jit(solution)/shard_map/ppermute | solution.py:26
  66.9 0.1 activations.1
  67.0 22.8 %all_to_all.22.s_ref = bf16[8,72,640]{2,1,0:T(8,128)(2,1)S(1)} all-to-all(bf16[8,72,640]{2,1,0:T(8,128)(2,1)S(1)} %activations.1), channel_id=1, replica_groups=mesh['x'=4,'zl'=4,'core'=2,'y'=8,'zh'=2] {'y'}, dimensions={0} | all-to-all | bytes 1474560 | tf_op jit(solution)/shard_map/all_to_all | solution.py:17
  89.8 0.7 shard_map.101
  90.6 0.1 reshape.40
  90.6 0.1 fusion.4
  90.7 0.0 copy-start.1
  90.7 0.0 copy-start.3
  90.7 4.7 %collective-permute-start.2 = (f32[2,16,24,128]{3,2,0,1:T(8,128)S(1)}, f32[2,16,24,128]{3,2,0,1:T(8,128)S(1)}, u32[]{:S(2)}, u32[]{:S(2)}) collective-permute-start(f32[2,16,24,128]{3,2,0,1:T(8,128)S(1)} %bitcast.24), channel_id=1, source_target_pairs={{0,16},{16,0},{1,17},{17,1},{2,18},{18,2},{3,19},{19,3},{4,20},{20... | collective-permute-start | bytes 1179656 | tf_op jit(solution)/shard_map/ppermute | solution.py:26
  95.4 1.3 %collective-permute-done.2 = f32[2,16,24,128]{3,2,0,1:T(8,128)S(1)} collective-permute-done((f32[2,16,24,128]{3,2,0,1:T(8,128)S(1)}, f32[2,16,24,128]{3,2,0,1:T(8,128)S(1)}, u32[]{:S(2)}, u32[]{:S(2)}) %collective-permute-start.2) | collective-permute-done | bytes 393248 | tf_op jit(solution)/shard_map/ppermute | solution.py:26
  96.7 0.7 fusion.1
  97.5 4.8 %all-to-all-start.3 = ((bf16[16,48,128]{2,1,0:T(8,128)(2,1)}), bf16[16,48,128]{2,1,0:T(8,128)(2,1)S(1)}, u32[]{:S(2)}, u32[]{:S(2)}) async-start(bf16[16,48,128]{2,1,0:T(8,128)(2,1)} %bitcast.9), calls=%async_computation.3 | async-start | bytes 393216 | tf_op jit(solution)/shard_map/all_to_all | solution.py:17
  102.3 0.0 copy-done.1
  102.3 0.0 copy-done.3
  102.4 1.8 %shard_map.102 = (bf16[640,512]{1,0:T(8,128)(2,1)}, bf16[512,640]{1,0:T(8,128)(2,1)}, bf16[512,640]{1,0:T(8,128)(2,1)}) custom-call(bf16[8,72,640]{2,1,0:T(8,128)(2,1)S(1)} %all_to_all.22.s_ref, bf16[192,512]{1,0:T(8,128)(2,1)S(1)} %copy-done.3, bf16[192,512]{1,0:T(8,128)(2,1)S(1)} %copy-done.1), custom_call_target="tpu_custom_call" | custom-call | flops 377487360 | bytes 2260992 | tf_op jit(solution)/shard_map/pallas_call | solution.py:37
  104.2 5.7 %all-to-all-done.3.a_ref = bf16[16,48,128]{2,1,0:T(8,128)(2,1)S(1)} async-done(((bf16[16,48,128]{2,1,0:T(8,128)(2,1)}), bf16[16,48,128]{2,1,0:T(8,128)(2,1)S(1)}, u32[]{:S(2)}, u32[]{:S(2)}) %all-to-all-start.3) | async-done | bytes 196640 | tf_op jit(solution)/shard_map/all_to_all | solution.py:17
  109.8 0.6 own_outputs.1
  (9 shorter events, 0.2 us)
Async XLA Ops:
  19.1 6.4 %collective-permute-start = (bf16[16,48,128]{2,1,0:T(8,128)(2,1)S(1)}, bf16[16,48,128]{2,1,0:T(8,128)(2,1)S(1)}, u32[]{:S(2)}, u32[]{:S(2)}) collective-permute-start(bf16[16,48,128]{2,1,0:T(8,128)(2,1)S(1)} %all_to_all.20), channel_id=1, source_target_pairs={{0,16},{16,0},{1,17},{17,1},{2,18},{18,2},{3,19},{19,3},{4,20},{20... | collective-permute-start | bytes 589832 | tf_op jit(solution)/shard_map/ppermute | solution.py:26
  25.7 0.9 copy-start
  25.9 0.7 copy-start.2
  55.9 10.9 %collective-permute-start.1 = (bf16[84,640]{1,0:T(8,128)(2,1)S(1)}, bf16[84,640]{1,0:T(8,128)(2,1)S(1)}, u32[]{:S(2)}, u32[]{:S(2)}) collective-permute-start(bf16[84,640]{1,0:T(8,128)(2,1)S(1)} %pad_maximum_fusion.1), channel_id=1, source_target_pairs={{0,1},{1,0},{2,3},{3,2},{4,5},{5,4},{6,7},{7,6},{8,9},{9,8},{10,11... | collective-permute-start | bytes 322568 | tf_op jit(solution)/shard_map/ppermute | solution.py:26
  90.7 11.6 %copy-start.1 = (bf16[192,512]{1,0:T(8,128)(2,1)S(1)}, bf16[192,512]{1,0:T(8,128)(2,1)}, u32[]{:S(2)}) copy-start(bf16[192,512]{1,0:T(8,128)(2,1)} %copy-done) | copy-start | bytes 589828
  90.7 11.6 %copy-start.3 = (bf16[192,512]{1,0:T(8,128)(2,1)S(1)}, bf16[192,512]{1,0:T(8,128)(2,1)}, u32[]{:S(2)}) copy-start(bf16[192,512]{1,0:T(8,128)(2,1)} %copy-done.2) | copy-start | bytes 589828
  90.7 6.0 %collective-permute-start.2 = (f32[2,16,24,128]{3,2,0,1:T(8,128)S(1)}, f32[2,16,24,128]{3,2,0,1:T(8,128)S(1)}, u32[]{:S(2)}, u32[]{:S(2)}) collective-permute-start(f32[2,16,24,128]{3,2,0,1:T(8,128)S(1)} %bitcast.24), channel_id=1, source_target_pairs={{0,16},{16,0},{1,17},{17,1},{2,18},{18,2},{3,19},{19,3},{4,20},{20... | collective-permute-start | bytes 1179656 | tf_op jit(solution)/shard_map/ppermute | solution.py:26
  97.5 12.4 %all-to-all-start.3 = ((bf16[16,48,128]{2,1,0:T(8,128)(2,1)}), bf16[16,48,128]{2,1,0:T(8,128)(2,1)S(1)}, u32[]{:S(2)}, u32[]{:S(2)}) async-start(bf16[16,48,128]{2,1,0:T(8,128)(2,1)} %bitcast.9), calls=%async_computation.3 | async-start | bytes 393216 | tf_op jit(solution)/shard_map/all_to_all | solution.py:17

commit v8 on v7

--- a/solution.py
+++ b/solution.py
@@ -47,6 +47,8 @@
 
 def read_weights(core, near, weights, keep_mask):
     half = keep_mask.shape[0] // 2
+    parts = keep_mask.shape[1] // lanes
+    packed = (keep_mask.shape[0] * parts, lanes)
 
     def kernel(
         core_ref, n_ref, g_hbm, u_hbm, d_hbm, k_hbm,
@@ -59,8 +61,11 @@
         moves[3].wait()
         whole = mask[...].astype(jnp.float32)
         a, b, first = whole[:half], whole[half:], core_ref[0] == 0
-        ordered[:half, :] = jnp.where(first, a, b)
-        ordered[half:, :] = jnp.where(first, b, a)
+        for c in range(parts):
+            to = slice(c * lanes, (c + 1) * lanes)
+            at = 2 * half * c
+            ordered[at : at + half, :] = jnp.where(first, a, b)[:, to]
+            ordered[at + half : at + 2 * half, :] = jnp.where(first, b, a)[:, to]
         keep_ref[...] = ordered[...].astype(keep_ref.dtype)
         for move in moves[:3]:
             move.wait()
@@ -71,13 +76,13 @@
         kernel,
         out_shape=(
             *(pltpu.VMEM(w.shape, w.dtype) for w in weights),
-            pltpu.VMEM(keep_mask.shape, jnp.bfloat16),
+            pltpu.VMEM(packed, jnp.bfloat16),
         ),
         in_specs=[pl.BlockSpec(memory_space=pltpu.SMEM), space, far, far, far, far],
         out_specs=(space,) * 4,
         scratch_shapes=[
             pltpu.VMEM(keep_mask.shape, keep_mask.dtype),
-            pltpu.VMEM(keep_mask.shape, jnp.float32),
+            pltpu.VMEM(packed, jnp.float32),
             pltpu.SemaphoreType.DMA((4,)),
         ],
         cost_estimate=pl.CostEstimate(flops=10**9, bytes_accessed=2 << 20, transcendentals=0),
@@ -86,56 +91,64 @@
     )(core, near, *operands)
 
 
-def activations(side, sums, other, keep, ring):
-    rows, units = sums.shape
-    rows = rows // 3
-    half = rows // 2
+def activations(side, sums, other, keep, ring, parts):
+    total = sums.shape[0]
+    half = other.shape[0] - total
+    rows, half = total // parts // 3, half // parts
 
     def kernel(side_ref, s_ref, o_ref, k_ref, out_ref, factor):
         mine = k_ref[...].astype(jnp.float32)
-        far = o_ref[3 * rows :, :].astype(jnp.float32)
+        far = o_ref[total:, :].astype(jnp.float32)
         first = side_ref[0] == 0
-        factor[:half, :] = jnp.where(first, mine, far)
-        factor[half:, :] = jnp.where(first, far, mine)
-        cuts = [slice(m * rows, (m + 1) * rows) for m in range(3)]
-        gate, up, grad = (s_ref[c, :] + o_ref[c, :].astype(jnp.float32) for c in cuts)
-        keep_factor = factor[...] * keep_scale
-        sigmoid_gate = jax.nn.sigmoid(gate)
-        silu_gate = gate * sigmoid_gate
-        grad_pre = grad * keep_factor
-        values = (
-            silu_gate * up * keep_factor,
-            grad_pre * up * sigmoid_gate * (1.0 + gate * (1.0 - sigmoid_gate)),
-            grad_pre * silu_gate,
-        )
-        for cut, value in zip(cuts, values):
-            value = value.astype(out_ref.dtype)
-            for y in range(ring):
-                out_ref[y, cut, :] = value
+        near, away = jnp.where(first, mine, far), jnp.where(first, far, mine)
+        for c in range(parts):
+            factor[:half, :] = near[half * c : half * (c + 1)]
+            factor[half:, :] = away[half * c : half * (c + 1)]
+            starts = [(3 * c + m) * rows for m in range(3)]
+            cuts = [slice(at, at + rows) for at in starts]
+            gate, up, grad = (s_ref[cut, :] + o_ref[cut, :].astype(jnp.float32) for cut in cuts)
+            keep_factor = factor[...] * keep_scale
+            sigmoid_gate = jax.nn.sigmoid(gate)
+            silu_gate = gate * sigmoid_gate
+            grad_pre = grad * keep_factor
+            values = (
+                silu_gate * up * keep_factor,
+                grad_pre * up * sigmoid_gate * (1.0 + gate * (1.0 - sigmoid_gate)),
+                grad_pre * silu_gate,
+            )
+            for cut, value in zip(cuts, values):
+                value = value.astype(out_ref.dtype)
+                for y in range(ring):
+                    out_ref[y, cut, :] = value
 
     space, smem = (pl.BlockSpec(memory_space=m) for m in (pltpu.VMEM, pltpu.SMEM))
     operands = [pltpu.with_memory_space_constraint(a, pltpu.VMEM) for a in (sums, other, keep)]
     return pl.pallas_call(
         kernel,
-        out_shape=pltpu.VMEM((ring, 3 * rows, units), jnp.bfloat16),
+        out_shape=pltpu.VMEM((ring, total, lanes), jnp.bfloat16),
         in_specs=[smem, space, space, space],
         out_specs=space,
-        scratch_shapes=[pltpu.VMEM((rows, units), jnp.float32)],
+        scratch_shapes=[pltpu.VMEM((rows, lanes), jnp.float32)],
         compiler_params=pltpu.CompilerParams(vmem_limit_bytes=4 << 20),
         name="activations",
     )(side, *operands)
 
 
+def joined(ref, m, rows, parts):
+    total = ref.shape[0] * rows
+    cuts = [slice((3 * c + m) * rows, (3 * c + m + 1) * rows) for c in range(parts)]
+    return jnp.concatenate([ref[:, cut, :].reshape(total, lanes) for cut in cuts], axis=1)
+
+
 def back_products(spread, weights):
     _, _, down_weight = weights
-    ring, rows, units = spread.shape
-    rows = rows // 3
-    total, width = ring * rows, down_weight.shape[1]
+    units, width = down_weight.shape
+    parts = units // lanes
+    ring, rows = spread.shape[0], spread.shape[1] // parts // 3
+    total = ring * rows
 
     def kernel(s_ref, g_ref, u_ref, d_ref, out_ref):
-        hidden, gate, up = (
-            s_ref[:, m * rows : (m + 1) * rows, :].reshape(total, units) for m in range(3)
-        )
+        hidden, gate, up = (joined(s_ref, m, rows, parts) for m in range(3))
         out_ref[0] = dot(hidden, d_ref[...])
         out_ref[1] = dot(gate, g_ref[...], contract_last) + dot(up, u_ref[...], contract_last)
 
@@ -145,14 +158,14 @@
 
 
 def weight_gradients(spread, tokens, cotangent):
-    _, rows, units = spread.shape
-    rows = rows // 3
     total, width = tokens.shape
+    ring = spread.shape[0]
+    rows = total // ring
+    parts = spread.shape[1] // rows // 3
+    units = parts * lanes
 
     def kernel(s_ref, t_ref, c_ref, down_hbm, gate_hbm, up_hbm, down_ref, gate_ref, up_ref, sems):
-        hidden, gate, up = (
-            s_ref[:, m * rows : (m + 1) * rows, :].reshape(total, units) for m in range(3)
-        )
+        hidden, gate, up = (joined(s_ref, m, rows, parts) for m in range(3))
         jobs = (
             (gate_ref, gate_hbm, t_ref, gate),
             (up_ref, up_hbm, t_ref, up),
@@ -197,17 +210,20 @@
 
 def products(tokens, cotangent, weights, place, ring):
     total, units = tokens.shape[0], weights[0].shape[1]
-    rows = total // ring
+    rows, parts = total // ring, units // lanes
 
     def kernel(at_ref, t_ref, c_ref, g_ref, u_ref, d_ref, out_ref, lost_ref, whole):
         own = pl.ds(pl.multiple_of(at_ref[0] * rows, rows), rows)
 
         def put(m, value):
-            to = slice(m * rows, (m + 1) * rows)
-            out_ref[:, to, :] = value.astype(out_ref.dtype).reshape(ring, rows, units)
             whole[...] = value
             kept = whole[own, :]
-            lost_ref[to, :] = kept - kept.astype(out_ref.dtype).astype(jnp.float32)
+            lost = kept - kept.astype(out_ref.dtype).astype(jnp.float32)
+            value = value.astype(out_ref.dtype).reshape(ring, rows, units)
+            for c in range(parts):
+                to = slice((3 * c + m) * rows, (3 * c + m + 1) * rows)
+                out_ref[:, to, :] = value[:, :, c * lanes : (c + 1) * lanes]
+                lost_ref[to, :] = lost[:, c * lanes : (c + 1) * lanes]
 
         put(0, dot(t_ref[...], g_ref[...]))
         put(1, dot(t_ref[...], u_ref[...]))
@@ -219,8 +235,8 @@
     return pl.pallas_call(
         kernel,
         out_shape=(
-            pltpu.VMEM((ring, 3 * rows, units), tokens.dtype),
-            pltpu.VMEM((3 * rows, units), jnp.float32),
+            pltpu.VMEM((ring, 3 * rows * parts, lanes), tokens.dtype),
+            pltpu.VMEM((3 * rows * parts, lanes), jnp.float32),
         ),
         in_specs=[smem] + [space] * len(operands),
         out_specs=(space, space),
@@ -233,7 +249,7 @@
 def body(tokens, gate_weight, up_weight, down_weight, keep_mask, cotangent):
     bf16, f32 = jnp.bfloat16, jnp.float32
     own, width = tokens.shape
-    share, _ = keep_mask.shape
+    share, units = keep_mask.shape
     ring = lax.axis_size("y")
     total = share * 2 * ring
     chips = total // own // 2
@@ -253,7 +269,7 @@
     parts, lost = products(all_tokens, all_cot, weights, place, ring)
     sums = exchange(parts, "y").astype(f32).sum(axis=0) + lost
     other = swapped(jnp.concatenate([sums.astype(bf16), keep], axis=0), "zh")
-    spread = exchange(activations(side, sums, other, keep, ring), "y")
+    spread = exchange(activations(side, sums, other, keep, ring, units // lanes), "y")
 
     parts = back_products(spread, weights).reshape(2, chips, 2, -1, lanes)
     kept, given = parts[:, :, 0], parts[:, :, 1]

time: 111 us -> 111 us (level)
  no operation moved by 1% of the time
where the time goes in v8:
time: 111 us; the launch traced here: 110 us
  blocking collectives  69.7 us (63%)
  starting transfers between devices  22.2 us (20%)
  waiting for transfers between devices  9.91 us (9%)
  Pallas kernels  5.54 us (5%)
  other arithmetic  1.64 us (1%)
    all_to_all x3, blocking collectives, exchange(): return lax.all_to_all(blocks, axis, split_axis=0, concat_axis=0, tiled=True)  69.7 us
    ppermute x3, starting transfers between devices, swapped(): return lax.ppermute(value, axis, [(0, 1), (1, 0)])  17.4 us
    all_to_all x1, waiting for transfers between devices, exchange(): return lax.all_to_all(blocks, axis, split_axis=0, concat_axis=0, tiled=True)  5.66 us
    all_to_all x1, starting transfers between devices, exchange(): return lax.all_to_all(blocks, axis, split_axis=0, concat_axis=0, tiled=True)  4.76 us
    ppermute x3, waiting for transfers between devices, swapped(): return lax.ppermute(value, axis, [(0, 1), (1, 0)])  4.24 us
    pallas_call x2, Pallas kernels, vmem_call(): pl.pallas_call(kernel, out_shape=tuple((out_space(*o) for o in outs)), in...  2.57 us
  transfers between devices with their start and end apart: 4, of which 3 were waited for; matrix products, arithmetic and copies ran while one was open for 0% of the time, Pallas kernels for 3%

profile of v8, /device:TPU:1, one launch (start us, length us, event | category | flops | bytes accessed | tf_op | source)
XLA Modules:
  0.0 110.3 jit_solution(12263726703349658476)
XLA Ops:
  0.6 0.7 pad_maximum_fusion.2
  1.4 17.7 %all_to_all.20 = bf16[16,48,128]{2,1,0:T(8,128)(2,1)S(1)} all-to-all(bf16[16,48,128]{2,1,0:T(8,128)(2,1)S(1)} %broadcast_in_dim.3), channel_id=1, replica_groups=mesh['x'=4,'zl'=4,'core'=2,'y'=8,'zh'=2] {'x','zl'}, dimensions={0} | all-to-all | bytes 393216 | tf_op jit(solution)/shard_map/all_to_all | solution.py:17
  19.1 4.8 %collective-permute-start = (bf16[16,48,128]{2,1,0:T(8,128)(2,1)S(1)}, bf16[16,48,128]{2,1,0:T(8,128)(2,1)S(1)}, u32[]{:S(2)}, u32[]{:S(2)}) collective-permute-start(bf16[16,48,128]{2,1,0:T(8,128)(2,1)S(1)} %all_to_all.20), channel_id=1, source_target_pairs={{0,16},{16,0},{1,17},{17,1},{2,18},{18,2},{3,19},{19,3},{4,20},{20... | collective-permute-start | bytes 589832 | tf_op jit(solution)/shard_map/ppermute | solution.py:26
  23.9 1.5 %read_weights.1 = (bf16[512,640]{1,0:T(8,128)(2,1)S(1)}, bf16[512,640]{1,0:T(8,128)(2,1)S(1)}, bf16[640,512]{1,0:T(8,128)(2,1)S(1)}, bf16[60,128]{1,0:T(8,128)(2,1)S(1)}) custom-call(s32[1]{0:T(128)} %bitcast.core_ref, bf16[8,128]{1,0:T(8,128)(2,1)S(1)} %slice_bitcast_fusion.n_ref, bf16[512,640]{1,0:T(8,128)(2,1)} %g_hbm.1, bf16[512,640]{1,0:T(8,128)(2,1)} %u_hbm.1, ...), custom_call_target="tpu_custom_call" | custom-call | flops 1000000000 | bytes 2097152 | tf_op jit(solution)/shard_map/read_weights/pallas_call | solution.py:75
  25.5 0.0 collective-permute-done
  25.6 0.1 reshape.39.c_ref
  25.7 0.0 copy-start
  25.7 0.1 reshape.38.t_ref
  25.9 0.0 copy-start.2
  25.9 0.7 products.1
  26.6 0.0 copy-done
  26.6 0.0 copy-done.2
  26.6 29.2 %all_to_all.21 = bf16[8,360,128]{2,1,0:T(8,128)(2,1)S(1)} all-to-all(bf16[8,360,128]{2,1,0:T(8,128)(2,1)S(1)} %get-tuple-element.27), channel_id=1, replica_groups=mesh['x'=4,'zl'=4,'core'=2,'y'=8,'zh'=2] {'y'}, dimensions={0} | all-to-all | bytes 1474560 | tf_op jit(solution)/shard_map/all_to_all | solution.py:17
  55.8 0.1 convert_reduce_fusion
  56.0 7.9 %collective-permute-start.1 = (bf16[420,128]{1,0:T(8,128)(2,1)S(1)}, bf16[420,128]{1,0:T(8,128)(2,1)S(1)}, u32[]{:S(2)}, u32[]{:S(2)}) collective-permute-start(bf16[420,128]{1,0:T(8,128)(2,1)S(1)} %pad_maximum_fusion.1), channel_id=1, source_target_pairs={{0,1},{1,0},{2,3},{3,2},{4,5},{5,4},{6,7},{7,6},{8,9},{9,8},{10,11... | collective-permute-start | bytes 322568 | tf_op jit(solution)/shard_map/ppermute | solution.py:26
  63.9 2.9 %collective-permute-done.1.o_ref = bf16[420,128]{1,0:T(8,128)(2,1)S(1)} collective-permute-done((bf16[420,128]{1,0:T(8,128)(2,1)S(1)}, bf16[420,128]{1,0:T(8,128)(2,1)S(1)}, u32[]{:S(2)}, u32[]{:S(2)}) %collective-permute-start.1) | collective-permute-done | bytes 107552 | tf_op jit(solution)/shard_map/ppermute | solution.py:26
  66.8 0.1 activations.1
  66.9 22.8 %all_to_all.22.s_ref = bf16[8,360,128]{2,1,0:T(8,128)(2,1)S(1)} all-to-all(bf16[8,360,128]{2,1,0:T(8,128)(2,1)S(1)} %activations.1), channel_id=1, replica_groups=mesh['x'=4,'zl'=4,'core'=2,'y'=8,'zh'=2] {'y'}, dimensions={0} | all-to-all | bytes 1474560 | tf_op jit(solution)/shard_map/all_to_all | solution.py:17
  89.7 0.7 shard_map.101
  90.5 0.1 reshape.40
  90.5 0.1 fusion.4
  90.6 0.0 copy-start.1
  90.6 0.0 copy-start.3
  90.6 4.7 %collective-permute-start.2 = (f32[2,16,24,128]{3,2,0,1:T(8,128)S(1)}, f32[2,16,24,128]{3,2,0,1:T(8,128)S(1)}, u32[]{:S(2)}, u32[]{:S(2)}) collective-permute-start(f32[2,16,24,128]{3,2,0,1:T(8,128)S(1)} %bitcast.24), channel_id=1, source_target_pairs={{0,16},{16,0},{1,17},{17,1},{2,18},{18,2},{3,19},{19,3},{4,20},{20... | collective-permute-start | bytes 1179656 | tf_op jit(solution)/shard_map/ppermute | solution.py:26
  95.3 1.3 %collective-permute-done.2 = f32[2,16,24,128]{3,2,0,1:T(8,128)S(1)} collective-permute-done((f32[2,16,24,128]{3,2,0,1:T(8,128)S(1)}, f32[2,16,24,128]{3,2,0,1:T(8,128)S(1)}, u32[]{:S(2)}, u32[]{:S(2)}) %collective-permute-start.2) | collective-permute-done | bytes 393248 | tf_op jit(solution)/shard_map/ppermute | solution.py:26
  96.6 0.7 fusion.1
  97.4 4.8 %all-to-all-start.3 = ((bf16[16,48,128]{2,1,0:T(8,128)(2,1)}), bf16[16,48,128]{2,1,0:T(8,128)(2,1)S(1)}, u32[]{:S(2)}, u32[]{:S(2)}) async-start(bf16[16,48,128]{2,1,0:T(8,128)(2,1)} %bitcast.9), calls=%async_computation.3 | async-start | bytes 393216 | tf_op jit(solution)/shard_map/all_to_all | solution.py:17
  102.1 0.0 copy-done.1
  102.2 0.0 copy-done.3
  102.2 1.8 %shard_map.102 = (bf16[640,512]{1,0:T(8,128)(2,1)}, bf16[512,640]{1,0:T(8,128)(2,1)}, bf16[512,640]{1,0:T(8,128)(2,1)}) custom-call(bf16[8,360,128]{2,1,0:T(8,128)(2,1)S(1)} %all_to_all.22.s_ref, bf16[192,512]{1,0:T(8,128)(2,1)S(1)} %copy-done.3, bf16[192,512]{1,0:T(8,128)(2,1)S(1)} %copy-done.1), custom_call_target="tpu_custom_call" | custom-call | flops 377487360 | bytes 2260992 | tf_op jit(solution)/shard_map/pallas_call | solution.py:37
  104.0 5.7 %all-to-all-done.3.a_ref = bf16[16,48,128]{2,1,0:T(8,128)(2,1)S(1)} async-done(((bf16[16,48,128]{2,1,0:T(8,128)(2,1)}), bf16[16,48,128]{2,1,0:T(8,128)(2,1)S(1)}, u32[]{:S(2)}, u32[]{:S(2)}) %all-to-all-start.3) | async-done | bytes 196640 | tf_op jit(solution)/shard_map/all_to_all | solution.py:17
  109.7 0.6 own_outputs.1
  (9 shorter events, 0.2 us)
Async XLA Ops:
  19.1 6.4 %collective-permute-start = (bf16[16,48,128]{2,1,0:T(8,128)(2,1)S(1)}, bf16[16,48,128]{2,1,0:T(8,128)(2,1)S(1)}, u32[]{:S(2)}, u32[]{:S(2)}) collective-permute-start(bf16[16,48,128]{2,1,0:T(8,128)(2,1)S(1)} %all_to_all.20), channel_id=1, source_target_pairs={{0,16},{16,0},{1,17},{17,1},{2,18},{18,2},{3,19},{19,3},{4,20},{20... | collective-permute-start | bytes 589832 | tf_op jit(solution)/shard_map/ppermute | solution.py:26
  25.7 0.9 copy-start
  25.9 0.7 copy-start.2
  56.0 10.9 %collective-permute-start.1 = (bf16[420,128]{1,0:T(8,128)(2,1)S(1)}, bf16[420,128]{1,0:T(8,128)(2,1)S(1)}, u32[]{:S(2)}, u32[]{:S(2)}) collective-permute-start(bf16[420,128]{1,0:T(8,128)(2,1)S(1)} %pad_maximum_fusion.1), channel_id=1, source_target_pairs={{0,1},{1,0},{2,3},{3,2},{4,5},{5,4},{6,7},{7,6},{8,9},{9,8},{10,11... | collective-permute-start | bytes 322568 | tf_op jit(solution)/shard_map/ppermute | solution.py:26
  90.6 11.5 %copy-start.1 = (bf16[192,512]{1,0:T(8,128)(2,1)S(1)}, bf16[192,512]{1,0:T(8,128)(2,1)}, u32[]{:S(2)}) copy-start(bf16[192,512]{1,0:T(8,128)(2,1)} %copy-done) | copy-start | bytes 589828
  90.6 11.5 %copy-start.3 = (bf16[192,512]{1,0:T(8,128)(2,1)S(1)}, bf16[192,512]{1,0:T(8,128)(2,1)}, u32[]{:S(2)}) copy-start(bf16[192,512]{1,0:T(8,128)(2,1)} %copy-done.2) | copy-start | bytes 589828
  90.6 6.0 %collective-permute-start.2 = (f32[2,16,24,128]{3,2,0,1:T(8,128)S(1)}, f32[2,16,24,128]{3,2,0,1:T(8,128)S(1)}, u32[]{:S(2)}, u32[]{:S(2)}) collective-permute-start(f32[2,16,24,128]{3,2,0,1:T(8,128)S(1)} %bitcast.24), channel_id=1, source_target_pairs={{0,16},{16,0},{1,17},{17,1},{2,18},{18,2},{3,19},{19,3},{4,20},{20... | collective-permute-start | bytes 1179656 | tf_op jit(solution)/shard_map/ppermute | solution.py:26
  97.4 12.3 %all-to-all-start.3 = ((bf16[16,48,128]{2,1,0:T(8,128)(2,1)}), bf16[16,48,128]{2,1,0:T(8,128)(2,1)S(1)}, u32[]{:S(2)}, u32[]{:S(2)}) async-start(bf16[16,48,128]{2,1,0:T(8,128)(2,1)} %bitcast.9), calls=%async_computation.3 | async-start | bytes 393216 | tf_op jit(solution)/shard_map/all_to_all | solution.py:17

commit v9 on v8

--- a/solution.py
+++ b/solution.py
@@ -93,12 +93,13 @@
 
 def activations(side, sums, other, keep, ring, parts):
     total = sums.shape[0]
-    half = other.shape[0] - total
-    rows, half = total // parts // 3, half // parts
+    rows = total // parts // 3
+    more = total + parts * rows
+    half = (other.shape[0] - more) // parts
 
     def kernel(side_ref, s_ref, o_ref, k_ref, out_ref, factor):
         mine = k_ref[...].astype(jnp.float32)
-        far = o_ref[total:, :].astype(jnp.float32)
+        far = o_ref[more:, :].astype(jnp.float32)
         first = side_ref[0] == 0
         near, away = jnp.where(first, mine, far), jnp.where(first, far, mine)
         for c in range(parts):
@@ -107,6 +108,8 @@
             starts = [(3 * c + m) * rows for m in range(3)]
             cuts = [slice(at, at + rows) for at in starts]
             gate, up, grad = (s_ref[cut, :] + o_ref[cut, :].astype(jnp.float32) for cut in cuts)
+            second = slice(total + c * rows, total + (c + 1) * rows)
+            gate = gate + o_ref[second, :].astype(jnp.float32)
             keep_factor = factor[...] * keep_scale
             sigmoid_gate = jax.nn.sigmoid(gate)
             silu_gate = gate * sigmoid_gate
@@ -268,7 +271,9 @@
 
     parts, lost = products(all_tokens, all_cot, weights, place, ring)
     sums = exchange(parts, "y").astype(f32).sum(axis=0) + lost
-    other = swapped(jnp.concatenate([sums.astype(bf16), keep], axis=0), "zh")
+    high = lax.reduce_precision(sums, 8, 7)
+    low = (sums - high).reshape(units // lanes, 3, -1, lanes)[:, 0].reshape(-1, lanes)
+    other = swapped(jnp.concatenate([high.astype(bf16), low.astype(bf16), keep], axis=0), "zh")
     spread = exchange(activations(side, sums, other, keep, ring, units // lanes), "y")
 
     parts = back_products(spread, weights).reshape(2, chips, 2, -1, lanes)

time: 111 us -> 113 us (1.018)
  no operation moved by 1% of the time
where the time goes in v9:
time: 113 us; the launch traced here: 112 us
  blocking collectives  69.7 us (62%)
  starting transfers between devices  22.8 us (20%)
  waiting for transfers between devices  10.6 us (9%)
  Pallas kernels  5.55 us (5%)
  other arithmetic  1.67 us (1%)
    all_to_all x3, blocking collectives, exchange(): return lax.all_to_all(blocks, axis, split_axis=0, concat_axis=0, tiled=True)  69.7 us
    ppermute x3, starting transfers between devices, swapped(): return lax.ppermute(value, axis, [(0, 1), (1, 0)])  17.4 us
    all_to_all x1, waiting for transfers between devices, exchange(): return lax.all_to_all(blocks, axis, split_axis=0, concat_axis=0, tiled=True)  5.66 us
    all_to_all x1, starting transfers between devices, exchange(): return lax.all_to_all(blocks, axis, split_axis=0, concat_axis=0, tiled=True)  5.41 us
    ppermute x3, waiting for transfers between devices, swapped(): return lax.ppermute(value, axis, [(0, 1), (1, 0)])  4.9 us
    pallas_call x2, Pallas kernels, vmem_call(): pl.pallas_call(kernel, out_shape=tuple((out_space(*o) for o in outs)), in...  2.57 us
  transfers between devices with their start and end apart: 4, of which 3 were waited for; matrix products, arithmetic and copies ran while one was open for 0% of the time, Pallas kernels for 3%

profile of v9, /device:TPU:1, one launch (start us, length us, event | category | flops | bytes accessed | tf_op | source)
XLA Modules:
  0.0 111.7 jit_solution(2998185009267246608)
XLA Ops:
  0.6 0.7 pad_maximum_fusion.2
  1.4 17.7 %all_to_all.20 = bf16[16,48,128]{2,1,0:T(8,128)(2,1)S(1)} all-to-all(bf16[16,48,128]{2,1,0:T(8,128)(2,1)S(1)} %broadcast_in_dim.3), channel_id=1, replica_groups=mesh['x'=4,'zl'=4,'core'=2,'y'=8,'zh'=2] {'x','zl'}, dimensions={0} | all-to-all | bytes 393216 | tf_op jit(solution)/shard_map/all_to_all | solution.py:17
  19.1 4.8 %collective-permute-start = (bf16[16,48,128]{2,1,0:T(8,128)(2,1)S(1)}, bf16[16,48,128]{2,1,0:T(8,128)(2,1)S(1)}, u32[]{:S(2)}, u32[]{:S(2)}) collective-permute-start(bf16[16,48,128]{2,1,0:T(8,128)(2,1)S(1)} %all_to_all.20), channel_id=1, source_target_pairs={{0,16},{16,0},{1,17},{17,1},{2,18},{18,2},{3,19},{19,3},{4,20},{20... | collective-permute-start | bytes 589832 | tf_op jit(solution)/shard_map/ppermute | solution.py:26
  23.9 1.5 %read_weights.1 = (bf16[512,640]{1,0:T(8,128)(2,1)S(1)}, bf16[512,640]{1,0:T(8,128)(2,1)S(1)}, bf16[640,512]{1,0:T(8,128)(2,1)S(1)}, bf16[60,128]{1,0:T(8,128)(2,1)S(1)}) custom-call(s32[1]{0:T(128)} %bitcast.core_ref, bf16[8,128]{1,0:T(8,128)(2,1)S(1)} %slice_bitcast_fusion.n_ref, bf16[512,640]{1,0:T(8,128)(2,1)} %g_hbm.1, bf16[512,640]{1,0:T(8,128)(2,1)} %u_hbm.1, ...), custom_call_target="tpu_custom_call" | custom-call | flops 1000000000 | bytes 2097152 | tf_op jit(solution)/shard_map/read_weights/pallas_call | solution.py:75
  25.5 0.0 collective-permute-done
  25.6 0.1 reshape.44.c_ref
  25.7 0.0 copy-start
  25.7 0.1 reshape.43.t_ref
  25.9 0.0 copy-start.2
  25.9 0.7 products.1
  26.6 0.0 copy-done
  26.6 0.0 copy-done.2
  26.6 29.2 %all_to_all.21 = bf16[8,360,128]{2,1,0:T(8,128)(2,1)S(1)} all-to-all(bf16[8,360,128]{2,1,0:T(8,128)(2,1)S(1)} %get-tuple-element.27), channel_id=1, replica_groups=mesh['x'=4,'zl'=4,'core'=2,'y'=8,'zh'=2] {'y'}, dimensions={0} | all-to-all | bytes 1474560 | tf_op jit(solution)/shard_map/all_to_all | solution.py:17
  55.8 0.1 convert_reduce_fusion
  56.0 7.9 %collective-permute-start.1 = (bf16[540,128]{1,0:T(8,128)(2,1)S(1)}, bf16[540,128]{1,0:T(8,128)(2,1)S(1)}, u32[]{:S(2)}, u32[]{:S(2)}) collective-permute-start(bf16[540,128]{1,0:T(8,128)(2,1)S(1)} %pad_maximum_fusion.1), channel_id=1, source_target_pairs={{0,1},{1,0},{2,3},{3,2},{4,5},{5,4},{6,7},{7,6},{8,9},{9,8},{10,11... | collective-permute-start | bytes 414728 | tf_op jit(solution)/shard_map/ppermute | solution.py:26
  64.0 3.6 %collective-permute-done.1.o_ref = bf16[540,128]{1,0:T(8,128)(2,1)S(1)} collective-permute-done((bf16[540,128]{1,0:T(8,128)(2,1)S(1)}, bf16[540,128]{1,0:T(8,128)(2,1)S(1)}, u32[]{:S(2)}, u32[]{:S(2)}) %collective-permute-start.1) | collective-permute-done | bytes 138272 | tf_op jit(solution)/shard_map/ppermute | solution.py:26
  67.5 0.1 activations.1
  67.6 22.8 %all_to_all.22.s_ref = bf16[8,360,128]{2,1,0:T(8,128)(2,1)S(1)} all-to-all(bf16[8,360,128]{2,1,0:T(8,128)(2,1)S(1)} %activations.1), channel_id=1, replica_groups=mesh['x'=4,'zl'=4,'core'=2,'y'=8,'zh'=2] {'y'}, dimensions={0} | all-to-all | bytes 1474560 | tf_op jit(solution)/shard_map/all_to_all | solution.py:17
  90.4 0.8 shard_map.101
  91.2 0.1 reshape.46
  91.2 0.1 fusion.4
  91.3 0.0 copy-start.1
  91.3 0.0 copy-start.3
  91.4 4.7 %collective-permute-start.2 = (f32[2,16,24,128]{3,2,0,1:T(8,128)S(1)}, f32[2,16,24,128]{3,2,0,1:T(8,128)S(1)}, u32[]{:S(2)}, u32[]{:S(2)}) collective-permute-start(f32[2,16,24,128]{3,2,0,1:T(8,128)S(1)} %bitcast.28), channel_id=1, source_target_pairs={{0,16},{16,0},{1,17},{17,1},{2,18},{18,2},{3,19},{19,3},{4,20},{20... | collective-permute-start | bytes 1179656 | tf_op jit(solution)/shard_map/ppermute | solution.py:26
  96.0 1.3 %collective-permute-done.2 = f32[2,16,24,128]{3,2,0,1:T(8,128)S(1)} collective-permute-done((f32[2,16,24,128]{3,2,0,1:T(8,128)S(1)}, f32[2,16,24,128]{3,2,0,1:T(8,128)S(1)}, u32[]{:S(2)}, u32[]{:S(2)}) %collective-permute-start.2) | collective-permute-done | bytes 393248 | tf_op jit(solution)/shard_map/ppermute | solution.py:26
  97.3 0.7 fusion.1
  98.1 5.4 %all-to-all-start.3 = ((bf16[16,48,128]{2,1,0:T(8,128)(2,1)}), bf16[16,48,128]{2,1,0:T(8,128)(2,1)S(1)}, u32[]{:S(2)}, u32[]{:S(2)}) async-start(bf16[16,48,128]{2,1,0:T(8,128)(2,1)} %bitcast.11), calls=%async_computation.3 | async-start | bytes 393216 | tf_op jit(solution)/shard_map/all_to_all | solution.py:17
  103.5 0.0 copy-done.1
  103.5 0.0 copy-done.3
  103.5 1.8 %shard_map.102 = (bf16[640,512]{1,0:T(8,128)(2,1)}, bf16[512,640]{1,0:T(8,128)(2,1)}, bf16[512,640]{1,0:T(8,128)(2,1)}) custom-call(bf16[8,360,128]{2,1,0:T(8,128)(2,1)S(1)} %all_to_all.22.s_ref, bf16[192,512]{1,0:T(8,128)(2,1)S(1)} %copy-done.3, bf16[192,512]{1,0:T(8,128)(2,1)S(1)} %copy-done.1), custom_call_target="tpu_custom_call" | custom-call | flops 377487360 | bytes 2260992 | tf_op jit(solution)/shard_map/pallas_call | solution.py:37
  105.4 5.7 %all-to-all-done.3.a_ref = bf16[16,48,128]{2,1,0:T(8,128)(2,1)S(1)} async-done(((bf16[16,48,128]{2,1,0:T(8,128)(2,1)}), bf16[16,48,128]{2,1,0:T(8,128)(2,1)S(1)}, u32[]{:S(2)}, u32[]{:S(2)}) %all-to-all-start.3) | async-done | bytes 196640 | tf_op jit(solution)/shard_map/all_to_all | solution.py:17
  111.0 0.6 own_outputs.1
  (11 shorter events, 0.2 us)
Async XLA Ops:
  19.1 6.4 %collective-permute-start = (bf16[16,48,128]{2,1,0:T(8,128)(2,1)S(1)}, bf16[16,48,128]{2,1,0:T(8,128)(2,1)S(1)}, u32[]{:S(2)}, u32[]{:S(2)}) collective-permute-start(bf16[16,48,128]{2,1,0:T(8,128)(2,1)S(1)} %all_to_all.20), channel_id=1, source_target_pairs={{0,16},{16,0},{1,17},{17,1},{2,18},{18,2},{3,19},{19,3},{4,20},{20... | collective-permute-start | bytes 589832 | tf_op jit(solution)/shard_map/ppermute | solution.py:26
  25.7 0.9 copy-start
  25.9 0.7 copy-start.2
  56.0 11.5 %collective-permute-start.1 = (bf16[540,128]{1,0:T(8,128)(2,1)S(1)}, bf16[540,128]{1,0:T(8,128)(2,1)S(1)}, u32[]{:S(2)}, u32[]{:S(2)}) collective-permute-start(bf16[540,128]{1,0:T(8,128)(2,1)S(1)} %pad_maximum_fusion.1), channel_id=1, source_target_pairs={{0,1},{1,0},{2,3},{3,2},{4,5},{5,4},{6,7},{7,6},{8,9},{9,8},{10,11... | collective-permute-start | bytes 414728 | tf_op jit(solution)/shard_map/ppermute | solution.py:26
  91.3 12.2 %copy-start.1 = (bf16[192,512]{1,0:T(8,128)(2,1)S(1)}, bf16[192,512]{1,0:T(8,128)(2,1)}, u32[]{:S(2)}) copy-start(bf16[192,512]{1,0:T(8,128)(2,1)} %copy-done) | copy-start | bytes 589828
  91.3 12.2 %copy-start.3 = (bf16[192,512]{1,0:T(8,128)(2,1)S(1)}, bf16[192,512]{1,0:T(8,128)(2,1)}, u32[]{:S(2)}) copy-start(bf16[192,512]{1,0:T(8,128)(2,1)} %copy-done.2) | copy-start | bytes 589828
  91.4 6.0 %collective-permute-start.2 = (f32[2,16,24,128]{3,2,0,1:T(8,128)S(1)}, f32[2,16,24,128]{3,2,0,1:T(8,128)S(1)}, u32[]{:S(2)}, u32[]{:S(2)}) collective-permute-start(f32[2,16,24,128]{3,2,0,1:T(8,128)S(1)} %bitcast.28), channel_id=1, source_target_pairs={{0,16},{16,0},{1,17},{17,1},{2,18},{18,2},{3,19},{19,3},{4,20},{20... | collective-permute-start | bytes 1179656 | tf_op jit(solution)/shard_map/ppermute | solution.py:26
  98.1 12.9 %all-to-all-start.3 = ((bf16[16,48,128]{2,1,0:T(8,128)(2,1)}), bf16[16,48,128]{2,1,0:T(8,128)(2,1)S(1)}, u32[]{:S(2)}, u32[]{:S(2)}) async-start(bf16[16,48,128]{2,1,0:T(8,128)(2,1)} %bitcast.11), calls=%async_computation.3 | async-start | bytes 393216 | tf_op jit(solution)/shard_map/all_to_all | solution.py:17

commit v10 on v8

--- a/solution.py
+++ b/solution.py
@@ -10,7 +10,7 @@
 contract_last = (((1,), (1,)), ((), ()))
 contract_first = (((0,), (0,)), ((), ()))
 lanes = 128
-plane = ("x", "zl")
+plane = ("zl", "x")
 
 
 def exchange(blocks, axis):
@@ -20,6 +20,11 @@
 def sent_to_all(block, axis):
     copies = jnp.broadcast_to(block, (lax.axis_size(axis), *block.shape))
     return exchange(copies, axis)
+
+
+def flipped(blocks, first, second):
+    sizes = lax.axis_size(first), lax.axis_size(second)
+    return jnp.swapaxes(blocks.reshape(*sizes, *blocks.shape[1:]), 0, 1).reshape(blocks.shape)
 
 
 def swapped(value, axis):
@@ -262,7 +267,7 @@
     weights = (gate_weight, up_weight, down_weight)
     other = swapped(near, "core")
     *weights, keep = read_weights(core, near[0, :8], weights, keep_mask)
-    both = jnp.stack([near, other], axis=1)
+    both = flipped(jnp.stack([near, other], axis=1), *plane)
     all_tokens = both[:, :, :half].reshape(total, width)
     all_cot = both[:, :, half:].reshape(total, width)
 
@@ -276,6 +281,7 @@
     other = swapped(given, "core")
     down_grad, gate_grad, up_grad = weight_gradients(spread, all_tokens, all_cot)
     parts = jnp.swapaxes((kept + other).astype(bf16), 0, 1).reshape(chips, -1, lanes)
+    parts = flipped(parts, *plane[::-1])
     mixed_out, input_grad = own_outputs(exchange(parts, plane), own, width)
     return (mixed_out, input_grad, gate_grad, up_grad, down_grad)
 

time: 111 us -> 112 us (level)
  waiting for transfers between devices: 9.91 us -> 11.3 us
    all_to_all x1, waiting for transfers between devices: 5.66 us -> 7.03 us  [exchange(): return lax.all_to_all(blocks, axis, split_axis=0, concat_axis=0, tiled=True)]
where the time goes in v10:
time: 112 us
  blocking collectives  70.6 us (63%)
  starting transfers between devices  21.2 us (19%)
  waiting for transfers between devices  11.3 us (10%)
  Pallas kernels  5.54 us (5%)
  local copies, waits for them, and re-layouts  1.22 us (1%)
    all_to_all x3, blocking collectives, exchange(): return lax.all_to_all(blocks, axis, split_axis=0, concat_axis=0, tiled=True)  70.6 us
    ppermute x3, starting transfers between devices, swapped(): return lax.ppermute(value, axis, [(0, 1), (1, 0)])  16.5 us
    all_to_all x1, waiting for transfers between devices, exchange(): return lax.all_to_all(blocks, axis, split_axis=0, concat_axis=0, tiled=True)  7.03 us
    all_to_all x1, starting transfers between devices, exchange(): return lax.all_to_all(blocks, axis, split_axis=0, concat_axis=0, tiled=True)  4.74 us
    ppermute x3, waiting for transfers between devices, swapped(): return lax.ppermute(value, axis, [(0, 1), (1, 0)])  4.24 us
    pallas_call x2, Pallas kernels, vmem_call(): pl.pallas_call(kernel, out_shape=tuple((out_space(*o) for o in outs)), in...  2.57 us
  transfers between devices with their start and end apart: 4, of which 3 were waited for; matrix products, arithmetic and copies ran while one was open for 0% of the time, Pallas kernels for 3%

profile of v10, /device:TPU:1, one launch (start us, length us, event | category | flops | bytes accessed | tf_op | source)
XLA Modules:
  0.0 111.7 jit_solution(9775748533331731191)
XLA Ops:
  0.6 0.7 pad_maximum_fusion.1
  1.4 18.6 %all_to_all.20 = bf16[16,48,128]{2,1,0:T(8,128)(2,1)S(1)} all-to-all(bf16[16,48,128]{2,1,0:T(8,128)(2,1)S(1)} %broadcast_in_dim.3), channel_id=1, replica_groups=mesh['x'=4,'zl'=4,'core'=2,'y'=8,'zh'=2] {'zl','x'}, dimensions={0} | all-to-all | bytes 393216 | tf_op jit(solution)/shard_map/all_to_all | solution.py:17
  20.1 4.0 %collective-permute-start = (bf16[16,48,128]{2,1,0:T(8,128)(2,1)S(1)}, bf16[16,48,128]{2,1,0:T(8,128)(2,1)S(1)}, u32[]{:S(2)}, u32[]{:S(2)}) collective-permute-start(bf16[16,48,128]{2,1,0:T(8,128)(2,1)S(1)} %all_to_all.20), channel_id=1, source_target_pairs={{0,16},{16,0},{1,17},{17,1},{2,18},{18,2},{3,19},{19,3},{4,20},{20... | collective-permute-start | bytes 589832 | tf_op jit(solution)/shard_map/ppermute | solution.py:31
  24.1 1.5 %read_weights.1 = (bf16[512,640]{1,0:T(8,128)(2,1)S(1)}, bf16[512,640]{1,0:T(8,128)(2,1)S(1)}, bf16[640,512]{1,0:T(8,128)(2,1)S(1)}, bf16[60,128]{1,0:T(8,128)(2,1)S(1)}) custom-call(s32[1]{0:T(128)} %bitcast.core_ref, bf16[8,128]{1,0:T(8,128)(2,1)S(1)} %slice_bitcast_fusion.n_ref, bf16[512,640]{1,0:T(8,128)(2,1)} %g_hbm.1, bf16[512,640]{1,0:T(8,128)(2,1)} %u_hbm.1, ...), custom_call_target="tpu_custom_call" | custom-call | flops 1000000000 | bytes 2097152 | tf_op jit(solution)/shard_map/read_weights/pallas_call | solution.py:80
  25.6 0.0 collective-permute-done
  25.8 0.1 reshape.48.c_ref
  25.9 0.0 copy-start
  25.9 0.1 reshape.47.t_ref
  26.0 0.0 copy-start.2
  26.1 0.7 products.1
  26.8 0.0 copy-done
  26.8 0.0 copy-done.2
  26.8 29.2 %all_to_all.21 = bf16[8,360,128]{2,1,0:T(8,128)(2,1)S(1)} all-to-all(bf16[8,360,128]{2,1,0:T(8,128)(2,1)S(1)} %get-tuple-element.27), channel_id=1, replica_groups=mesh['x'=4,'zl'=4,'core'=2,'y'=8,'zh'=2] {'y'}, dimensions={0} | all-to-all | bytes 1474560 | tf_op jit(solution)/shard_map/all_to_all | solution.py:17
  56.0 0.1 convert_reduce_fusion
  56.1 7.9 %collective-permute-start.1 = (bf16[420,128]{1,0:T(8,128)(2,1)S(1)}, bf16[420,128]{1,0:T(8,128)(2,1)S(1)}, u32[]{:S(2)}, u32[]{:S(2)}) collective-permute-start(bf16[420,128]{1,0:T(8,128)(2,1)S(1)} %pad_maximum_fusion), channel_id=1, source_target_pairs={{0,1},{1,0},{2,3},{3,2},{4,5},{5,4},{6,7},{7,6},{8,9},{9,8},{10,11... | collective-permute-start | bytes 322568 | tf_op jit(solution)/shard_map/ppermute | solution.py:31
  64.1 2.9 %collective-permute-done.1.o_ref = bf16[420,128]{1,0:T(8,128)(2,1)S(1)} collective-permute-done((bf16[420,128]{1,0:T(8,128)(2,1)S(1)}, bf16[420,128]{1,0:T(8,128)(2,1)S(1)}, u32[]{:S(2)}, u32[]{:S(2)}) %collective-permute-start.1) | collective-permute-done | bytes 107552 | tf_op jit(solution)/shard_map/ppermute | solution.py:31
  67.0 0.1 activations.1
  67.1 22.8 %all_to_all.22.s_ref = bf16[8,360,128]{2,1,0:T(8,128)(2,1)S(1)} all-to-all(bf16[8,360,128]{2,1,0:T(8,128)(2,1)S(1)} %activations.1), channel_id=1, replica_groups=mesh['x'=4,'zl'=4,'core'=2,'y'=8,'zh'=2] {'y'}, dimensions={0} | all-to-all | bytes 1474560 | tf_op jit(solution)/shard_map/all_to_all | solution.py:17
  89.9 0.8 shard_map.101
  90.6 0.1 reshape.49
  90.7 0.1 fusion.3
  90.8 4.5 %collective-permute-start.2 = (f32[2,16,24,128]{3,2,0,1:T(8,128)S(1)}, f32[2,16,24,128]{3,2,0,1:T(8,128)S(1)}, u32[]{:S(2)}, u32[]{:S(2)}) collective-permute-start(f32[2,16,24,128]{3,2,0,1:T(8,128)S(1)} %bitcast.32), channel_id=1, source_target_pairs={{0,16},{16,0},{1,17},{17,1},{2,18},{18,2},{3,19},{19,3},{4,20},{20... | collective-permute-start | bytes 1179656 | tf_op jit(solution)/shard_map/ppermute | solution.py:31
  95.3 1.3 %collective-permute-done.2 = f32[2,16,24,128]{3,2,0,1:T(8,128)S(1)} collective-permute-done((f32[2,16,24,128]{3,2,0,1:T(8,128)S(1)}, f32[2,16,24,128]{3,2,0,1:T(8,128)S(1)}, u32[]{:S(2)}, u32[]{:S(2)}) %collective-permute-start.2) | collective-permute-done | bytes 393248 | tf_op jit(solution)/shard_map/ppermute | solution.py:31
  96.7 0.0 copy-start.1
  96.7 0.0 copy-start.3
  96.7 0.1 fusion.1
  96.7 0.7 copy.16
  97.4 4.7 %all-to-all-start.3 = ((bf16[16,48,128]{2,1,0:T(8,128)(2,1)}), bf16[16,48,128]{2,1,0:T(8,128)(2,1)S(1)}, u32[]{:S(2)}, u32[]{:S(2)}) async-start(bf16[16,48,128]{2,1,0:T(8,128)(2,1)} %bitcast.13), calls=%async_computation.3 | async-start | bytes 393216 | tf_op jit(solution)/shard_map/all_to_all | solution.py:17
  102.2 0.0 copy-done.1
  102.2 0.0 copy-done.3
  102.2 1.8 %shard_map.102 = (bf16[640,512]{1,0:T(8,128)(2,1)}, bf16[512,640]{1,0:T(8,128)(2,1)}, bf16[512,640]{1,0:T(8,128)(2,1)}) custom-call(bf16[8,360,128]{2,1,0:T(8,128)(2,1)S(1)} %all_to_all.22.s_ref, bf16[192,512]{1,0:T(8,128)(2,1)S(1)} %copy-done.3, bf16[192,512]{1,0:T(8,128)(2,1)S(1)} %copy-done.1), custom_call_target="tpu_custom_call" | custom-call | flops 377487360 | bytes 2260992 | tf_op jit(solution)/shard_map/pallas_call | solution.py:42
  104.0 7.0 %all-to-all-done.3.a_ref = bf16[16,48,128]{2,1,0:T(8,128)(2,1)S(1)} async-done(((bf16[16,48,128]{2,1,0:T(8,128)(2,1)}), bf16[16,48,128]{2,1,0:T(8,128)(2,1)S(1)}, u32[]{:S(2)}, u32[]{:S(2)}) %all-to-all-start.3) | async-done | bytes 196640 | tf_op jit(solution)/shard_map/all_to_all | solution.py:17
  111.0 0.6 own_outputs.1
  (9 shorter events, 0.2 us)
Async XLA Ops:
  20.1 5.6 %collective-permute-start = (bf16[16,48,128]{2,1,0:T(8,128)(2,1)S(1)}, bf16[16,48,128]{2,1,0:T(8,128)(2,1)S(1)}, u32[]{:S(2)}, u32[]{:S(2)}) collective-permute-start(bf16[16,48,128]{2,1,0:T(8,128)(2,1)S(1)} %all_to_all.20), channel_id=1, source_target_pairs={{0,16},{16,0},{1,17},{17,1},{2,18},{18,2},{3,19},{19,3},{4,20},{20... | collective-permute-start | bytes 589832 | tf_op jit(solution)/shard_map/ppermute | solution.py:31
  25.9 0.9 copy-start
  26.0 0.7 copy-start.2
  56.1 10.9 %collective-permute-start.1 = (bf16[420,128]{1,0:T(8,128)(2,1)S(1)}, bf16[420,128]{1,0:T(8,128)(2,1)S(1)}, u32[]{:S(2)}, u32[]{:S(2)}) collective-permute-start(bf16[420,128]{1,0:T(8,128)(2,1)S(1)} %pad_maximum_fusion), channel_id=1, source_target_pairs={{0,1},{1,0},{2,3},{3,2},{4,5},{5,4},{6,7},{7,6},{8,9},{9,8},{10,11... | collective-permute-start | bytes 322568 | tf_op jit(solution)/shard_map/ppermute | solution.py:31
  90.8 5.9 %collective-permute-start.2 = (f32[2,16,24,128]{3,2,0,1:T(8,128)S(1)}, f32[2,16,24,128]{3,2,0,1:T(8,128)S(1)}, u32[]{:S(2)}, u32[]{:S(2)}) collective-permute-start(f32[2,16,24,128]{3,2,0,1:T(8,128)S(1)} %bitcast.32), channel_id=1, source_target_pairs={{0,16},{16,0},{1,17},{17,1},{2,18},{18,2},{3,19},{19,3},{4,20},{20... | collective-permute-start | bytes 1179656 | tf_op jit(solution)/shard_map/ppermute | solution.py:31
  96.7 5.5 %copy-start.1 = (bf16[192,512]{1,0:T(8,128)(2,1)S(1)}, bf16[192,512]{1,0:T(8,128)(2,1)}, u32[]{:S(2)}) copy-start(bf16[192,512]{1,0:T(8,128)(2,1)} %copy-done) | copy-start | bytes 589828
  96.7 5.5 %copy-start.3 = (bf16[192,512]{1,0:T(8,128)(2,1)S(1)}, bf16[192,512]{1,0:T(8,128)(2,1)}, u32[]{:S(2)}) copy-start(bf16[192,512]{1,0:T(8,128)(2,1)} %copy-done.2) | copy-start | bytes 589828
  97.4 13.6 %all-to-all-start.3 = ((bf16[16,48,128]{2,1,0:T(8,128)(2,1)}), bf16[16,48,128]{2,1,0:T(8,128)(2,1)S(1)}, u32[]{:S(2)}, u32[]{:S(2)}) async-start(bf16[16,48,128]{2,1,0:T(8,128)(2,1)} %bitcast.13), calls=%async_computation.3 | async-start | bytes 393216 | tf_op jit(solution)/shard_map/all_to_all | solution.py:17

commit v11 on v8

--- a/solution.py
+++ b/solution.py
@@ -89,6 +89,19 @@
         compiler_params=pltpu.CompilerParams(vmem_limit_bytes=4 << 20),
         name="read_weights",
     )(core, near, *operands)
+
+
+def collected(arrived, lost, keep):
+    rows = lost.shape[0]
+
+    def kernel(a_ref, l_ref, k_ref, sums_ref, sent_ref):
+        sums = a_ref[...].astype(jnp.float32).sum(axis=0) + l_ref[...]
+        sums_ref[...] = sums
+        sent_ref[:rows, :] = sums.astype(sent_ref.dtype)
+        sent_ref[rows:, :] = k_ref[...]
+
+    outs = ((lost.shape, jnp.float32), ((rows + keep.shape[0], lanes), keep.dtype))
+    return vmem_call(kernel, (arrived, lost, keep), outs, arrived.size)
 
 
 def activations(side, sums, other, keep, ring, parts):
@@ -247,7 +260,7 @@
 
 
 def body(tokens, gate_weight, up_weight, down_weight, keep_mask, cotangent):
-    bf16, f32 = jnp.bfloat16, jnp.float32
+    bf16 = jnp.bfloat16
     own, width = tokens.shape
     share, units = keep_mask.shape
     ring = lax.axis_size("y")
@@ -267,8 +280,8 @@
     all_cot = both[:, :, half:].reshape(total, width)
 
     parts, lost = products(all_tokens, all_cot, weights, place, ring)
-    sums = exchange(parts, "y").astype(f32).sum(axis=0) + lost
-    other = swapped(jnp.concatenate([sums.astype(bf16), keep], axis=0), "zh")
+    sums, sent = collected(exchange(parts, "y"), lost, keep)
+    other = swapped(sent, "zh")
     spread = exchange(activations(side, sums, other, keep, ring, units // lanes), "y")
 
     parts = back_products(spread, weights).reshape(2, chips, 2, -1, lanes)

time: 111 us -> 112 us (level)
  local copies, waits for them, and re-layouts: 0.51 us -> 1.68 us
    unnamed x9 -> x13, local copies, waits for them, and re-layouts: 0.05 us -> 1.23 us
    pallas_call x2 -> x3, Pallas kernels: 2.57 us -> 2.68 us  [vmem_call(): pl.pallas_call(kernel, out_shape=tuple((out_space(*o) for o in outs)), in...]
where the time goes in v11:
time: 112 us; the launch traced here: 111 us
  blocking collectives  69.6 us (62%)
  starting transfers between devices  22.2 us (20%)
  waiting for transfers between devices  9.9 us (9%)
  Pallas kernels  5.64 us (5%)
  local copies, waits for them, and re-layouts  1.68 us (2%)
    all_to_all x3, blocking collectives, exchange(): return lax.all_to_all(blocks, axis, split_axis=0, concat_axis=0, tiled=True)  69.6 us
    ppermute x3, starting transfers between devices, swapped(): return lax.ppermute(value, axis, [(0, 1), (1, 0)])  17.3 us
    all_to_all x1, waiting for transfers between devices, exchange(): return lax.all_to_all(blocks, axis, split_axis=0, concat_axis=0, tiled=True)  5.66 us
    all_to_all x1, starting transfers between devices, exchange(): return lax.all_to_all(blocks, axis, split_axis=0, concat_axis=0, tiled=True)  4.88 us
    ppermute x3, waiting for transfers between devices, swapped(): return lax.ppermute(value, axis, [(0, 1), (1, 0)])  4.24 us
    pallas_call x3, Pallas kernels, vmem_call(): pl.pallas_call(kernel, out_shape=tuple((out_space(*o) for o in outs)), in...  2.68 us
  transfers between devices with their start and end apart: 4, of which 3 were waited for; matrix products, arithmetic and copies ran while one was open for 0% of the time, Pallas kernels for 3%

profile of v11, /device:TPU:1, one launch (start us, length us, event | category | flops | bytes accessed | tf_op | source)
XLA Modules:
  0.0 110.7 jit_solution(7108088456595801490)
XLA Ops:
  0.6 0.0 copy-start.5
  0.6 0.0 copy-start.4
  0.7 0.7 copy-done.5
  1.3 0.0 copy-done.4
  1.4 17.7 %all_to_all.20 = bf16[16,48,128]{2,1,0:T(8,128)(2,1)S(1)} all-to-all(bf16[16,48,128]{2,1,0:T(8,128)(2,1)S(1)} %broadcast_in_dim.3), channel_id=1, replica_groups=mesh['x'=4,'zl'=4,'core'=2,'y'=8,'zh'=2] {'x','zl'}, dimensions={0} | all-to-all | bytes 393216 | tf_op jit(solution)/shard_map/all_to_all | solution.py:17
  19.1 4.8 %collective-permute-start = (bf16[16,48,128]{2,1,0:T(8,128)(2,1)S(1)}, bf16[16,48,128]{2,1,0:T(8,128)(2,1)S(1)}, u32[]{:S(2)}, u32[]{:S(2)}) collective-permute-start(bf16[16,48,128]{2,1,0:T(8,128)(2,1)S(1)} %all_to_all.20), channel_id=1, source_target_pairs={{0,16},{16,0},{1,17},{17,1},{2,18},{18,2},{3,19},{19,3},{4,20},{20... | collective-permute-start | bytes 589832 | tf_op jit(solution)/shard_map/ppermute | solution.py:26
  23.9 1.5 %read_weights.1 = (bf16[512,640]{1,0:T(8,128)(2,1)S(1)}, bf16[512,640]{1,0:T(8,128)(2,1)S(1)}, bf16[640,512]{1,0:T(8,128)(2,1)S(1)}, bf16[60,128]{1,0:T(8,128)(2,1)S(1)}) custom-call(s32[1]{0:T(128)} %bitcast.core_ref, bf16[8,128]{1,0:T(8,128)(2,1)S(1)} %slice_bitcast_fusion.n_ref, bf16[512,640]{1,0:T(8,128)(2,1)} %g_hbm.1, bf16[512,640]{1,0:T(8,128)(2,1)} %u_hbm.1, ...), custom_call_target="tpu_custom_call" | custom-call | flops 1000000000 | bytes 2097152 | tf_op jit(solution)/shard_map/read_weights/pallas_call | solution.py:75
  25.5 0.0 collective-permute-done
  25.6 0.1 reshape.39.c_ref
  25.7 0.0 copy-start
  25.7 0.1 reshape.38.t_ref
  25.9 0.0 copy-start.2
  25.9 0.5 copy-done
  26.4 0.7 products.1
  27.1 0.0 copy-done.2
  27.1 29.2 %all_to_all.21.a_ref = bf16[8,360,128]{2,1,0:T(8,128)(2,1)S(1)} all-to-all(bf16[8,360,128]{2,1,0:T(8,128)(2,1)S(1)} %get-tuple-element.29), channel_id=1, replica_groups=mesh['x'=4,'zl'=4,'core'=2,'y'=8,'zh'=2] {'y'}, dimensions={0} | all-to-all | bytes 1474560 | tf_op jit(solution)/shard_map/all_to_all | solution.py:17
  56.3 0.1 shard_map.101
  56.4 7.9 %collective-permute-start.1 = (bf16[420,128]{1,0:T(8,128)(2,1)S(1)}, bf16[420,128]{1,0:T(8,128)(2,1)S(1)}, u32[]{:S(2)}, u32[]{:S(2)}) collective-permute-start(bf16[420,128]{1,0:T(8,128)(2,1)S(1)} %get-tuple-element.33), channel_id=1, source_target_pairs={{0,1},{1,0},{2,3},{3,2},{4,5},{5,4},{6,7},{7,6},{8,9},{9,8},{10,11... | collective-permute-start | bytes 322568 | tf_op jit(solution)/shard_map/ppermute | solution.py:26
  64.3 2.9 %collective-permute-done.1.o_ref = bf16[420,128]{1,0:T(8,128)(2,1)S(1)} collective-permute-done((bf16[420,128]{1,0:T(8,128)(2,1)S(1)}, bf16[420,128]{1,0:T(8,128)(2,1)S(1)}, u32[]{:S(2)}, u32[]{:S(2)}) %collective-permute-start.1) | collective-permute-done | bytes 107552 | tf_op jit(solution)/shard_map/ppermute | solution.py:26
  67.2 0.1 activations.1
  67.3 22.8 %all_to_all.22.s_ref = bf16[8,360,128]{2,1,0:T(8,128)(2,1)S(1)} all-to-all(bf16[8,360,128]{2,1,0:T(8,128)(2,1)S(1)} %activations.1), channel_id=1, replica_groups=mesh['x'=4,'zl'=4,'core'=2,'y'=8,'zh'=2] {'y'}, dimensions={0} | all-to-all | bytes 1474560 | tf_op jit(solution)/shard_map/all_to_all | solution.py:17
  90.1 0.7 shard_map.102
  90.9 0.1 reshape.40
  91.0 0.1 fusion.3
  91.0 4.5 %collective-permute-start.2 = (f32[2,16,24,128]{3,2,0,1:T(8,128)S(1)}, f32[2,16,24,128]{3,2,0,1:T(8,128)S(1)}, u32[]{:S(2)}, u32[]{:S(2)}) collective-permute-start(f32[2,16,24,128]{3,2,0,1:T(8,128)S(1)} %bitcast.24), channel_id=1, source_target_pairs={{0,16},{16,0},{1,17},{17,1},{2,18},{18,2},{3,19},{19,3},{4,20},{20... | collective-permute-start | bytes 1179656 | tf_op jit(solution)/shard_map/ppermute | solution.py:26
  95.6 1.3 %collective-permute-done.2 = f32[2,16,24,128]{3,2,0,1:T(8,128)S(1)} collective-permute-done((f32[2,16,24,128]{3,2,0,1:T(8,128)S(1)}, f32[2,16,24,128]{3,2,0,1:T(8,128)S(1)}, u32[]{:S(2)}, u32[]{:S(2)}) %collective-permute-start.2) | collective-permute-done | bytes 393248 | tf_op jit(solution)/shard_map/ppermute | solution.py:26
  96.9 0.7 fusion.1
  97.6 0.0 copy-start.1
  97.6 0.0 copy-start.3
  97.6 4.9 %all-to-all-start.3 = ((bf16[16,48,128]{2,1,0:T(8,128)(2,1)}), bf16[16,48,128]{2,1,0:T(8,128)(2,1)S(1)}, u32[]{:S(2)}, u32[]{:S(2)}) async-start(bf16[16,48,128]{2,1,0:T(8,128)(2,1)} %bitcast.9), calls=%async_computation.3 | async-start | bytes 393216 | tf_op jit(solution)/shard_map/all_to_all | solution.py:17
  102.5 0.0 copy-done.1
  102.5 0.0 copy-done.3
  102.5 1.8 %shard_map.103 = (bf16[640,512]{1,0:T(8,128)(2,1)}, bf16[512,640]{1,0:T(8,128)(2,1)}, bf16[512,640]{1,0:T(8,128)(2,1)}) custom-call(bf16[8,360,128]{2,1,0:T(8,128)(2,1)S(1)} %all_to_all.22.s_ref, bf16[192,512]{1,0:T(8,128)(2,1)S(1)} %copy-done.3, bf16[192,512]{1,0:T(8,128)(2,1)S(1)} %copy-done.1), custom_call_target="tpu_custom_call" | custom-call | flops 377487360 | bytes 2260992 | tf_op jit(solution)/shard_map/pallas_call | solution.py:37
  104.4 5.7 %all-to-all-done.3.a_ref = bf16[16,48,128]{2,1,0:T(8,128)(2,1)S(1)} async-done(((bf16[16,48,128]{2,1,0:T(8,128)(2,1)}), bf16[16,48,128]{2,1,0:T(8,128)(2,1)S(1)}, u32[]{:S(2)}, u32[]{:S(2)}) %all-to-all-start.3) | async-done | bytes 196640 | tf_op jit(solution)/shard_map/all_to_all | solution.py:17
  110.0 0.6 own_outputs.1
  (8 shorter events, 0.2 us)
Async XLA Ops:
  0.6 0.7 copy-start.5
  0.6 0.7 copy-start.4
  19.1 6.4 %collective-permute-start = (bf16[16,48,128]{2,1,0:T(8,128)(2,1)S(1)}, bf16[16,48,128]{2,1,0:T(8,128)(2,1)S(1)}, u32[]{:S(2)}, u32[]{:S(2)}) collective-permute-start(bf16[16,48,128]{2,1,0:T(8,128)(2,1)S(1)} %all_to_all.20), channel_id=1, source_target_pairs={{0,16},{16,0},{1,17},{17,1},{2,18},{18,2},{3,19},{19,3},{4,20},{20... | collective-permute-start | bytes 589832 | tf_op jit(solution)/shard_map/ppermute | solution.py:26
  25.7 0.7 copy-start
  25.9 1.2 %copy-start.2 = (bf16[192,512]{1,0:T(8,128)(2,1)}, bf16[192,512]{1,0:T(8,128)(2,1)S(1)}, u32[]{:S(2)}) copy-start(bf16[192,512]{1,0:T(8,128)(2,1)S(1)} %reshape.38.t_ref) | copy-start | bytes 589828
  56.4 10.9 %collective-permute-start.1 = (bf16[420,128]{1,0:T(8,128)(2,1)S(1)}, bf16[420,128]{1,0:T(8,128)(2,1)S(1)}, u32[]{:S(2)}, u32[]{:S(2)}) collective-permute-start(bf16[420,128]{1,0:T(8,128)(2,1)S(1)} %get-tuple-element.33), channel_id=1, source_target_pairs={{0,1},{1,0},{2,3},{3,2},{4,5},{5,4},{6,7},{7,6},{8,9},{9,8},{10,11... | collective-permute-start | bytes 322568 | tf_op jit(solution)/shard_map/ppermute | solution.py:26
  91.0 5.9 %collective-permute-start.2 = (f32[2,16,24,128]{3,2,0,1:T(8,128)S(1)}, f32[2,16,24,128]{3,2,0,1:T(8,128)S(1)}, u32[]{:S(2)}, u32[]{:S(2)}) collective-permute-start(f32[2,16,24,128]{3,2,0,1:T(8,128)S(1)} %bitcast.24), channel_id=1, source_target_pairs={{0,16},{16,0},{1,17},{17,1},{2,18},{18,2},{3,19},{19,3},{4,20},{20... | collective-permute-start | bytes 1179656 | tf_op jit(solution)/shard_map/ppermute | solution.py:26
  97.6 4.9 %copy-start.1 = (bf16[192,512]{1,0:T(8,128)(2,1)S(1)}, bf16[192,512]{1,0:T(8,128)(2,1)}, u32[]{:S(2)}) copy-start(bf16[192,512]{1,0:T(8,128)(2,1)} %copy-done) | copy-start | bytes 589828
  97.6 4.9 %copy-start.3 = (bf16[192,512]{1,0:T(8,128)(2,1)S(1)}, bf16[192,512]{1,0:T(8,128)(2,1)}, u32[]{:S(2)}) copy-start(bf16[192,512]{1,0:T(8,128)(2,1)} %copy-done.2) | copy-start | bytes 589828
  97.6 12.4 %all-to-all-start.3 = ((bf16[16,48,128]{2,1,0:T(8,128)(2,1)}), bf16[16,48,128]{2,1,0:T(8,128)(2,1)S(1)}, u32[]{:S(2)}, u32[]{:S(2)}) async-start(bf16[16,48,128]{2,1,0:T(8,128)(2,1)} %bitcast.9), calls=%async_computation.3 | async-start | bytes 393216 | tf_op jit(solution)/shard_map/all_to_all | solution.py:17
